TPU v7x, 32 devices: a whole 2x2x4 slice. The times are simulated.
32 devices in a mesh: blk: 16 (over z, y, core), head: 2 (over x).
Axes of the slice: x: 2, y: 2, z: 4, core: 2. Of those that a mesh axis runs over, the one named last changes fastest.
Arguments:
- queries: bfloat16 [8192, 16, 128], P('blk', 'head'), may hold values from -6 to 6
- out_grad: bfloat16 [8192, 16, 128], P('blk', 'head'), may hold values from -6 to 6
- outputs: bfloat16 [8192, 16, 128], P('blk', 'head'), may hold values from -6 to 6
- key_vectors: bfloat16 [8192, 128], P('blk'), may hold values from -6 to 6
- value_vectors: bfloat16 [8192, 128], P('blk'), may hold values from -6 to 6
- logsumexp: float32 [8192, 16], P('blk', 'head'), may hold values from 4 to 7
- positions: int32 [8192], P('blk'), may hold values from 0 to 8191, as said below
- doc_start: int32 [8192], P('blk'), may hold values from 0 to 8191, as said below
Outputs:
- query_grad: bfloat16 [8192, 16, 128], P('blk', 'head')
- key_grad: bfloat16 [8192, 128], P('blk')
- value_grad: bfloat16 [8192, 128], P('blk')
Inputs may be any that keep to these rules, and one draw needn't show every extreme that they name: positions is a permutation of 0 to 8191; row r holds position (r mod 512) * 16 + sigma(r div 512), sigma a permutation of the blocks of 512 rows. doc_start of a row is the first position of the document that holds the row's position; documents are runs of consecutive positions, the first starting at 0, and the last position starts a document of its own.
All inputs are finite; a program needn't handle non-finite values.
Results may differ from a plain program's by a relative error of at most 0.0063.
Values may be sent and summed in bfloat16 or wider, within the bound.
No kernel may reach another device: no remote copies, remote signals or barrier semaphores. Data moves between devices by JAX's collectives and lax.ppermute only.
A program may use at most 64 MiB of HBM per device.

v0:
```python
import jax
import jax.numpy as jnp
from jax import lax
from jax.sharding import PartitionSpec as P

STEPS = 4


def from_behind(block, axis, distance):
    devices = range(lax.axis_size(axis))
    route = [((i - distance) % len(devices), i) for i in devices]
    return lax.ppermute(block, axis, route)


def block_grads(
    queries,
    out_grad,
    logsumexp,
    row_delta,
    query_places,
    query_starts,
    key_vectors,
    value_vectors,
    key_places,
):
    scaling = queries.shape[-1] ** (-0.5)
    scores = (
        jnp.einsum("thd,kd->htk", queries, key_vectors, preferred_element_type=jnp.float32)
        * scaling
    )
    allowed = (key_places[None, :] <= query_places[:, None]) & (
        key_places[None, :] >= query_starts[:, None]
    )
    attend = jnp.where(allowed[None], jnp.exp(scores - logsumexp.T[:, :, None]), 0.0)
    attend_low = attend.astype(jnp.bfloat16)
    attend_grad = jnp.einsum(
        "thd,kd->htk", out_grad, value_vectors, preferred_element_type=jnp.float32
    )
    score_grad = attend * (attend_grad - row_delta.T[:, :, None])
    score_low = score_grad.astype(jnp.bfloat16)
    value_part = jnp.einsum("htk,thd->kd", attend_low, out_grad, preferred_element_type=jnp.float32)
    key_part = scaling * jnp.einsum(
        "htk,thd->kd", score_low, queries, preferred_element_type=jnp.float32
    )
    query_part = scaling * jnp.einsum(
        "htk,kd->thd", score_low, key_vectors, preferred_element_type=jnp.float32
    )
    return (query_part, key_part, value_part)


def on_device(
    queries, out_grad, outputs, key_vectors, value_vectors, logsumexp, positions, doc_start
):
    row_delta = jnp.sum(out_grad.astype(jnp.float32) * outputs.astype(jnp.float32), axis=-1)
    query_places = positions.astype(jnp.float32)
    query_starts = doc_start.astype(jnp.float32)
    key_zeros = jnp.zeros(key_vectors.shape, jnp.float32)
    guest_keys, guest_values = (key_vectors, value_vectors)
    carried = (key_zeros, key_zeros, query_places)
    query_total = jnp.zeros(queries.shape, jnp.float32)
    for cycle_step in range(STEPS):
        if cycle_step > 0:
            guest_keys, guest_values = from_behind((guest_keys, guest_values), "blk", -1)
            carried = from_behind((carried[0], carried[1], carried[2]), "blk", -1)
        query_part, key_part, value_part = block_grads(
            queries,
            out_grad,
            logsumexp,
            row_delta,
            query_places,
            query_starts,
            guest_keys,
            guest_values,
            carried[2],
        )
        query_total = query_total + query_part
        carried = (carried[0] + key_part, carried[1] + value_part, carried[2])
    key_total, value_total = from_behind((carried[0], carried[1]), "blk", STEPS - 1)
    key_total, value_total = lax.psum((key_total, value_total), "head")
    key_grad = key_total.astype(jnp.bfloat16)
    value_grad = value_total.astype(jnp.bfloat16)
    return (query_total.astype(jnp.bfloat16), key_grad, value_grad)


def solution(mesh):
    in_specs = (
        P("blk", "head", None),
        P("blk", "head", None),
        P("blk", "head", None),
        P("blk", None),
        P("blk", None),
        P("blk", "head"),
        P("blk"),
        P("blk"),
    )
    out_specs = (P("blk", "head", None), P("blk", None), P("blk", None))
    return jax.shard_map(
        on_device, mesh=mesh, in_specs=in_specs, out_specs=out_specs, check_vma=False
    )
```

profile of v0, /device:TPU:0, one launch (start us, length us, event | category | flops | bytes accessed | tf_op | source)
XLA Modules:
  0.0 120.1 jit_solution(15478278479440468709)
XLA Ops:
  0.7 0.8 convert_element_type.43
  1.5 5.5 %collective-permute-start = (f32[512]{0:T(512)S(1)}, f32[512]{0:T(512)S(1)}, u32[]{:S(2)}, u32[]{:S(2)}) collective-permute-start(f32[512]{0:T(512)S(1)} %convert_element_type.43), channel_id=1, source_target_pairs={{2,0},{4,2},{6,4},{8,6},{10,8},{12,10},{14,12},{16,14},{18,16},{20... | collective-permute-start | bytes 6152 | tf_op jit(solution)/shard_map/ppermute | solution.py:12
  7.0 0.7 collective-permute-start.1
  7.7 0.0 collective-permute-start.2
  7.7 0.6 collective-permute-done
  8.3 4.4 %collective-permute-start.3 = (f32[512]{0:T(512)S(1)}, f32[512]{0:T(512)S(1)}, u32[]{:S(2)}, u32[]{:S(2)}) collective-permute-start(f32[512]{0:T(512)S(1)} %collective-permute-done), channel_id=1, source_target_pairs={{2,0},{4,2},{6,4},{8,6},{10,8},{12,10},{14,12},{16,14},{18,16},{20... | collective-permute-start | bytes 6152 | tf_op jit(solution)/shard_map/ppermute | solution.py:12
  12.7 5.4 %fusion.77 = f32[512,512,8]{1,0,2:T(8,128)} fusion(bf16[512,8,128]{2,1,0:T(8,128)(2,1)S(1)} %copy-done, bf16[512,128]{1,0:T(8,128)(2,1)} %param.11), kind=kOutput, calls=%fused_computation.77 | convolution fusion | flops 536870912 | bytes 9568256 | tf_op jit(solution)/shard_map/thd,kd->htk/dot_general | solution.py:28
  18.1 0.3 collective-permute-start.6
  18.4 0.6 multiply_reduce_fusion
  19.1 0.1 copy.34
  19.2 0.5 collective-permute-done.6
  19.7 0.9 compare_and_fusion.2
  20.6 6.2 %fusion.38 = f32[512,128]{1,0:T(8,128)} fusion(f32[512,512,8]{1,0,2:T(8,128)} %fusion.77, f32[8,512]{1,0:T(8,128)S(1)} %bitcast.159, pred[512,512]{0,1:T(8,128)(4,1)S(1)} %get-tuple-element.14, bf16[512,8,128]{2,1,0:T(8,128)(2,1)} %param.9), kind=kOutput, calls=%fused_computation.48 | convolution fusion | flops 545259520 | bytes 9977856 | tf_op jit(solution)/shard_map/htk,thd->kd/dot_general | solution.py:41
  26.9 5.2 %fusion.13 = bf16[8,512,512]{1,2,0:T(8,128)(2,1)S(1)} fusion(f32[512,512,8]{1,0,2:T(8,128)} %fusion.77, f32[8,512]{1,0:T(8,128)S(1)} %copy.34, f32[8,512]{1,0:T(8,128)S(1)} %bitcast.160, pred[512,512]{0,1:T(8,128)(4,1)S(1)} %get-tuple-element.14, bf16[512,8,128]{2,1,0:T(8,128)(2,1)S(1)} %copy-done.3, bf16[512,128]{1,0:T(8,128)(2,1)S(1)} %copy-done.12), kind=kOutput, calls=%fused_computation.20 | convolution fusion | flops 549453824 | bytes 14057472 | tf_op jit(solution)/shard_map/thd,kd->htk/dot_general | solution.py:36
  32.0 2.0 %fusion.33 = f32[512,128]{1,0:T(8,128)} fusion(bf16[8,512,512]{1,2,0:T(8,128)(2,1)S(1)} %fusion.13, bf16[512,8,128]{2,1,0:T(8,128)(2,1)S(1)} %copy-done), kind=kOutput, calls=%fused_computation.43 | convolution fusion | flops 536936448 | bytes 5505024 | tf_op jit(solution)/shard_map/htk,thd->kd/dot_general | solution.py:42
  34.0 1.3 %fusion.91 = f32[8,512,128]{2,1,0:T(8,128)S(1)} fusion(bf16[8,512,512]{1,2,0:T(8,128)(2,1)S(1)} %fusion.13, bf16[512,128]{1,0:T(8,128)(2,1)S(1)} %copy-done.5), kind=kOutput, calls=%fused_computation.91 | convolution fusion | flops 536870912 | bytes 6422528 | tf_op jit(solution)/shard_map/htk,kd->thd/dot_general | solution.py:45
  35.3 4.5 %collective-permute-start.9 = (f32[512,128]{1,0:T(8,128)}, f32[512,128]{1,0:T(8,128)}, u32[]{:S(2)}, u32[]{:S(2)}) collective-permute-start(f32[512,128]{1,0:T(8,128)} %fusion.33), channel_id=1, source_target_pairs={{2,0},{4,2},{6,4},{8,6},{10,8},{12,10},{14,12},{16,14},{18,16},{20... | collective-permute-start | bytes 786440 | tf_op jit(solution)/shard_map/ppermute | solution.py:12
  39.7 0.1 collective-permute-start.13
  39.8 1.3 %fusion.75 = f32[512,512,8]{1,0,2:T(8,128)S(1)} fusion(bf16[512,8,128]{2,1,0:T(8,128)(2,1)S(1)} %copy-done, bf16[512,128]{1,0:T(8,128)(2,1)S(1)} %collective-permute-done.1), kind=kOutput, calls=%fused_computation.75 | convolution fusion | flops 536870912 | bytes 9568256 | tf_op jit(solution)/shard_map/thd,kd->htk/dot_general | solution.py:28
  41.1 0.1 collective-permute-start.4
  41.1 0.2 collective-permute-start.5
  41.4 4.0 %fusion.9 = bf16[8,512,512]{1,2,0:T(8,128)(2,1)S(1)} fusion(f32[512,512,8]{1,0,2:T(8,128)S(1)} %fusion.75, f32[8,512]{1,0:T(8,128)S(1)} %copy.34, f32[8,512]{1,0:T(8,128)S(1)} %bitcast.161, pred[512,512]{0,1:T(8,128)(4,1)S(1)} %get-tuple-element.11, bf16[512,8,128]{2,1,0:T(8,128)(2,1)S(1)} %copy-done.4, bf16[512,128]{1,0:T(8,128)(2,1)} %collective-permute-done.2), kind=kOutput, calls=%fused_computation.14 | convolution fusion | flops 549453824 | bytes 14057472 | tf_op jit(solution)/shard_map/thd,kd->htk/dot_general | solution.py:36
  45.5 1.3 %fusion.87 = f32[8,512,128]{2,1,0:T(8,128)S(1)} fusion(bf16[8,512,512]{1,2,0:T(8,128)(2,1)S(1)} %fusion.9, bf16[512,128]{1,0:T(8,128)(2,1)S(1)} %collective-permute-done.1), kind=kOutput, calls=%fused_computation.87 | convolution fusion | flops 536870912 | bytes 6422528 | tf_op jit(solution)/shard_map/htk,kd->thd/dot_general | solution.py:45
  46.8 1.3 %collective-permute-done.4 = bf16[512,128]{1,0:T(8,128)(2,1)S(1)} collective-permute-done((bf16[512,128]{1,0:T(8,128)(2,1)S(1)}, bf16[512,128]{1,0:T(8,128)(2,1)S(1)}, u32[]{:S(2)}, u32[]{:S(2)}) %collective-permute-start.4) | collective-permute-done | bytes 131104 | tf_op jit(solution)/shard_map/ppermute | solution.py:12
  48.0 1.3 %fusion.73 = f32[512,512,8]{1,0,2:T(8,128)S(1)} fusion(bf16[512,8,128]{2,1,0:T(8,128)(2,1)S(1)} %copy-done, bf16[512,128]{1,0:T(8,128)(2,1)S(1)} %collective-permute-done.4), kind=kOutput, calls=%fused_computation.73 | convolution fusion | flops 536870912 | bytes 9568256 | tf_op jit(solution)/shard_map/thd,kd->htk/dot_general | solution.py:28
  49.3 0.3 collective-permute-done.5
  49.6 5.3 %fusion.5 = bf16[8,512,512]{1,2,0:T(8,128)(2,1)} fusion(f32[512,512,8]{1,0,2:T(8,128)S(1)} %fusion.73, f32[8,512]{1,0:T(8,128)S(1)} %copy.34, f32[8,512]{1,0:T(8,128)S(1)} %bitcast.162, pred[512,512]{0,1:T(8,128)(4,1)S(1)} %get-tuple-element.12, bf16[512,8,128]{2,1,0:T(8,128)(2,1)S(1)} %copy-done.4, bf16[512,128]{1,0:T(8,128)(2,1)} %collective-permute-done.5), kind=kOutput, calls=%fused_computation.8 | convolution fusion | flops 549453824 | bytes 14057472 | tf_op jit(solution)/shard_map/thd,kd->htk/dot_general | solution.py:36
  54.8 3.5 %fusion.36 = f32[512,128]{1,0:T(8,128)S(1)} fusion(bf16[8,512,512]{1,2,0:T(8,128)(2,1)} %fusion.5, bf16[512,8,128]{2,1,0:T(8,128)(2,1)S(1)} %copy-done), kind=kOutput, calls=%fused_computation.46 | convolution fusion | flops 536936448 | bytes 5505024 | tf_op jit(solution)/shard_map/htk,thd->kd/dot_general | solution.py:42
  58.3 4.7 %collective-permute-start.7 = (bf16[512,128]{1,0:T(8,128)(2,1)S(1)}, bf16[512,128]{1,0:T(8,128)(2,1)S(1)}, u32[]{:S(2)}, u32[]{:S(2)}) collective-permute-start(bf16[512,128]{1,0:T(8,128)(2,1)S(1)} %collective-permute-done.4), channel_id=1, source_target_pairs={{2,0},{4,2},{6,4},{8,6},{10,8},{12,10},{14,12},{16,14},{18,16},{20... | collective-permute-start | bytes 393224 | tf_op jit(solution)/shard_map/ppermute | solution.py:12
  63.0 0.1 collective-permute-start.8
  63.0 3.5 %fusion.83 = f32[8,512,128]{2,1,0:T(8,128)S(1)} fusion(bf16[8,512,512]{1,2,0:T(8,128)(2,1)} %fusion.5, bf16[512,128]{1,0:T(8,128)(2,1)S(1)} %collective-permute-done.4), kind=kOutput, calls=%fused_computation.83 | convolution fusion | flops 536870912 | bytes 6422528 | tf_op jit(solution)/shard_map/htk,kd->thd/dot_general | solution.py:45
  66.5 2.9 %fusion.35 = f32[512,128]{1,0:T(8,128)} fusion(f32[512,128]{1,0:T(8,128)} %collective-permute-done.9, bf16[8,512,512]{1,2,0:T(8,128)(2,1)S(1)} %fusion.9, bf16[512,8,128]{2,1,0:T(8,128)(2,1)S(1)} %copy-done), kind=kOutput, calls=%fused_computation.45 | convolution fusion | flops 537001984 | bytes 5767168 | tf_op jit(solution)/shard_map/htk,thd->kd/dot_general | solution.py:42
  69.5 3.6 %fusion.56 = f32[512,128]{1,0:T(8,128)} fusion(f32[512,128]{1,0:T(8,128)} %collective-permute-done.13, f32[512,512,8]{1,0,2:T(8,128)S(1)} %fusion.75, f32[8,512]{1,0:T(8,128)S(1)} %bitcast.163, pred[512,512]{0,1:T(8,128)(4,1)S(1)} %copy-done.10, bf16[512,8,128]{2,1,0:T(8,128)(2,1)S(1)} %copy-done.4), kind=kOutput, calls=%fused_computation.54 | convolution fusion | flops 545325056 | bytes 10240000 | tf_op jit(solution)/shard_map/htk,thd->kd/dot_general | solution.py:41
  73.1 1.3 %fusion.71 = f32[512,512,8]{1,0,2:T(8,128)S(1)} fusion(bf16[512,8,128]{2,1,0:T(8,128)(2,1)S(1)} %copy-done, bf16[512,128]{1,0:T(8,128)(2,1)S(1)} %collective-permute-done.7), kind=kOutput, calls=%fused_computation.71 | convolution fusion | flops 536870912 | bytes 9568256 | tf_op jit(solution)/shard_map/thd,kd->htk/dot_general | solution.py:28
  74.4 0.6 copy-done.13
  75.0 4.0 %fusion.1 = bf16[8,512,512]{1,2,0:T(8,128)(2,1)S(1)} fusion(f32[512,512,8]{1,0,2:T(8,128)S(1)} %fusion.71, f32[8,512]{1,0:T(8,128)S(1)} %copy.34, f32[8,512]{1,0:T(8,128)S(1)} %bitcast.164, pred[512,512]{0,1:T(8,128)(4,1)S(1)} %get-tuple-element.13, bf16[512,8,128]{2,1,0:T(8,128)(2,1)S(1)} %copy-done.4, bf16[512,128]{1,0:T(8,128)(2,1)} %copy-done.13), kind=kOutput, calls=%fused_computation.2 | convolution fusion | flops 549453824 | bytes 14057472 | tf_op jit(solution)/shard_map/thd,kd->htk/dot_general | solution.py:36
  79.1 0.1 collective-permute-start.11
  79.2 2.9 %fusion.53 = f32[512,128]{1,0:T(8,128)S(1)} fusion(f32[512,128]{1,0:T(8,128)} %collective-permute-done.14, f32[512,512,8]{1,0,2:T(8,128)S(1)} %fusion.73, f32[8,512]{1,0:T(8,128)S(1)} %bitcast.165, pred[512,512]{0,1:T(8,128)(4,1)} %copy-done.8, bf16[512,8,128]{2,1,0:T(8,128)(2,1)S(1)} %copy-done.4), kind=kOutput, calls=%fused_computation.53 | convolution fusion | flops 545325056 | bytes 10240000 | tf_op jit(solution)/shard_map/htk,thd->kd/dot_general | solution.py:41
  82.1 2.8 %collective-permute-start.15 = (f32[512,128]{1,0:T(8,128)S(1)}, f32[512,128]{1,0:T(8,128)S(1)}, u32[]{:S(2)}, u32[]{:S(2)}) collective-permute-start(f32[512,128]{1,0:T(8,128)S(1)} %fusion.53), channel_id=1, source_target_pairs={{2,0},{4,2},{6,4},{8,6},{10,8},{12,10},{14,12},{16,14},{18,16},{20... | collective-permute-start | bytes 786440 | tf_op jit(solution)/shard_map/ppermute | solution.py:12
  84.9 1.2 %fusion.37 = f32[512,128]{1,0:T(8,128)S(1)} fusion(bf16[8,512,512]{1,2,0:T(8,128)(2,1)S(1)} %fusion.1, bf16[512,8,128]{2,1,0:T(8,128)(2,1)S(1)} %copy-done), kind=kOutput, calls=%fused_computation.47 | convolution fusion | flops 536936448 | bytes 5505024 | tf_op jit(solution)/shard_map/htk,thd->kd/dot_general | solution.py:42
  86.2 1.9 %collective-permute-start.12 = (f32[512,128]{1,0:T(8,128)S(1)}, f32[512,128]{1,0:T(8,128)S(1)}, u32[]{:S(2)}, u32[]{:S(2)}) collective-permute-start(f32[512,128]{1,0:T(8,128)S(1)} %add.42), channel_id=1, source_target_pairs={{26,0},{28,2},{30,4},{0,6},{2,8},{4,10},{6,12},{8,14},{10,16},{12,... | collective-permute-start | bytes 786440 | tf_op jit(solution)/shard_map/ppermute | solution.py:12
  88.1 1.7 %collective-permute-done.15 = f32[512,128]{1,0:T(8,128)S(1)} collective-permute-done((f32[512,128]{1,0:T(8,128)S(1)}, f32[512,128]{1,0:T(8,128)S(1)}, u32[]{:S(2)}, u32[]{:S(2)}) %collective-permute-start.15) | collective-permute-done | bytes 262176 | tf_op jit(solution)/shard_map/ppermute | solution.py:12
  89.8 1.9 %fusion.50 = f32[512,128]{1,0:T(8,128)S(1)} fusion(f32[512,128]{1,0:T(8,128)S(1)} %collective-permute-done.15, f32[512,512,8]{1,0,2:T(8,128)S(1)} %fusion.71, f32[8,512]{1,0:T(8,128)S(1)} %bitcast.166, pred[512,512]{0,1:T(8,128)(4,1)S(1)} %copy-done.7, bf16[512,8,128]{2,1,0:T(8,128)(2,1)S(1)} %copy-done.4), kind=kOutput, calls=%fused_computation.52 | convolution fusion | flops 545325056 | bytes 10240000 | tf_op jit(solution)/shard_map/htk,thd->kd/dot_general | solution.py:41
  91.7 1.6 %collective-permute-start.16 = (f32[512,128]{1,0:T(8,128)S(1)}, f32[512,128]{1,0:T(8,128)}, u32[]{:S(2)}, u32[]{:S(2)}) collective-permute-start(f32[512,128]{1,0:T(8,128)S(1)} %fusion.50), channel_id=1, source_target_pairs={{26,0},{28,2},{30,4},{0,6},{2,8},{4,10},{6,12},{8,14},{10,16},{12,... | collective-permute-start | bytes 786440 | tf_op jit(solution)/shard_map/ppermute | solution.py:12
  93.3 1.4 %fusion.32 = bf16[512,8,128]{2,0,1:T(8,128)(2,1)S(1)} fusion(bf16[8,512,512]{1,2,0:T(8,128)(2,1)S(1)} %fusion.1, f32[8,512,128]{2,1,0:T(8,128)S(1)} %fusion.83, f32[8,512,128]{2,1,0:T(8,128)S(1)} %fusion.91, f32[8,512,128]{2,1,0:T(8,128)S(1)} %fusion.87, bf16[512,128]{1,0:T(8,128)(2,1)S(1)} %collective-permute-done.7), kind=kOutput, calls=%fused_computation.38 | convolution fusion | flops 539492352 | bytes 11665408 | tf_op jit(solution)/shard_map/htk,kd->thd/dot_general | solution.py:45
  94.7 1.7 %copy.53 = bf16[512,8,128]{2,1,0:T(8,128)(2,1)} copy(bf16[512,8,128]{2,0,1:T(8,128)(2,1)S(1)} %fusion.32) | data formatting | bytes 2097152
  96.4 3.1 %collective-permute-done.16 = f32[512,128]{1,0:T(8,128)} collective-permute-done((f32[512,128]{1,0:T(8,128)S(1)}, f32[512,128]{1,0:T(8,128)}, u32[]{:S(2)}, u32[]{:S(2)}) %collective-permute-start.16) | collective-permute-done | bytes 262176 | tf_op jit(solution)/shard_map/ppermute | solution.py:12
  99.5 20.6 %all-reduce.2 = (bf16[512,128]{1,0:T(8,128)(2,1)}, bf16[512,128]{1,0:T(8,128)(2,1)}) all-reduce(f32[512,128]{1,0:T(8,128)S(1)} %collective-permute-done.12, f32[512,128]{1,0:T(8,128)} %collective-permute-done.16), channel_id=1, replica_groups=mesh['blk'=16,'head'=2] {'head'}, use_global_device_ids=true, to_apply=%region_1.2 | all-reduce | flops 131072 | bytes 786432 | tf_op jit(solution)/shard_map/psum | solution.py:79
  (51 shorter events, 0.2 us)
Async XLA Ops:
  0.6 12.1 %copy-start = (bf16[512,8,128]{2,1,0:T(8,128)(2,1)S(1)}, bf16[512,8,128]{2,1,0:T(8,128)(2,1)}, u32[]{:S(2)}) copy-start(bf16[512,8,128]{2,1,0:T(8,128)(2,1)} %param.8) | copy-start | bytes 3145732
  0.6 17.8 %copy-start.1 = (bf16[512,8,128]{2,1,0:T(8,128)(2,1)S(1)}, bf16[512,8,128]{2,1,0:T(8,128)(2,1)}, u32[]{:S(2)}) copy-start(bf16[512,8,128]{2,1,0:T(8,128)(2,1)} %param.10) | copy-start | bytes 3145732
  0.7 17.8 %copy-start.2 = (bf16[512,8,128]{2,1,0:T(8,128)(2,1)S(1)}, bf16[512,8,128]{2,1,0:T(8,128)(2,1)}, u32[]{:S(2)}) copy-start(bf16[512,8,128]{2,1,0:T(8,128)(2,1)} %param.9) | copy-start | bytes 3145732
  0.7 18.4 %copy-start.11 = (s32[512]{0:T(512)S(1)}, s32[512]{0:T(512)}, u32[]{:S(2)}) copy-start(s32[512]{0:T(512)} %param.15) | copy-start | bytes 6148
  0.7 20.0 %copy-start.14 = (f32[512,8]{0,1:T(8,128)S(1)}, f32[512,8]{0,1:T(8,128)}, u32[]{:S(2)}) copy-start(f32[512,8]{0,1:T(8,128)} %param.13) | copy-start | bytes 49156
  1.5 6.8 %collective-permute-start = (f32[512]{0:T(512)S(1)}, f32[512]{0:T(512)S(1)}, u32[]{:S(2)}, u32[]{:S(2)}) collective-permute-start(f32[512]{0:T(512)S(1)} %convert_element_type.43), channel_id=1, source_target_pairs={{2,0},{4,2},{6,4},{8,6},{10,8},{12,10},{14,12},{16,14},{18,16},{20... | collective-permute-start | bytes 6152 | tf_op jit(solution)/shard_map/ppermute | solution.py:12
  7.0 32.8 %collective-permute-start.1 = (bf16[512,128]{1,0:T(8,128)(2,1)}, bf16[512,128]{1,0:T(8,128)(2,1)S(1)}, u32[]{:S(2)}, u32[]{:S(2)}) collective-permute-start(bf16[512,128]{1,0:T(8,128)(2,1)} %param.11), channel_id=1, source_target_pairs={{2,0},{4,2},{6,4},{8,6},{10,8},{12,10},{14,12},{16,14},{18,16},{20... | collective-permute-start | bytes 393224 | tf_op jit(solution)/shard_map/ppermute | solution.py:12
  7.7 33.5 %collective-permute-start.2 = (bf16[512,128]{1,0:T(8,128)(2,1)}, bf16[512,128]{1,0:T(8,128)(2,1)}, u32[]{:S(2)}, u32[]{:S(2)}) collective-permute-start(bf16[512,128]{1,0:T(8,128)(2,1)} %param.12), channel_id=1, source_target_pairs={{2,0},{4,2},{6,4},{8,6},{10,8},{12,10},{14,12},{16,14},{18,16},{20... | collective-permute-start | bytes 393224 | tf_op jit(solution)/shard_map/ppermute | solution.py:12
  8.3 9.8 %collective-permute-start.3 = (f32[512]{0:T(512)S(1)}, f32[512]{0:T(512)S(1)}, u32[]{:S(2)}, u32[]{:S(2)}) collective-permute-start(f32[512]{0:T(512)S(1)} %collective-permute-done), channel_id=1, source_target_pairs={{2,0},{4,2},{6,4},{8,6},{10,8},{12,10},{14,12},{16,14},{18,16},{20... | collective-permute-start | bytes 6152 | tf_op jit(solution)/shard_map/ppermute | solution.py:12
  18.1 1.6 %collective-permute-start.6 = (f32[512]{0:T(512)S(1)}, f32[512]{0:T(512)S(1)}, u32[]{:S(2)}, u32[]{:S(2)}) collective-permute-start(f32[512]{0:T(512)S(1)} %collective-permute-done.3), channel_id=1, source_target_pairs={{2,0},{4,2},{6,4},{8,6},{10,8},{12,10},{14,12},{16,14},{18,16},{20... | collective-permute-start | bytes 6152 | tf_op jit(solution)/shard_map/ppermute | solution.py:12
  19.1 7.8 %copy-start.3 = (bf16[512,8,128]{2,1,0:T(8,128)(2,1)S(1)}, bf16[512,8,128]{2,1,0:T(8,128)(2,1)}, u32[]{:S(2)}) copy-start(bf16[512,8,128]{2,1,0:T(8,128)(2,1)} %param.9) | copy-start | bytes 3145732
  19.1 7.8 %copy-start.12 = (bf16[512,128]{1,0:T(8,128)(2,1)S(1)}, bf16[512,128]{1,0:T(8,128)(2,1)}, u32[]{:S(2)}) copy-start(bf16[512,128]{1,0:T(8,128)(2,1)} %param.12) | copy-start | bytes 393220
  20.6 20.8 %copy-start.9 = (pred[512,512]{0,1:T(8,128)(4,1)}, pred[512,512]{0,1:T(8,128)(4,1)S(1)}, u32[]{:S(2)}) copy-start(pred[512,512]{0,1:T(8,128)(4,1)S(1)} %get-tuple-element.11) | copy-start | bytes 786436
  20.6 28.9 %copy-start.8 = (pred[512,512]{0,1:T(8,128)(4,1)}, pred[512,512]{0,1:T(8,128)(4,1)S(1)}, u32[]{:S(2)}) copy-start(pred[512,512]{0,1:T(8,128)(4,1)S(1)} %get-tuple-element.12) | copy-start | bytes 786436
  20.6 54.4 %copy-start.6 = (pred[512,512]{0,1:T(8,128)(4,1)}, pred[512,512]{0,1:T(8,128)(4,1)S(1)}, u32[]{:S(2)}) copy-start(pred[512,512]{0,1:T(8,128)(4,1)S(1)} %get-tuple-element.13) | copy-start | bytes 786436
  26.9 7.1 %copy-start.5 = (bf16[512,128]{1,0:T(8,128)(2,1)S(1)}, bf16[512,128]{1,0:T(8,128)(2,1)}, u32[]{:S(2)}) copy-start(bf16[512,128]{1,0:T(8,128)(2,1)} %param.11) | copy-start | bytes 393220
  34.0 7.4 %copy-start.4 = (bf16[512,8,128]{2,1,0:T(8,128)(2,1)S(1)}, bf16[512,8,128]{2,1,0:T(8,128)(2,1)}, u32[]{:S(2)}) copy-start(bf16[512,8,128]{2,1,0:T(8,128)(2,1)} %param.9) | copy-start | bytes 3145732
  34.0 7.4 %copy-start.15 = (f32[512,8]{0,1:T(8,128)S(1)}, f32[512,8]{0,1:T(8,128)}, u32[]{:S(2)}) copy-start(f32[512,8]{0,1:T(8,128)} %param.13) | copy-start | bytes 49156
  35.3 31.2 %collective-permute-start.9 = (f32[512,128]{1,0:T(8,128)}, f32[512,128]{1,0:T(8,128)}, u32[]{:S(2)}, u32[]{:S(2)}) collective-permute-start(f32[512,128]{1,0:T(8,128)} %fusion.33), channel_id=1, source_target_pairs={{2,0},{4,2},{6,4},{8,6},{10,8},{12,10},{14,12},{16,14},{18,16},{20... | collective-permute-start | bytes 786440 | tf_op jit(solution)/shard_map/ppermute | solution.py:12
  39.7 29.7 %collective-permute-start.13 = (f32[512,128]{1,0:T(8,128)}, f32[512,128]{1,0:T(8,128)}, u32[]{:S(2)}, u32[]{:S(2)}) collective-permute-start(f32[512,128]{1,0:T(8,128)} %fusion.38), channel_id=1, source_target_pairs={{2,0},{4,2},{6,4},{8,6},{10,8},{12,10},{14,12},{16,14},{18,16},{20... | collective-permute-start | bytes 786440 | tf_op jit(solution)/shard_map/ppermute | solution.py:12
  41.1 7.0 %collective-permute-start.4 = (bf16[512,128]{1,0:T(8,128)(2,1)S(1)}, bf16[512,128]{1,0:T(8,128)(2,1)S(1)}, u32[]{:S(2)}, u32[]{:S(2)}) collective-permute-start(bf16[512,128]{1,0:T(8,128)(2,1)S(1)} %collective-permute-done.1), channel_id=1, source_target_pairs={{2,0},{4,2},{6,4},{8,6},{10,8},{12,10},{14,12},{16,14},{18,16},{20... | collective-permute-start | bytes 393224 | tf_op jit(solution)/shard_map/ppermute | solution.py:12
  41.1 8.4 %collective-permute-start.5 = (bf16[512,128]{1,0:T(8,128)(2,1)}, bf16[512,128]{1,0:T(8,128)(2,1)}, u32[]{:S(2)}, u32[]{:S(2)}) collective-permute-start(bf16[512,128]{1,0:T(8,128)(2,1)} %collective-permute-done.2), channel_id=1, source_target_pairs={{2,0},{4,2},{6,4},{8,6},{10,8},{12,10},{14,12},{16,14},{18,16},{20... | collective-permute-start | bytes 393224 | tf_op jit(solution)/shard_map/ppermute | solution.py:12
  54.8 14.6 %copy-start.10 = (pred[512,512]{0,1:T(8,128)(4,1)S(1)}, pred[512,512]{0,1:T(8,128)(4,1)}, u32[]{:S(2)}) copy-start(pred[512,512]{0,1:T(8,128)(4,1)} %copy-done.9) | copy-start | bytes 786436
  54.8 14.6 %copy-start.16 = (f32[512,8]{0,1:T(8,128)S(1)}, f32[512,8]{0,1:T(8,128)}, u32[]{:S(2)}) copy-start(f32[512,8]{0,1:T(8,128)} %param.13) | copy-start | bytes 49156
  58.3 14.8 %collective-permute-start.7 = (bf16[512,128]{1,0:T(8,128)(2,1)S(1)}, bf16[512,128]{1,0:T(8,128)(2,1)S(1)}, u32[]{:S(2)}, u32[]{:S(2)}) collective-permute-start(bf16[512,128]{1,0:T(8,128)(2,1)S(1)} %collective-permute-done.4), channel_id=1, source_target_pairs={{2,0},{4,2},{6,4},{8,6},{10,8},{12,10},{14,12},{16,14},{18,16},{20... | collective-permute-start | bytes 393224 | tf_op jit(solution)/shard_map/ppermute | solution.py:12
  63.0 11.4 %collective-permute-start.8 = (bf16[512,128]{1,0:T(8,128)(2,1)}, bf16[512,128]{1,0:T(8,128)(2,1)S(1)}, u32[]{:S(2)}, u32[]{:S(2)}) collective-permute-start(bf16[512,128]{1,0:T(8,128)(2,1)} %collective-permute-done.5), channel_id=1, source_target_pairs={{2,0},{4,2},{6,4},{8,6},{10,8},{12,10},{14,12},{16,14},{18,16},{20... | collective-permute-start | bytes 393224 | tf_op jit(solution)/shard_map/ppermute | solution.py:12
  69.4 9.6 %collective-permute-start.10 = (f32[512,128]{1,0:T(8,128)}, f32[512,128]{1,0:T(8,128)S(1)}, u32[]{:S(2)}, u32[]{:S(2)}) collective-permute-start(f32[512,128]{1,0:T(8,128)} %fusion.35), channel_id=1, source_target_pairs={{2,0},{4,2},{6,4},{8,6},{10,8},{12,10},{14,12},{16,14},{18,16},{20... | collective-permute-start | bytes 786440 | tf_op jit(solution)/shard_map/ppermute | solution.py:12
  73.1 6.1 %collective-permute-start.14 = (f32[512,128]{1,0:T(8,128)}, f32[512,128]{1,0:T(8,128)}, u32[]{:S(2)}, u32[]{:S(2)}) collective-permute-start(f32[512,128]{1,0:T(8,128)} %fusion.56), channel_id=1, source_target_pairs={{2,0},{4,2},{6,4},{8,6},{10,8},{12,10},{14,12},{16,14},{18,16},{20... | collective-permute-start | bytes 786440 | tf_op jit(solution)/shard_map/ppermute | solution.py:12
  74.3 0.7 copy-start.13
  79.1 10.8 %copy-start.7 = (pred[512,512]{0,1:T(8,128)(4,1)S(1)}, pred[512,512]{0,1:T(8,128)(4,1)}, u32[]{:S(2)}) copy-start(pred[512,512]{0,1:T(8,128)(4,1)} %copy-done.6) | copy-start | bytes 786436
  79.1 10.8 %copy-start.17 = (f32[512,8]{0,1:T(8,128)S(1)}, f32[512,8]{0,1:T(8,128)}, u32[]{:S(2)}) copy-start(f32[512,8]{0,1:T(8,128)} %param.13) | copy-start | bytes 49156
  79.1 7.0 %collective-permute-start.11 = (f32[512,128]{1,0:T(8,128)S(1)}, f32[512,128]{1,0:T(8,128)S(1)}, u32[]{:S(2)}, u32[]{:S(2)}) collective-permute-start(f32[512,128]{1,0:T(8,128)S(1)} %add.41), channel_id=1, source_target_pairs={{2,0},{4,2},{6,4},{8,6},{10,8},{12,10},{14,12},{16,14},{18,16},{20... | collective-permute-start | bytes 786440 | tf_op jit(solution)/shard_map/ppermute | solution.py:12
  82.1 7.7 %collective-permute-start.15 = (f32[512,128]{1,0:T(8,128)S(1)}, f32[512,128]{1,0:T(8,128)S(1)}, u32[]{:S(2)}, u32[]{:S(2)}) collective-permute-start(f32[512,128]{1,0:T(8,128)S(1)} %fusion.53), channel_id=1, source_target_pairs={{2,0},{4,2},{6,4},{8,6},{10,8},{12,10},{14,12},{16,14},{18,16},{20... | collective-permute-start | bytes 786440 | tf_op jit(solution)/shard_map/ppermute | solution.py:12
  86.2 10.2 %collective-permute-start.12 = (f32[512,128]{1,0:T(8,128)S(1)}, f32[512,128]{1,0:T(8,128)S(1)}, u32[]{:S(2)}, u32[]{:S(2)}) collective-permute-start(f32[512,128]{1,0:T(8,128)S(1)} %add.42), channel_id=1, source_target_pairs={{26,0},{28,2},{30,4},{0,6},{2,8},{4,10},{6,12},{8,14},{10,16},{12,... | collective-permute-start | bytes 786440 | tf_op jit(solution)/shard_map/ppermute | solution.py:12
  91.7 7.8 %collective-permute-start.16 = (f32[512,128]{1,0:T(8,128)S(1)}, f32[512,128]{1,0:T(8,128)}, u32[]{:S(2)}, u32[]{:S(2)}) collective-permute-start(f32[512,128]{1,0:T(8,128)S(1)} %fusion.50), channel_id=1, source_target_pairs={{26,0},{28,2},{30,4},{0,6},{2,8},{4,10},{6,12},{8,14},{10,16},{12,... | collective-permute-start | bytes 786440 | tf_op jit(solution)/shard_map/ppermute | solution.py:12
where the time goes:
time: 120 us
  matrix products  59.4 us (50%)
  starting transfers between devices  26.8 us (22%)
  blocking collectives  20.6 us (17%)
  waiting for transfers between devices  7.5 us (6%)
  local copies, waits for them, and re-layouts  2.48 us (2%)
  other arithmetic  2.42 us (2%)
    ppermute x17, starting transfers between devices, from_behind(): return lax.ppermute(block, axis, route)  26.8 us
    psum x1, blocking collectives, on_device(): key_total, value_total = lax.psum((key_total, value_total), 'head')  20.6 us
    dot_general x4, matrix products, block_grads(): jnp.einsum('thd,kd->htk', out_grad, value_vectors, preferred_element_type...  18.5 us
    dot_general x4, matrix products, block_grads(): jnp.einsum('htk,thd->kd', attend_low, out_grad, preferred_element_type=jn...  14.6 us
    dot_general x4, matrix products, block_grads(): jnp.einsum('htk,thd->kd', score_low, queries, preferred_element_type=jnp....  9.58 us
    dot_general x4, matrix products, block_grads(): jnp.einsum('thd,kd->htk', queries, key_vectors, preferred_element_type=jn...  9.21 us
    ppermute x17, waiting for transfers between devices, from_behind(): return lax.ppermute(block, axis, route)  7.5 us
    dot_general x4, matrix products, block_grads(): jnp.einsum('htk,kd->thd', score_low, key_vectors, preferred_element_type=...  7.47 us
  transfers between devices with their start and end apart: 17, of which 6 were waited for; matrix products, arithmetic and copies ran while one was open for 52% of the time, Pallas kernels for 0%

commit v1 on v0

v1 whole, which is shorter than its diff:
```python
import functools, math
import jax
import jax.numpy as jnp
from jax import lax
from jax.experimental import pallas as pl
from jax.experimental.pallas import tpu as pltpu
from jax.sharding import PartitionSpec as P

F32, BF16 = jnp.float32, jnp.bfloat16
NT = (((1,), (1,)), ((), ()))
TN = (((0,), (0,)), ((), ()))
TILE = 64
WIN = 128

def split3(x):
    a = x.astype(BF16); r = x - a.astype(F32)
    b = r.astype(BF16); r = r - b.astype(F32)
    return a, b, r.astype(BF16)

def kernel_body(nb, first, n_blk, heads, starts_ref, plane_ref, *refs):
    if first:
        (q_ref, g_ref, o_ref, tab_ref, *rest) = refs
        dq_out, vec_out, same_out, cross_out, kp, vp, dk_acc, dv_acc = rest[nb:]
        vec_ref = vec_out
    else:
        (q_ref, g_ref, vec_ref, dq_in, *rest) = refs
        dq_out, same_out, cross_out, kp, vp, dk_acc, dv_acc = rest[nb:]
    kv_refs = rest[:nb]
    hd = q_ref.shape[1]
    pad = WIN - TILE
    cols = TILE * heads
    tok = q_ref.shape[0] // heads
    c = hd ** -0.5 * math.log2(math.e)
    zero_pad = jnp.zeros((pad, hd), BF16)
    for b in range(nb):
        kp[b, :pad] = zero_pad
        vp[b, :pad] = zero_pad
        kp[b, pad:] = kv_refs[b][:tok]
        vp[b, pad:] = kv_refs[b][tok:2 * tok]
    dk_acc[...] = jnp.zeros_like(dk_acc)
    dv_acc[...] = jnp.zeros_like(dv_acc)
    sigs = [kv_refs[b][2 * tok:, :1].astype(F32) for b in range(nb)]

    def prep(i):
        rows = pl.ds(pl.multiple_of(i * cols, cols), cols)
        prod = g_ref[rows, :].astype(F32) * o_ref[rows, :].astype(F32)
        hi = prod.astype(BF16)
        lo = (prod - hi.astype(F32)).astype(BF16)
        ones = jnp.ones((8, 2 * hd), BF16)
        delta = lax.dot_general(ones, jnp.concatenate([hi, lo], axis=1), NT, preferred_element_type=F32)
        t = tab_ref[pl.ds(pl.multiple_of(i * TILE, TILE), TILE), :]
        w = t.shape[1]
        x = jnp.broadcast_to(t[:, None, :], (TILE, heads, w)).reshape(cols, w)
        lane = lax.broadcasted_iota(jnp.int32, (cols, w), 1)
        sub = lax.broadcasted_iota(jnp.int32, (cols, w), 0) % heads
        x = jnp.where((lane == sub) | (lane >= heads), x, 0.0)
        parts = split3(x)
        sel_row = lax.broadcasted_iota(jnp.int32, (16, w), 0)
        sel_lane = lax.broadcasted_iota(jnp.int32, (16, w), 1)
        sel = jnp.where((sel_row < 8) == (sel_lane < heads), 1.0, 0.0).astype(BF16)
        both = sum(lax.dot_general(sel, p_, NT, preferred_element_type=F32) for p_ in parts)
        vec_out[0:8, rows] = both[:8] * math.log2(math.e)
        vec_out[8:16, rows] = delta
        vec_out[16:24, rows] = both[8:]
        token = lax.broadcasted_iota(jnp.int32, (8, cols), 1) // heads + i * TILE
        vec_out[24:32, rows] = token.astype(F32) * n_blk + sigs[0][:8]

    def window(i, at, dq):
        rows = pl.ds(pl.multiple_of(i * cols, cols), cols)
        keys = pl.ds(pl.multiple_of(at, 64), WIN)
        qs, gs = q_ref[rows, :], g_ref[rows, :]
        kw = kp[:, keys, :].reshape(nb * WIN, hd)
        vw = vp[:, keys, :].reshape(nb * WIN, hd)
        lse = vec_ref[0:1, rows]
        delta = vec_ref[8:9, rows]
        begin = vec_ref[16:17, rows]
        s = lax.dot_general(kw, qs, NT, preferred_element_type=F32)
        dp = lax.dot_general(vw, gs, NT, preferred_element_type=F32)
        place = vec_ref[24:25, rows]
        key_row = (lax.broadcasted_iota(jnp.int32, (WIN, 1), 0) + (at - pad)).astype(F32) * n_blk
        key_place = jnp.concatenate([key_row + sg[:1] for sg in sigs], axis=0)
        ok = (key_place >= begin) & (key_place <= place)
        p = jnp.where(ok, jnp.exp2(s * c - lse), 0.0)
        ds = p * (dp - delta)
        p_low, ds_low = p.astype(BF16), ds.astype(BF16)
        dv = jnp.dot(p_low, gs, preferred_element_type=F32)
        dk = jnp.dot(ds_low, qs, preferred_element_type=F32)
        dv_acc[:, keys, :] += dv.reshape(nb, WIN, hd)
        dk_acc[:, keys, :] += dk.reshape(nb, WIN, hd)
        return dq + lax.dot_general(kw, ds_low, TN, preferred_element_type=F32)

    def tile(i, carry):
        rows = pl.ds(pl.multiple_of(i * cols, cols), cols)
        if first:
            prep(i)
            dq = jnp.zeros((hd, cols), F32)
        else:
            dq = dq_in[:, rows]
        dq = window(i, i * TILE, dq)
        low = starts_ref[i * TILE] // n_blk
        far = jnp.maximum((i - 1) * TILE - low + WIN - 1, 0) // WIN
        def more(w, dq):
            return window(i, jnp.maximum(i * TILE - (w + 1) * WIN, 0), dq)
        dq = lax.fori_loop(0, far, more, dq)
        if first:
            dq_out[:, rows] = dq
        else:
            dq_out[rows, :] = (dq * hd ** -0.5).T.astype(BF16)
        return carry

    lax.fori_loop(0, tok // TILE, tile, 0)
    keeps_keys = plane_ref[0] == 0
    for b in range(nb):
        dk = dk_acc[b, pad:] * hd ** -0.5
        dv = dv_acc[b, pad:]
        same_out[b] = jnp.where(keeps_keys, dk, dv).astype(same_out.dtype)
        cross_out[b] = jnp.where(keeps_keys, dv, dk).astype(cross_out.dtype)


def grads(nb, first, n_blk, heads, vmem_mib=40):
    def call(starts, plane, *args):
        rows, hd = args[0].shape
        tok = rows // heads
        vm = pl.BlockSpec(memory_space=pltpu.VMEM)
        S = jax.ShapeDtypeStruct
        outs = [S((hd, rows), F32), S((32, rows), F32)] if first else [S((rows, hd), BF16)]
        outs += [S((nb, tok, hd), F32 if first else BF16), S((nb, tok, hd), BF16)]
        pad = WIN - TILE
        return pl.pallas_call(
            functools.partial(kernel_body, nb, first, n_blk, heads),
            out_shape=outs,
            in_specs=[pl.BlockSpec(memory_space=pltpu.SMEM)] * 2 + [vm] * len(args),
            out_specs=[vm] * len(outs),
            scratch_shapes=[pltpu.VMEM((nb, tok + pad, hd), BF16)] * 2 + [pltpu.VMEM((nb, tok + pad, hd), F32)] * 2,
            compiler_params=pltpu.CompilerParams(vmem_limit_bytes=vmem_mib * 2**20),
            cost_estimate=pl.CostEstimate(flops=nb * tok * tok * heads * hd * 4, bytes_accessed=8 * 2**20, transcendentals=nb * tok * tok * heads // 2),
        )(starts, plane, *args)
    return call


def move(block, axes, pairs):
    return lax.ppermute(block, axes, pairs)


def on_device(queries, out_grad, outputs, keys, values, logsumexp, positions, doc_start):
    n = lax.axis_size("blk")
    tok, heads, hd = queries.shape
    devices = range(n)
    plane = lax.axis_index("head")
    kv = jnp.concatenate([keys, values, jnp.full((16, hd), positions[0], BF16)], axis=0)

    two_back = [(s, (s - 2) % n) for s in devices]
    odd_even = [(s, (s - 1) % n if s % 2 else (s - 3) % n) for s in devices]
    cores = [(s, s ^ 1) for s in devices]
    kv_a = move(kv, "blk", two_back)
    kv_b = move(kv, "blk", odd_even)
    kv_c = move(kv_a, "blk", cores)

    q, g, o = (x.reshape(tok * heads, hd) for x in (queries, out_grad, outputs))
    begin = doc_start.astype(F32)[:, None]
    table = jnp.concatenate([logsumexp, begin, jnp.zeros((tok, 7), F32)], axis=1)
    which = plane.astype(jnp.int32).reshape(1)
    dq, vec, own_same, own_cross = grads(1, True, n, heads)(doc_start, which, q, g, o, table, kv)
    dq, same, cross = grads(3, False, n, heads)(doc_start, which, q, g, vec, dq, kv_a, kv_b, kv_c)

    other = [(0, 1), (1, 0)]
    got = [move(own_cross[0], "head", other)]
    near = move(jnp.stack([same[2], cross[2]]), "blk", cores)
    both = lambda pairs, flip: [(2 * d + h, 2 * t + (h ^ flip)) for d, t in pairs for h in range(2)]
    back = lambda pairs: [(t, s) for s, t in pairs]
    got.append(move(same[0] + near[0], ("blk", "head"), both(back(two_back), 0)))
    got.append(move(cross[0] + near[1], ("blk", "head"), both(back(two_back), 1)))
    got.append(move(same[1], ("blk", "head"), both(back(odd_even), 0)))
    got.append(move(cross[1], ("blk", "head"), both(back(odd_even), 1)))
    total = own_same[0]
    for part in got:
        total = total + part.astype(F32)
    mine = total.astype(BF16)
    theirs = move(mine, "head", other)
    key_grad = jnp.where(plane == 0, mine, theirs)
    value_grad = jnp.where(plane == 0, theirs, mine)
    return dq.reshape(tok, heads, hd), key_grad, value_grad


def solution(mesh):
    in_specs = (
        P("blk", "head", None),
        P("blk", "head", None),
        P("blk", "head", None),
        P("blk", None),
        P("blk", None),
        P("blk", "head"),
        P("blk"),
        P("blk"),
    )
    out_specs = (P("blk", "head", None), P("blk", None), P("blk", None))
    return jax.shard_map(on_device, mesh=mesh, in_specs=in_specs, out_specs=out_specs, check_vma=False)
```

time: 120 us -> 58.6 us (0.49)
  matrix products: 59.4 us -> 0 us
  blocking collectives: 20.6 us -> 0 us
  Pallas kernels: 0 us -> 16.9 us
  starting transfers between devices: 26.8 us -> 12.9 us
  waiting for transfers between devices: 7.5 us -> 18.2 us
  local copies, waits for them, and re-layouts: 2.48 us -> 5.74 us
  other arithmetic: 2.42 us -> 4.22 us
    dot_general x20 -> x0, matrix products: 59.4 us -> none  [the longest x4 18.5 us: block_grads(): jnp.einsum('thd,kd->htk', out_grad, value_vectors, preferred_element_type...]
    psum x1 -> x0, blocking collectives: 20.6 us -> none  [on_device(): key_total, value_total = lax.psum((key_total, value_total), 'head')]
    pallas_call x0 -> x2, Pallas kernels: none -> 16.9 us  [call(): pl.pallas_call(functools.partial(kernel_body, nb, first, n_blk, heads), o...]
    ppermute x17 -> x10, starting transfers between devices: 26.8 us -> 12.9 us  [move(): return lax.ppermute(block, axes, pairs)]
    ppermute x17 -> x10, waiting for transfers between devices: 7.5 us -> 18.2 us  [move(): return lax.ppermute(block, axes, pairs)]
    unnamed x37 -> x8, local copies, waits for them, and re-layouts: 2.39 us -> 4.35 us
    concatenate x0 -> x2, other arithmetic: none -> 1.96 us  [the longest x1 1.17 us: on_device(): jnp.concatenate([keys, values, jnp.full((16, hd), positions[0], BF16)], a...]
  transfers between devices with their start and end apart: 17 -> 10, of which waited for: 6 -> 5; matrix products, arithmetic and copies ran while one was open for 52% -> 3% of each run, Pallas kernels for 0% -> 12%
where the time goes in v1:
time: 58.6 us
  waiting for transfers between devices  18.2 us (31%)
  Pallas kernels  16.9 us (29%)
  starting transfers between devices  12.9 us (22%)
  local copies, waits for them, and re-layouts  5.74 us (10%)
  other arithmetic  4.22 us (7%)
  between operations  0.73 us (1%)
    ppermute x10, waiting for transfers between devices, move(): return lax.ppermute(block, axes, pairs)  18.2 us
    pallas_call x2, Pallas kernels, call(): pl.pallas_call(functools.partial(kernel_body, nb, first, n_blk, heads), o...  16.9 us
    ppermute x10, starting transfers between devices, move(): return lax.ppermute(block, axes, pairs)  12.9 us
    unnamed x8, local copies, waits for them, and re-layouts  4.35 us
    concatenate x1, other arithmetic, on_device(): jnp.concatenate([keys, values, jnp.full((16, hd), positions[0], BF16)], a...  1.17 us
  transfers between devices with their start and end apart: 10, of which 5 were waited for; matrix products, arithmetic and copies ran while one was open for 3% of the time, Pallas kernels for 12%

profile of v1, /device:TPU:0, one launch (start us, length us, event | category | flops | bytes accessed | tf_op | source)
XLA Modules:
  0.0 58.6 jit_solution(12569058070213233903)
XLA Ops:
  0.6 0.7 %convert.3 = bf16[512]{0:T(512)(128)(2,1)S(1)} convert(s32[512]{0:T(512)} %param.14) | non-fusion elementwise | flops 512 | bytes 3072 | tf_op jit(solution)/shard_map/convert
  1.3 0.5 slice.28
  1.8 0.6 %broadcast_in_dim.11 = bf16[16]{0:T(256)(128)(2,1)S(1)} broadcast(bf16[]{:T(256)} %bitcast.5), dimensions={} | broadcast | bytes 34 | tf_op jit(solution)/shard_map/broadcast_in_dim | solution.py:150
  2.5 1.2 %maximum_maximum_fusion.refs_4_ = bf16[1040,128]{1,0:T(8,128)(2,1)S(1)} fusion(bf16[512,128]{1,0:T(8,128)(2,1)} %param.12, bf16[512,128]{1,0:T(8,128)(2,1)} %param.11, bf16[1040]{0:T(1024)(128)(2,1)S(1)} %pad.4.clone), kind=kLoop, calls=%fused_computation | loop fusion | flops 798720 | bytes 530464 | tf_op jit(solution)/shard_map/concatenate | solution.py:150
  3.7 6.1 %collective-permute-start = (bf16[1040,128]{1,0:T(8,128)(2,1)S(1)}, bf16[1040,128]{1,0:T(8,128)(2,1)S(1)}, u32[]{:S(2)}, u32[]{:S(2)}) collective-permute-start(bf16[1040,128]{1,0:T(8,128)(2,1)S(1)} %maximum_maximum_fusion.refs_4_), channel_id=1, source_target_pairs={{0,28},{2,30},{4,0},{6,2},{8,4},{10,6},{12,8},{14,10},{16,12},{18,... | collective-permute-start | bytes 798728 | tf_op jit(solution)/shard_map/ppermute | solution.py:142
  9.8 0.0 collective-permute-start.1
  9.8 0.7 %convert_element_type.25 = f32[512]{0:T(512)S(1)} convert(s32[512]{0:T(512)} %starts_ref.3) | non-fusion elementwise | flops 512 | bytes 4096 | tf_op jit(solution)/shard_map/convert_element_type | solution.py:160
  10.5 0.1 pad.7.clone
  10.5 4.9 %collective-permute-done.refs_4_ = bf16[1040,128]{1,0:T(8,128)(2,1)S(1)} collective-permute-done((bf16[1040,128]{1,0:T(8,128)(2,1)S(1)}, bf16[1040,128]{1,0:T(8,128)(2,1)S(1)}, u32[]{:S(2)}, u32[]{:S(2)}) %collective-permute-start) | collective-permute-done | bytes 266272 | tf_op jit(solution)/shard_map/ppermute | solution.py:142
  15.4 0.0 collective-permute-start.2
  15.4 0.8 %maximum_maximum_fusion.1 = f32[512,16]{0,1:T(8,128)S(1)} fusion(f32[512,1]{0,1:T(1,128)S(1)} %bitcast.34, f32[512,8]{0,1:T(8,128)} %param.13, f32[16]{0:T(128)S(1)} %pad.7.clone), kind=kLoop, calls=%fused_computation.16 | loop fusion | flops 16384 | bytes 51264 | tf_op jit(solution)/shard_map/concatenate | solution.py:161
  16.2 0.1 copy.14.refs_3_
  16.3 0.0 copy-start
  16.3 0.7 %copy-done = s32[512]{0:T(512)S(1)} copy-done((s32[512]{0:T(512)S(1)}, s32[512]{0:T(512)}, u32[]{:S(2)}) %copy-start) | copy-done | bytes 2072
  17.0 0.0 copy-start.1
  17.0 1.2 %copy-done.1 = bf16[512,8,128]{2,1,0:T(8,128)(2,1)S(1)} copy-done((bf16[512,8,128]{2,1,0:T(8,128)(2,1)S(1)}, bf16[512,8,128]{2,1,0:T(8,128)(2,1)}, u32[]{:S(2)}) %copy-start.1) | copy-done | bytes 1048600
  18.3 0.0 copy-start.2
  18.3 1.2 %copy-done.2 = bf16[512,8,128]{2,1,0:T(8,128)(2,1)S(1)} copy-done((bf16[512,8,128]{2,1,0:T(8,128)(2,1)S(1)}, bf16[512,8,128]{2,1,0:T(8,128)(2,1)}, u32[]{:S(2)}) %copy-start.2) | copy-done | bytes 1048600
  19.5 0.0 copy-start.3
  19.5 1.2 %copy-done.3 = bf16[512,8,128]{2,1,0:T(8,128)(2,1)S(1)} copy-done((bf16[512,8,128]{2,1,0:T(8,128)(2,1)S(1)}, bf16[512,8,128]{2,1,0:T(8,128)(2,1)}, u32[]{:S(2)}) %copy-start.3) | copy-done | bytes 1048600
  20.7 6.8 %shard_map.103 = (f32[128,4096]{1,0:T(8,128)S(1)}, f32[32,4096]{1,0:T(8,128)S(1)}, f32[1,512,128]{2,1,0:T(8,128)S(1)}, bf16[1,512,128]{2,1,0:T(8,128)(2,1)S(1)}) custom-call(s32[512]{0:T(512)S(1)} %copy-done, s32[1]{0:T(128)} %bitcast.plane_ref, bf16[4096,128]{1,0:T(8,128)(2,1)S(1)} %bitcast.29, bf16[4096,128]{1,0:T(8,128)(2,1)S(1)} %bitcast.31, ...), custom_call_target="tpu_custom_call" | custom-call | flops 1073741824 | bytes 8388608 | tf_op jit(solution)/shard_map/pallas_call | solution.py:129
  27.5 0.0 collective-permute-done.1.refs_5_
  27.5 0.0 collective-permute-done.2.refs_6_
  27.5 10.1 %shard_map.104 = (bf16[4096,128]{1,0:T(8,128)(2,1)}, bf16[3,512,128]{2,1,0:T(8,128)(2,1)S(1)}, bf16[3,512,128]{2,1,0:T(8,128)(2,1)S(1)}) custom-call(s32[512]{0:T(512)S(1)} %copy-done, s32[1]{0:T(128)} %bitcast.plane_ref, bf16[4096,128]{1,0:T(8,128)(2,1)S(1)} %bitcast.30, bf16[4096,128]{1,0:T(8,128)(2,1)S(1)} %bitcast.32, ...), custom_call_target="tpu_custom_call" | custom-call | flops 3221225472 | bytes 8388608 | tf_op jit(solution)/shard_map/pallas_call | solution.py:129
  37.7 0.6 collective-permute-start.4
  38.3 1.5 %collective-permute-start.3 = (bf16[512,128]{1,0:T(8,128)(2,1)S(1)}, bf16[512,128]{1,0:T(8,128)(2,1)S(1)}, u32[]{:S(2)}, u32[]{:S(2)}) collective-permute-start(bf16[512,128]{1,0:T(8,128)(2,1)S(1)} %bitcast.33), channel_id=1, source_target_pairs={{0,1},{1,0},{2,3},{3,2},{4,5},{5,4},{6,7},{7,6},{8,9},{9,8},{10,11... | collective-permute-start | bytes 393224 | tf_op jit(solution)/shard_map/ppermute | solution.py:142
  39.7 0.0 collective-permute-done.4
  39.8 0.4 collective-permute-start.5
  40.2 1.2 %collective-permute-start.6 = (bf16[512,128]{1,0:T(8,128)(2,1)S(1)}, bf16[512,128]{1,0:T(8,128)(2,1)S(1)}, u32[]{:S(2)}, u32[]{:S(2)}) collective-permute-start(bf16[512,128]{1,0:T(8,128)(2,1)S(1)} %get-tuple-element.24), channel_id=1, source_target_pairs={{28,1},{29,0},{30,3},{31,2},{0,5},{1,4},{2,7},{3,6},{4,9},{5,8},{6... | collective-permute-start | bytes 393224 | tf_op jit(solution)/shard_map/ppermute | solution.py:142
  41.4 0.0 collective-permute-start.7
  41.4 2.2 %collective-permute-start.8 = (bf16[512,128]{1,0:T(8,128)(2,1)S(1)}, bf16[512,128]{1,0:T(8,128)(2,1)S(1)}, u32[]{:S(2)}, u32[]{:S(2)}) collective-permute-start(bf16[512,128]{1,0:T(8,128)(2,1)S(1)} %get-tuple-element.23), channel_id=1, source_target_pairs={{26,1},{27,0},{0,3},{1,2},{30,5},{31,4},{4,7},{5,6},{2,9},{3,8},{8... | collective-permute-start | bytes 393224 | tf_op jit(solution)/shard_map/ppermute | solution.py:142
  43.6 1.1 %collective-permute-done.3 = bf16[512,128]{1,0:T(8,128)(2,1)S(1)} collective-permute-done((bf16[512,128]{1,0:T(8,128)(2,1)S(1)}, bf16[512,128]{1,0:T(8,128)(2,1)S(1)}, u32[]{:S(2)}, u32[]{:S(2)}) %collective-permute-start.3) | collective-permute-done | bytes 131104 | tf_op jit(solution)/shard_map/ppermute | solution.py:142
  44.6 4.8 %collective-permute-done.5 = bf16[512,128]{1,0:T(8,128)(2,1)S(1)} collective-permute-done((bf16[512,128]{1,0:T(8,128)(2,1)S(1)}, bf16[512,128]{1,0:T(8,128)(2,1)S(1)}, u32[]{:S(2)}, u32[]{:S(2)}) %collective-permute-start.5) | collective-permute-done | bytes 131104 | tf_op jit(solution)/shard_map/ppermute | solution.py:142
  49.4 3.4 %collective-permute-done.6 = bf16[512,128]{1,0:T(8,128)(2,1)S(1)} collective-permute-done((bf16[512,128]{1,0:T(8,128)(2,1)S(1)}, bf16[512,128]{1,0:T(8,128)(2,1)S(1)}, u32[]{:S(2)}, u32[]{:S(2)}) %collective-permute-start.6) | collective-permute-done | bytes 131104 | tf_op jit(solution)/shard_map/ppermute | solution.py:142
  52.8 0.0 collective-permute-done.7
  52.8 0.0 collective-permute-done.8
  52.8 0.1 fusion.4
  52.9 1.0 %collective-permute-start.9 = (bf16[512,128]{1,0:T(8,128)(2,1)S(1)}, bf16[512,128]{1,0:T(8,128)(2,1)S(1)}, u32[]{:S(2)}, u32[]{:S(2)}) collective-permute-start(bf16[512,128]{1,0:T(8,128)(2,1)S(1)} %fusion.4), channel_id=1, source_target_pairs={{0,1},{1,0},{2,3},{3,2},{4,5},{5,4},{6,7},{7,6},{8,9},{9,8},{10,11... | collective-permute-start | bytes 393224 | tf_op jit(solution)/shard_map/ppermute | solution.py:142
  53.9 4.1 %collective-permute-done.9 = bf16[512,128]{1,0:T(8,128)(2,1)S(1)} collective-permute-done((bf16[512,128]{1,0:T(8,128)(2,1)S(1)}, bf16[512,128]{1,0:T(8,128)(2,1)S(1)}, u32[]{:S(2)}, u32[]{:S(2)}) %collective-permute-start.9) | collective-permute-done | bytes 131104 | tf_op jit(solution)/shard_map/ppermute | solution.py:142
  57.9 0.7 %broadcast_select_fusion = (bf16[512,128]{1,0:T(8,128)(2,1)}, bf16[512,128]{1,0:T(8,128)(2,1)}) fusion(bf16[512,128]{1,0:T(8,128)(2,1)S(1)} %collective-permute-done.9, bf16[512,128]{1,0:T(8,128)(2,1)S(1)} %fusion.4, pred[]{:T(512)S(6)} %eq.4), kind=kLoop, calls=%fused_computation.14 | loop fusion | flops 131072 | bytes 524289 | tf_op jit(solution)/shard_map/jit(_where)/select_n | solution.py:181
  (6 shorter events, 0.1 us)
Async XLA Ops:
  3.7 11.7 %collective-permute-start = (bf16[1040,128]{1,0:T(8,128)(2,1)S(1)}, bf16[1040,128]{1,0:T(8,128)(2,1)S(1)}, u32[]{:S(2)}, u32[]{:S(2)}) collective-permute-start(bf16[1040,128]{1,0:T(8,128)(2,1)S(1)} %maximum_maximum_fusion.refs_4_), channel_id=1, source_target_pairs={{0,28},{2,30},{4,0},{6,2},{8,4},{10,6},{12,8},{14,10},{16,12},{18,... | collective-permute-start | bytes 798728 | tf_op jit(solution)/shard_map/ppermute | solution.py:142
  9.8 17.7 %collective-permute-start.1 = (bf16[1040,128]{1,0:T(8,128)(2,1)S(1)}, bf16[1040,128]{1,0:T(8,128)(2,1)S(1)}, u32[]{:S(2)}, u32[]{:S(2)}) collective-permute-start(bf16[1040,128]{1,0:T(8,128)(2,1)S(1)} %maximum_maximum_fusion.refs_4_), channel_id=1, source_target_pairs={{0,26},{2,0},{4,30},{6,4},{8,2},{10,8},{12,6},{14,12},{16,10},{18,... | collective-permute-start | bytes 798728 | tf_op jit(solution)/shard_map/ppermute | solution.py:142
  15.4 12.1 %collective-permute-start.2 = (bf16[1040,128]{1,0:T(8,128)(2,1)S(1)}, bf16[1040,128]{1,0:T(8,128)(2,1)S(1)}, u32[]{:S(2)}, u32[]{:S(2)}) collective-permute-start(bf16[1040,128]{1,0:T(8,128)(2,1)S(1)} %collective-permute-done.refs_4_), channel_id=1, source_target_pairs={{0,2},{2,0},{4,6},{6,4},{8,10},{10,8},{12,14},{14,12},{16,18},{18,... | collective-permute-start | bytes 798728 | tf_op jit(solution)/shard_map/ppermute | solution.py:142
  16.3 0.7 %copy-start = (s32[512]{0:T(512)S(1)}, s32[512]{0:T(512)}, u32[]{:S(2)}) copy-start(s32[512]{0:T(512)} %starts_ref.3) | copy-start | bytes 6148
  17.0 1.2 %copy-start.1 = (bf16[512,8,128]{2,1,0:T(8,128)(2,1)S(1)}, bf16[512,8,128]{2,1,0:T(8,128)(2,1)}, u32[]{:S(2)}) copy-start(bf16[512,8,128]{2,1,0:T(8,128)(2,1)} %param.10) | copy-start | bytes 3145732
  18.3 1.2 %copy-start.2 = (bf16[512,8,128]{2,1,0:T(8,128)(2,1)S(1)}, bf16[512,8,128]{2,1,0:T(8,128)(2,1)}, u32[]{:S(2)}) copy-start(bf16[512,8,128]{2,1,0:T(8,128)(2,1)} %param.8) | copy-start | bytes 3145732
  19.5 1.2 %copy-start.3 = (bf16[512,8,128]{2,1,0:T(8,128)(2,1)S(1)}, bf16[512,8,128]{2,1,0:T(8,128)(2,1)}, u32[]{:S(2)}) copy-start(bf16[512,8,128]{2,1,0:T(8,128)(2,1)} %param.9) | copy-start | bytes 3145732
  37.7 2.1 %collective-permute-start.4 = (bf16[2,512,128]{2,1,0:T(8,128)(2,1)S(1)}, bf16[2,512,128]{2,1,0:T(8,128)(2,1)S(1)}, u32[]{:S(2)}, u32[]{:S(2)}) collective-permute-start(bf16[2,512,128]{2,1,0:T(8,128)(2,1)S(1)} %pad_maximum_fusion), channel_id=1, source_target_pairs={{0,2},{2,0},{4,6},{6,4},{8,10},{10,8},{12,14},{14,12},{16,18},{18,... | collective-permute-start | bytes 786440 | tf_op jit(solution)/shard_map/ppermute | solution.py:142
  38.3 6.4 %collective-permute-start.3 = (bf16[512,128]{1,0:T(8,128)(2,1)S(1)}, bf16[512,128]{1,0:T(8,128)(2,1)S(1)}, u32[]{:S(2)}, u32[]{:S(2)}) collective-permute-start(bf16[512,128]{1,0:T(8,128)(2,1)S(1)} %bitcast.33), channel_id=1, source_target_pairs={{0,1},{1,0},{2,3},{3,2},{4,5},{5,4},{6,7},{7,6},{8,9},{9,8},{10,11... | collective-permute-start | bytes 393224 | tf_op jit(solution)/shard_map/ppermute | solution.py:142
  39.8 9.6 %collective-permute-start.5 = (bf16[512,128]{1,0:T(8,128)(2,1)S(1)}, bf16[512,128]{1,0:T(8,128)(2,1)S(1)}, u32[]{:S(2)}, u32[]{:S(2)}) collective-permute-start(bf16[512,128]{1,0:T(8,128)(2,1)S(1)} %get-tuple-element.17), channel_id=1, source_target_pairs={{28,0},{29,1},{30,2},{31,3},{0,4},{1,5},{2,6},{3,7},{4,8},{5,9},{6... | collective-permute-start | bytes 393224 | tf_op jit(solution)/shard_map/ppermute | solution.py:142
  40.2 12.6 %collective-permute-start.6 = (bf16[512,128]{1,0:T(8,128)(2,1)S(1)}, bf16[512,128]{1,0:T(8,128)(2,1)S(1)}, u32[]{:S(2)}, u32[]{:S(2)}) collective-permute-start(bf16[512,128]{1,0:T(8,128)(2,1)S(1)} %get-tuple-element.24), channel_id=1, source_target_pairs={{28,1},{29,0},{30,3},{31,2},{0,5},{1,4},{2,7},{3,6},{4,9},{5,8},{6... | collective-permute-start | bytes 393224 | tf_op jit(solution)/shard_map/ppermute | solution.py:142
  41.4 11.4 %collective-permute-start.7 = (bf16[512,128]{1,0:T(8,128)(2,1)S(1)}, bf16[512,128]{1,0:T(8,128)(2,1)S(1)}, u32[]{:S(2)}, u32[]{:S(2)}) collective-permute-start(bf16[512,128]{1,0:T(8,128)(2,1)S(1)} %get-tuple-element.18), channel_id=1, source_target_pairs={{26,0},{27,1},{0,2},{1,3},{30,4},{31,5},{4,6},{5,7},{2,8},{3,9},{8... | collective-permute-start | bytes 393224 | tf_op jit(solution)/shard_map/ppermute | solution.py:142
  41.4 11.4 %collective-permute-start.8 = (bf16[512,128]{1,0:T(8,128)(2,1)S(1)}, bf16[512,128]{1,0:T(8,128)(2,1)S(1)}, u32[]{:S(2)}, u32[]{:S(2)}) collective-permute-start(bf16[512,128]{1,0:T(8,128)(2,1)S(1)} %get-tuple-element.23), channel_id=1, source_target_pairs={{26,1},{27,0},{0,3},{1,2},{30,5},{31,4},{4,7},{5,6},{2,9},{3,8},{8... | collective-permute-start | bytes 393224 | tf_op jit(solution)/shard_map/ppermute | solution.py:142
  52.9 5.0 %collective-permute-start.9 = (bf16[512,128]{1,0:T(8,128)(2,1)S(1)}, bf16[512,128]{1,0:T(8,128)(2,1)S(1)}, u32[]{:S(2)}, u32[]{:S(2)}) collective-permute-start(bf16[512,128]{1,0:T(8,128)(2,1)S(1)} %fusion.4), channel_id=1, source_target_pairs={{0,1},{1,0},{2,3},{3,2},{4,5},{5,4},{6,7},{7,6},{8,9},{9,8},{10,11... | collective-permute-start | bytes 393224 | tf_op jit(solution)/shard_map/ppermute | solution.py:142

commit v2 on v0

v2 whole, which is shorter than its diff:
```python
import functools
import math

import jax
import jax.numpy as jnp
from jax import lax
from jax.experimental import pallas as pl
from jax.experimental.pallas import tpu as pltpu
from jax.sharding import PartitionSpec as P

F32, BF16 = jnp.float32, jnp.bfloat16
NT = (((1,), (1,)), ((), ()))
TN = (((0,), (0,)), ((), ()))
NN = (((1,), (0,)), ((), ()))
TILE = 64
WIN = 128
LOG2E = math.log2(math.e)


def dot(a, b, dims):
    return lax.dot_general(a, b, dims, preferred_element_type=F32)


def split3(x):
    high = x.astype(BF16)
    rest = x - high.astype(F32)
    mid = rest.astype(BF16)
    return high, mid, (rest - mid.astype(F32)).astype(BF16)


def columns(i, cols):
    return pl.ds(i * cols, cols)


def prep_kernel(
    q_hbm, g_hbm, o_hbm, places_hbm, starts_hbm, lse_hbm,
    vec_ref, q_ref, g_ref, o_ref, places_ref, starts_ref, lse_ref, sems, row_sems,
):
    heads, tok = lse_ref.shape
    hd = g_ref.shape[1]
    part = 128
    cols = part * heads
    pairs = ((g_hbm, g_ref), (o_hbm, o_ref), (q_hbm, q_ref))
    copies = [
        [
            pltpu.make_async_copy(src.at[columns(i, cols)], dst.at[columns(i, cols)], sems.at[m, i])
            for i in range(tok // part)
        ]
        for m, (src, dst) in enumerate(pairs)
    ]
    small = ((places_hbm, places_ref), (starts_hbm, starts_ref), (lse_hbm, lse_ref))
    small = [pltpu.make_async_copy(x, y, row_sems.at[m]) for m, (x, y) in enumerate(small)]
    for copy in small + copies[0] + copies[1] + copies[2]:
        copy.start()
    for copy in small:
        copy.wait()
    spread = lax.broadcasted_iota(jnp.int32, (part, cols), 1) // heads == lax.broadcasted_iota(
        jnp.int32, (part, cols), 0
    )
    spread = jnp.where(spread, 1.0, 0.0).astype(BF16)
    own = lax.broadcasted_iota(jnp.int32, (heads, cols), 1) % heads == lax.broadcasted_iota(
        jnp.int32, (heads, cols), 0
    )
    ones = jnp.ones((8, 2 * hd), BF16)
    for i in range(tok // part):
        rows, lanes = columns(i, cols), pl.ds(i * part, part)
        lse = sum(dot(x, spread, NN) for x in split3(lse_ref[:, lanes] * LOG2E))
        lse = jnp.sum(jnp.where(own, lse, 0.0), axis=0, keepdims=True)
        vec_ref[0:8, rows] = jnp.broadcast_to(lse, (8, cols))
        for at, ref in ((16, starts_ref), (24, places_ref)):
            row = jnp.broadcast_to(ref[:, lanes].astype(F32), (8, part))
            vec_ref[at : at + 8, rows] = sum(dot(x, spread, NN) for x in split3(row)[:2])
        copies[0][i].wait()
        copies[1][i].wait()
        prod = g_ref[rows, :].astype(F32) * o_ref[rows, :].astype(F32)
        high = prod.astype(BF16)
        low = (prod - high.astype(F32)).astype(BF16)
        vec_ref[8:16, rows] = dot(ones, jnp.concatenate([high, low], axis=1), NT)
    for copy in copies[2]:
        copy.wait()


def grads_kernel(nb, n_blk, starts_ref, vec_ref, q_ref, g_ref, *refs):
    ks, vs, places, refs = refs[:nb], refs[nb : 2 * nb], refs[2 * nb : 3 * nb], refs[3 * nb :]
    dq_ref, own_ref, c_ref, a_ref, b_ref, dk_acc, dv_acc = refs
    hd = q_ref.shape[1]
    tok = ks[0].shape[0]
    heads = q_ref.shape[0] // tok
    tiles = tok // TILE
    cols = TILE * heads
    scale = hd**-0.5
    dk_acc[...] = jnp.zeros_like(dk_acc)
    dv_acc[...] = jnp.zeros_like(dv_acc)

    def window(i, at, top):
        rows = columns(i, cols)
        keys = pl.ds(at, WIN)
        qs, gs = q_ref[rows, :], g_ref[rows, :]
        kw = jnp.concatenate([k[keys, :] for k in ks], axis=0)
        vw = jnp.concatenate([v[keys, :] for v in vs], axis=0)
        lse, delta = vec_ref[0:1, rows], vec_ref[8:9, rows]
        begin, place = vec_ref[16:17, rows], vec_ref[24:25, rows]
        s = dot(kw, qs, NT)
        dp = dot(vw, gs, NT)
        row = lax.broadcasted_iota(jnp.int32, (WIN, cols), 0) + at
        row_place = (row * n_blk).astype(F32)
        oks = []
        for p in places:
            first = p[0:1, 0:1].astype(F32)
            ok = row_place >= begin - first
            oks.append(ok & (row_place <= place - first if top is None else row < top))
        ok = jnp.concatenate(oks, axis=0)
        attend = jnp.where(ok, jnp.exp2(s * (scale * LOG2E) - lse), 0.0)
        low = (attend * (dp - delta)).astype(BF16)
        dv = dot(attend.astype(BF16), gs, NN)
        dk = dot(low, qs, NN)
        for b in range(nb):
            dv_acc[b, keys, :] += dv[b * WIN : (b + 1) * WIN]
            dk_acc[b, keys, :] += dk[b * WIN : (b + 1) * WIN]
        return dot(kw, low, TN)

    for i in range(tiles):
        dq_ref[:, columns(i, cols)] = window(i, max((i + 1) * TILE - WIN, 0), None)
    for i in range(tiles):
        top = (i + 1) * TILE - WIN
        if top <= 0:
            continue
        far = jnp.maximum(top - starts_ref[i * TILE] // n_blk + WIN - 1, 0) // WIN

        def more(w, carry, i=i, top=top):
            edge = top - w * WIN
            at = pl.multiple_of(jnp.maximum(edge - WIN, 0), TILE)
            dq_ref[:, columns(i, cols)] += window(i, at, edge)
            return carry

        lax.fori_loop(0, far, more, 0)

    for b, out in enumerate((own_ref, a_ref, b_ref, c_ref)):
        out[0] = (dk_acc[b] * scale).astype(out.dtype)
        out[1] = dv_acc[b].astype(out.dtype)


def finish_kernel(heads, dq_ref, out_ref):
    hd, rows = dq_ref.shape
    cols = TILE * heads
    for i in range(rows // cols):
        at = columns(i, cols)
        out_ref[at, :] = (dq_ref[:, at] * hd**-0.5).T.astype(BF16)


def call(body, outs, specs, scratch, flops, *args):
    vmem = pl.BlockSpec(memory_space=pltpu.VMEM)
    return pl.pallas_call(
        body,
        out_shape=outs,
        in_specs=specs + [vmem] * (len(args) - len(specs)),
        out_specs=jax.tree.map(lambda _: vmem, outs),
        scratch_shapes=scratch,
        compiler_params=pltpu.CompilerParams(vmem_limit_bytes=32 * 2**20),
        cost_estimate=pl.CostEstimate(flops=flops, bytes_accessed=4 * 2**20, transcendentals=0),
    )(*args)


def on_device(queries, out_grad, outputs, keys, values, logsumexp, positions, doc_start):
    n = lax.axis_size("blk")
    tok, heads, hd = queries.shape
    rows = tok * heads
    shape = jax.ShapeDtypeStruct
    blocks = range(n)

    two_back = [(s, (s - 2) % n) for s in blocks]
    odd_even = [(s, (s - 1) % n if s % 2 else (s - 3) % n) for s in blocks]
    cores = [(s, s ^ 1) for s in blocks]
    move = lambda group, pairs: tuple(lax.ppermute(x, "blk", pairs) for x in group)
    mine = (keys, values, positions)
    a = move(mine, two_back)
    b = move(mine, odd_even)

    q, g, o = (x.reshape(rows, hd) for x in (queries, out_grad, outputs))
    line = lambda x: x.reshape(1, tok)
    vec, q, g = call(
        prep_kernel,
        [shape((32, rows), F32)] + [shape((rows, hd), BF16)] * 2,
        [pl.BlockSpec(memory_space=pltpu.HBM)] * 6,
        [
            pltpu.VMEM((rows, hd), BF16),
            pltpu.VMEM((1, tok), jnp.int32),
            pltpu.VMEM((1, tok), jnp.int32),
            pltpu.VMEM((heads, tok), F32),
            pltpu.SemaphoreType.DMA((3, tok // 128)),
            pltpu.SemaphoreType.DMA((3,)),
        ],
        2**32,
        *(
            pltpu.with_memory_space_constraint(x, pltpu.HBM)
            for x in (q, g, o, line(positions), line(doc_start), logsumexp.T)
        ),
    )
    a, vec = lax.optimization_barrier((a, vec))
    c = move(a, cores)
    part = shape((2, tok, hd), BF16)
    groups = (mine, a, b, c)
    dq, own, c_part, a_part, b_part = call(
        functools.partial(grads_kernel, 4, n),
        [shape((hd, rows), F32), shape((2, tok, hd), F32), part, part, part],
        [pl.BlockSpec(memory_space=pltpu.SMEM)],
        [pltpu.VMEM((4, tok, hd), F32)] * 2,
        2**35,
        doc_start, vec, q, g, *(x[0] for x in groups), *(x[1] for x in groups), *(line(x[2]) for x in groups),
    )

    other = [(0, 1), (1, 0)]
    back = lambda x, pairs: lax.ppermute(x, "blk", [(d, s) for s, d in pairs])
    near = lax.ppermute(c_part, "blk", cores)
    from_b = back(b_part, odd_even)
    from_a = [back(a_part[i] + near[i], two_back) for i in range(2)]
    query_grad = call(
        functools.partial(finish_kernel, heads), shape((rows, hd), BF16), [], [], 2**32, dq
    )
    from_b, query_grad = lax.optimization_barrier((from_b, query_grad))
    halves, rests = [], []
    for i in range(2):
        if i:
            from_a[i], halves[0] = lax.optimization_barrier((from_a[i], halves[0]))
        half = own[i] + from_a[i].astype(F32) + from_b[i].astype(F32)
        halves.append(half.astype(BF16))
        rests.append(lax.ppermute(halves[i], "head", other))
    grads = []
    for i in range(2):
        grads.append((halves[i].astype(F32) + rests[i].astype(F32)).astype(BF16))
    key_grad, value_grad = grads
    return query_grad.reshape(tok, heads, hd), key_grad, value_grad


def solution(mesh):
    in_specs = (
        P("blk", "head", None),
        P("blk", "head", None),
        P("blk", "head", None),
        P("blk", None),
        P("blk", None),
        P("blk", "head"),
        P("blk"),
        P("blk"),
    )
    out_specs = (P("blk", "head", None), P("blk", None), P("blk", None))
    return jax.shard_map(
        on_device, mesh=mesh, in_specs=in_specs, out_specs=out_specs, check_vma=False
    )
```

time: 120 us -> 54.1 us (0.45)
  matrix products: 59.4 us -> 0 us
  blocking collectives: 20.6 us -> 0 us
  Pallas kernels: 0 us -> 13.6 us
  waiting for transfers between devices: 7.5 us -> 20.9 us
  starting transfers between devices: 26.8 us -> 17.2 us
  local copies, waits for them, and re-layouts: 2.48 us -> 0.01 us
    dot_general x20 -> x0, matrix products: 59.4 us -> none  [the longest x4 18.5 us: block_grads(): jnp.einsum('thd,kd->htk', out_grad, value_vectors, preferred_element_type...]
    psum x1 -> x0, blocking collectives: 20.6 us -> none  [on_device(): key_total, value_total = lax.psum((key_total, value_total), 'head')]
    pallas_call x0 -> x3, Pallas kernels: none -> 13.6 us  [call(): pl.pallas_call(body, out_shape=outs, in_specs=specs + [vmem] * (len(args)...]
    ppermute x17 -> x15, waiting for transfers between devices: 7.5 us -> 20.9 us  [the longest x3 8.99 us: on_device(): back = lambda x, pairs: lax.ppermute(x, 'blk', [(d, s) for s, d in pairs])]
    ppermute x17 -> x15, starting transfers between devices: 26.8 us -> 17.2 us  [the longest x9 10.6 us: on_device(): lax.ppermute(x, 'blk', pairs)]
    unnamed x37 -> x8, local copies, waits for them, and re-layouts: 2.39 us -> 0.01 us
  transfers between devices with their start and end apart: 17 -> 15, of which waited for: 6 -> 9; matrix products, arithmetic and copies ran while one was open for 52% -> 1% of each run, Pallas kernels for 0% -> 10%
where the time goes in v2:
time: 54.1 us; the launch traced here: 53.9 us
  waiting for transfers between devices  20.9 us (39%)
  starting transfers between devices  17.2 us (32%)
  Pallas kernels  13.6 us (25%)
  other arithmetic  1.53 us (3%)
  between operations  0.7 us (1%)
    pallas_call x3, Pallas kernels, call(): pl.pallas_call(body, out_shape=outs, in_specs=specs + [vmem] * (len(args)...  13.6 us
    ppermute x9, starting transfers between devices, on_device(): lax.ppermute(x, 'blk', pairs)  10.6 us
    ppermute x3, waiting for transfers between devices, on_device(): back = lambda x, pairs: lax.ppermute(x, 'blk', [(d, s) for s, d in pairs])  8.99 us
    ppermute x2, waiting for transfers between devices, on_device(): rests.append(lax.ppermute(halves[i], 'head', other))  6.12 us
    ppermute x9, waiting for transfers between devices, on_device(): lax.ppermute(x, 'blk', pairs)  4.77 us
    ppermute x3, starting transfers between devices, on_device(): back = lambda x, pairs: lax.ppermute(x, 'blk', [(d, s) for s, d in pairs])  4.15 us
    ppermute x2, starting transfers between devices, on_device(): rests.append(lax.ppermute(halves[i], 'head', other))  2.09 us
    convert_element_type x2, other arithmetic, on_device(): grads.append((halves[i].astype(F32) + rests[i].astype(F32)).astype(BF16))  1.38 us
  transfers between devices with their start and end apart: 15, of which 9 were waited for; matrix products, arithmetic and copies ran while one was open for 1% of the time, Pallas kernels for 10%

profile of v2, /device:TPU:0, one launch (start us, length us, event | category | flops | bytes accessed | tf_op | source)
XLA Modules:
  0.0 53.9 jit_solution(10212799947397868022)
XLA Ops:
  0.6 6.1 %collective-permute-start = (bf16[512,128]{1,0:T(8,128)(2,1)}, bf16[512,128]{1,0:T(8,128)(2,1)S(1)}, u32[]{:S(2)}, u32[]{:S(2)}) collective-permute-start(bf16[512,128]{1,0:T(8,128)(2,1)} %refs_0_.1), channel_id=1, source_target_pairs={{0,28},{2,30},{4,0},{6,2},{8,4},{10,6},{12,8},{14,10},{16,12},{18,... | collective-permute-start | bytes 393224 | tf_op jit(solution)/shard_map/ppermute | solution.py:174
  6.7 0.0 collective-permute-start.3
  6.7 0.5 collective-permute-start.1
  7.2 0.3 collective-permute-start.5
  7.5 1.4 %collective-permute-start.2 = (s32[512]{0:T(512)}, s32[512]{0:T(512)S(1)}, u32[]{:S(2)}, u32[]{:S(2)}) collective-permute-start(s32[512]{0:T(512)} %param.14), channel_id=1, source_target_pairs={{0,28},{2,30},{4,0},{6,2},{8,4},{10,6},{12,8},{14,10},{16,12},{18,... | collective-permute-start | bytes 6152 | tf_op jit(solution)/shard_map/ppermute | solution.py:174
  8.9 0.0 copy-start.3
  8.9 0.0 copy-start
  8.9 0.0 copy-start.1
  8.9 0.0 copy-start.2
  8.9 3.9 %shard_map.103 = (f32[32,4096]{1,0:T(8,128)S(1)}, bf16[4096,128]{1,0:T(8,128)(2,1)S(1)}, bf16[4096,128]{1,0:T(8,128)(2,1)S(1)}) custom-call(bf16[4096,128]{1,0:T(8,128)(2,1)} %bitcast.34, bf16[4096,128]{1,0:T(8,128)(2,1)} %bitcast.35, bf16[4096,128]{1,0:T(8,128)(2,1)} %bitcast.36, s32[1,512]{1,0:T(1,128)} %bitcast.29, s32[1,512]{1,0:T(1,128)} %bitcast.28, ...), custom_call_target="tpu_custom_call" | custom-call | flops 4294967296 | bytes 4194304 | tf_op jit(solution)/shard_map/pallas_call | solution.py:153
  12.8 2.6 %collective-permute-done.2 = s32[512]{0:T(512)S(1)} collective-permute-done((s32[512]{0:T(512)}, s32[512]{0:T(512)S(1)}, u32[]{:S(2)}, u32[]{:S(2)}) %collective-permute-start.2) | collective-permute-done | bytes 2080 | tf_op jit(solution)/shard_map/ppermute | solution.py:174
  15.4 0.0 collective-permute-done.refs_1_
  15.4 0.0 collective-permute-done.1.refs_5_
  15.4 0.0 collective-permute-start.4
  15.4 0.5 collective-permute-start.6
  15.9 0.0 copy-done.3
  16.0 0.1 collective-permute-start.7
  16.1 1.3 %collective-permute-done.7 = s32[512]{0:T(512)S(1)} collective-permute-done((s32[512]{0:T(512)S(1)}, s32[512]{0:T(512)S(1)}, u32[]{:S(2)}, u32[]{:S(2)}) %collective-permute-start.7) | collective-permute-done | bytes 2080 | tf_op jit(solution)/shard_map/ppermute | solution.py:174
  17.4 1.6 %collective-permute-start.8 = (s32[512]{0:T(512)S(1)}, s32[512]{0:T(512)S(1)}, u32[]{:S(2)}, u32[]{:S(2)}) collective-permute-start(s32[512]{0:T(512)S(1)} %collective-permute-done.2), channel_id=1, source_target_pairs={{0,2},{2,0},{4,6},{6,4},{8,10},{10,8},{12,14},{14,12},{16,18},{18,... | collective-permute-start | bytes 6152 | tf_op jit(solution)/shard_map/ppermute | solution.py:174
  19.0 0.0 collective-permute-done.3.refs_2_
  19.0 0.0 collective-permute-done.5.refs_6_
  19.0 0.8 %collective-permute-done.8 = s32[512]{0:T(512)S(1)} collective-permute-done((s32[512]{0:T(512)S(1)}, s32[512]{0:T(512)S(1)}, u32[]{:S(2)}, u32[]{:S(2)}) %collective-permute-start.8) | collective-permute-done | bytes 2080 | tf_op jit(solution)/shard_map/ppermute | solution.py:174
  19.9 0.0 collective-permute-done.4.refs_3_
  19.9 0.0 collective-permute-done.6.refs_7_
  19.9 0.0 copy-done
  19.9 0.0 copy-done.1
  19.9 0.0 copy-done.2
  19.9 8.4 %shard_map.104 = (f32[128,4096]{1,0:T(8,128)S(1)}, f32[2,512,128]{2,1,0:T(8,128)S(1)}, bf16[2,512,128]{2,1,0:T(8,128)(2,1)S(1)}, bf16[2,512,128]{2,1,0:T(8,128)(2,1)S(1)}, bf16[2,512,128]{2,1,0:T(8,128)(2,1)S(1)}) custom-call(s32[512]{0:T(512)S(1)} %copy-done.2, f32[32,4096]{1,0:T(8,128)S(1)} %get-tuple-element.20.vec_ref, ...), custom_call_target="tpu_custom_call" | custom-call | flops 34359738368 | bytes 4194304 | tf_op jit(solution)/shard_map/pallas_call | solution.py:153
  28.3 0.4 collective-permute-start.10
  28.7 0.2 collective-permute-start.9
  28.9 1.0 %collective-permute-done.10 = bf16[2,512,128]{2,1,0:T(8,128)(2,1)S(1)} collective-permute-done((bf16[2,512,128]{2,1,0:T(8,128)(2,1)S(1)}, bf16[2,512,128]{2,1,0:T(8,128)(2,1)S(1)}, u32[]{:S(2)}, u32[]{:S(2)}) %collective-permute-start.10) | collective-permute-done | bytes 262176 | tf_op jit(solution)/shard_map/ppermute | solution.py:214
  29.9 4.0 %collective-permute-start.12 = (bf16[512,128]{1,0:T(8,128)(2,1)S(1)}, bf16[512,128]{1,0:T(8,128)(2,1)S(1)}, u32[]{:S(2)}, u32[]{:S(2)}) collective-permute-start(bf16[512,128]{1,0:T(8,128)(2,1)S(1)} %get-tuple-element.36), channel_id=1, source_target_pairs={{28,0},{30,2},{0,4},{2,6},{4,8},{6,10},{8,12},{10,14},{12,16},{14,... | collective-permute-start | bytes 393224 | tf_op jit(solution)/shard_map/ppermute | solution.py:213
  33.9 1.3 %shard_map.105 = bf16[4096,128]{1,0:T(8,128)(2,1)} custom-call(f32[128,4096]{1,0:T(8,128)S(1)} %get-tuple-element.27.dq_ref), custom_call_target="tpu_custom_call" | custom-call | flops 4294967296 | bytes 4194304 | tf_op jit(solution)/shard_map/pallas_call | solution.py:153
  35.2 0.0 collective-permute-start.11
  35.2 1.1 %collective-permute-done.9 = bf16[2,512,128]{2,1,0:T(8,128)(2,1)S(1)} collective-permute-done((bf16[2,512,128]{2,1,0:T(8,128)(2,1)S(1)}, bf16[2,512,128]{2,1,0:T(8,128)(2,1)S(1)}, u32[]{:S(2)}, u32[]{:S(2)}) %collective-permute-start.9) | collective-permute-done | bytes 262176 | tf_op jit(solution)/shard_map/ppermute | solution.py:213
  36.3 4.9 %collective-permute-done.12 = bf16[512,128]{1,0:T(8,128)(2,1)S(1)} collective-permute-done((bf16[512,128]{1,0:T(8,128)(2,1)S(1)}, bf16[512,128]{1,0:T(8,128)(2,1)S(1)}, u32[]{:S(2)}, u32[]{:S(2)}) %collective-permute-start.12) | collective-permute-done | bytes 131104 | tf_op jit(solution)/shard_map/ppermute | solution.py:213
  41.2 0.1 fusion.1
  41.3 3.0 %collective-permute-done.11 = bf16[512,128]{1,0:T(8,128)(2,1)S(1)} collective-permute-done((bf16[512,128]{1,0:T(8,128)(2,1)S(1)}, bf16[512,128]{1,0:T(8,128)(2,1)S(1)}, u32[]{:S(2)}, u32[]{:S(2)}) %collective-permute-start.11) | collective-permute-done | bytes 131104 | tf_op jit(solution)/shard_map/ppermute | solution.py:213
  44.3 0.1 fusion
  44.3 1.6 %collective-permute-start.14 = (bf16[512,128]{1,0:T(8,128)(2,1)S(1)}, bf16[512,128]{1,0:T(8,128)(2,1)S(1)}, u32[]{:S(2)}, u32[]{:S(2)}) collective-permute-start(bf16[512,128]{1,0:T(8,128)(2,1)S(1)} %fusion), channel_id=1, source_target_pairs={{0,1},{1,0},{2,3},{3,2},{4,5},{5,4},{6,7},{7,6},{8,9},{9,8},{10,11... | collective-permute-start | bytes 393224 | tf_op jit(solution)/shard_map/ppermute | solution.py:227
  45.9 0.5 collective-permute-start.13
  46.4 4.3 %collective-permute-done.14 = bf16[512,128]{1,0:T(8,128)(2,1)S(1)} collective-permute-done((bf16[512,128]{1,0:T(8,128)(2,1)S(1)}, bf16[512,128]{1,0:T(8,128)(2,1)S(1)}, u32[]{:S(2)}, u32[]{:S(2)}) %collective-permute-start.14) | collective-permute-done | bytes 131104 | tf_op jit(solution)/shard_map/ppermute | solution.py:227
  50.8 0.7 %add_convert_fusion = bf16[512,128]{1,0:T(8,128)(2,1)} fusion(bf16[512,128]{1,0:T(8,128)(2,1)S(1)} %collective-permute-done.14, bf16[512,128]{1,0:T(8,128)(2,1)S(1)} %fusion), kind=kLoop, calls=%fused_computation.6 | loop fusion | flops 262144 | bytes 393216 | tf_op jit(solution)/shard_map/convert_element_type | solution.py:230
  51.5 1.8 %collective-permute-done.13 = bf16[512,128]{1,0:T(8,128)(2,1)S(1)} collective-permute-done((bf16[512,128]{1,0:T(8,128)(2,1)S(1)}, bf16[512,128]{1,0:T(8,128)(2,1)S(1)}, u32[]{:S(2)}, u32[]{:S(2)}) %collective-permute-start.13) | collective-permute-done | bytes 131104 | tf_op jit(solution)/shard_map/ppermute | solution.py:227
  53.2 0.7 %add_convert_fusion.1 = bf16[512,128]{1,0:T(8,128)(2,1)} fusion(bf16[512,128]{1,0:T(8,128)(2,1)S(1)} %collective-permute-done.13, bf16[512,128]{1,0:T(8,128)(2,1)S(1)} %fusion.1), kind=kLoop, calls=%fused_computation.7 | loop fusion | flops 262144 | bytes 393216 | tf_op jit(solution)/shard_map/convert_element_type | solution.py:230
  (1 shorter events, 0.0 us)
Async XLA Ops:
  0.6 14.8 %collective-permute-start = (bf16[512,128]{1,0:T(8,128)(2,1)}, bf16[512,128]{1,0:T(8,128)(2,1)S(1)}, u32[]{:S(2)}, u32[]{:S(2)}) collective-permute-start(bf16[512,128]{1,0:T(8,128)(2,1)} %refs_0_.1), channel_id=1, source_target_pairs={{0,28},{2,30},{4,0},{6,2},{8,4},{10,6},{12,8},{14,10},{16,12},{18,... | collective-permute-start | bytes 393224 | tf_op jit(solution)/shard_map/ppermute | solution.py:174
  6.7 12.3 %collective-permute-start.3 = (bf16[512,128]{1,0:T(8,128)(2,1)}, bf16[512,128]{1,0:T(8,128)(2,1)S(1)}, u32[]{:S(2)}, u32[]{:S(2)}) collective-permute-start(bf16[512,128]{1,0:T(8,128)(2,1)} %refs_0_.1), channel_id=1, source_target_pairs={{0,26},{2,0},{4,30},{6,4},{8,2},{10,8},{12,6},{14,12},{16,10},{18,... | collective-permute-start | bytes 393224 | tf_op jit(solution)/shard_map/ppermute | solution.py:174
  6.7 8.7 %collective-permute-start.1 = (bf16[512,128]{1,0:T(8,128)(2,1)}, bf16[512,128]{1,0:T(8,128)(2,1)S(1)}, u32[]{:S(2)}, u32[]{:S(2)}) collective-permute-start(bf16[512,128]{1,0:T(8,128)(2,1)} %refs_4_.1), channel_id=1, source_target_pairs={{0,28},{2,30},{4,0},{6,2},{8,4},{10,6},{12,8},{14,10},{16,12},{18,... | collective-permute-start | bytes 393224 | tf_op jit(solution)/shard_map/ppermute | solution.py:174
  7.2 11.8 %collective-permute-start.5 = (bf16[512,128]{1,0:T(8,128)(2,1)}, bf16[512,128]{1,0:T(8,128)(2,1)S(1)}, u32[]{:S(2)}, u32[]{:S(2)}) collective-permute-start(bf16[512,128]{1,0:T(8,128)(2,1)} %refs_4_.1), channel_id=1, source_target_pairs={{0,26},{2,0},{4,30},{6,4},{8,2},{10,8},{12,6},{14,12},{16,10},{18,... | collective-permute-start | bytes 393224 | tf_op jit(solution)/shard_map/ppermute | solution.py:174
  7.5 7.9 %collective-permute-start.2 = (s32[512]{0:T(512)}, s32[512]{0:T(512)S(1)}, u32[]{:S(2)}, u32[]{:S(2)}) collective-permute-start(s32[512]{0:T(512)} %param.14), channel_id=1, source_target_pairs={{0,28},{2,30},{4,0},{6,2},{8,4},{10,6},{12,8},{14,10},{16,12},{18,... | collective-permute-start | bytes 6152 | tf_op jit(solution)/shard_map/ppermute | solution.py:174
  8.9 7.0 %copy-start.3 = (s32[512]{0:T(512)S(1)}, s32[512]{0:T(512)}, u32[]{:S(2)}) copy-start(s32[512]{0:T(512)} %param.14) | copy-start | bytes 6148
  8.9 10.9 %copy-start = (bf16[512,128]{1,0:T(8,128)(2,1)S(1)}, bf16[512,128]{1,0:T(8,128)(2,1)}, u32[]{:S(2)}) copy-start(bf16[512,128]{1,0:T(8,128)(2,1)} %refs_0_.1) | copy-start | bytes 393220
  8.9 10.9 %copy-start.1 = (bf16[512,128]{1,0:T(8,128)(2,1)S(1)}, bf16[512,128]{1,0:T(8,128)(2,1)}, u32[]{:S(2)}) copy-start(bf16[512,128]{1,0:T(8,128)(2,1)} %refs_4_.1) | copy-start | bytes 393220
  8.9 11.0 %copy-start.2 = (s32[512]{0:T(512)S(1)}, s32[512]{0:T(512)}, u32[]{:S(2)}) copy-start(s32[512]{0:T(512)} %starts_ref.1) | copy-start | bytes 6148
  15.4 4.4 %collective-permute-start.4 = (bf16[512,128]{1,0:T(8,128)(2,1)S(1)}, bf16[512,128]{1,0:T(8,128)(2,1)S(1)}, u32[]{:S(2)}, u32[]{:S(2)}) collective-permute-start(bf16[512,128]{1,0:T(8,128)(2,1)S(1)} %collective-permute-done.refs_1_), channel_id=1, source_target_pairs={{0,2},{2,0},{4,6},{6,4},{8,10},{10,8},{12,14},{14,12},{16,18},{18,... | collective-permute-start | bytes 393224 | tf_op jit(solution)/shard_map/ppermute | solution.py:174
  15.4 4.4 %collective-permute-start.6 = (bf16[512,128]{1,0:T(8,128)(2,1)S(1)}, bf16[512,128]{1,0:T(8,128)(2,1)S(1)}, u32[]{:S(2)}, u32[]{:S(2)}) collective-permute-start(bf16[512,128]{1,0:T(8,128)(2,1)S(1)} %collective-permute-done.1.refs_5_), channel_id=1, source_target_pairs={{0,2},{2,0},{4,6},{6,4},{8,10},{10,8},{12,14},{14,12},{16,18},{18,... | collective-permute-start | bytes 393224 | tf_op jit(solution)/shard_map/ppermute | solution.py:174
  16.0 1.4 %collective-permute-start.7 = (s32[512]{0:T(512)S(1)}, s32[512]{0:T(512)S(1)}, u32[]{:S(2)}, u32[]{:S(2)}) collective-permute-start(s32[512]{0:T(512)S(1)} %copy-done.3), channel_id=1, source_target_pairs={{0,26},{2,0},{4,30},{6,4},{8,2},{10,8},{12,6},{14,12},{16,10},{18,... | collective-permute-start | bytes 6152 | tf_op jit(solution)/shard_map/ppermute | solution.py:174
  17.4 2.5 %collective-permute-start.8 = (s32[512]{0:T(512)S(1)}, s32[512]{0:T(512)S(1)}, u32[]{:S(2)}, u32[]{:S(2)}) collective-permute-start(s32[512]{0:T(512)S(1)} %collective-permute-done.2), channel_id=1, source_target_pairs={{0,2},{2,0},{4,6},{6,4},{8,10},{10,8},{12,14},{14,12},{16,18},{18,... | collective-permute-start | bytes 6152 | tf_op jit(solution)/shard_map/ppermute | solution.py:174
  28.3 1.6 %collective-permute-start.10 = (bf16[2,512,128]{2,1,0:T(8,128)(2,1)S(1)}, bf16[2,512,128]{2,1,0:T(8,128)(2,1)S(1)}, u32[]{:S(2)}, u32[]{:S(2)}) collective-permute-start(bf16[2,512,128]{2,1,0:T(8,128)(2,1)S(1)} %get-tuple-element.30), channel_id=1, source_target_pairs={{0,2},{2,0},{4,6},{6,4},{8,10},{10,8},{12,14},{14,12},{16,18},{18,... | collective-permute-start | bytes 786440 | tf_op jit(solution)/shard_map/ppermute | solution.py:214
  28.7 7.6 %collective-permute-start.9 = (bf16[2,512,128]{2,1,0:T(8,128)(2,1)S(1)}, bf16[2,512,128]{2,1,0:T(8,128)(2,1)S(1)}, u32[]{:S(2)}, u32[]{:S(2)}) collective-permute-start(bf16[2,512,128]{2,1,0:T(8,128)(2,1)S(1)} %get-tuple-element.26), channel_id=1, source_target_pairs={{26,0},{0,2},{30,4},{4,6},{2,8},{8,10},{6,12},{12,14},{10,16},{16,... | collective-permute-start | bytes 786440 | tf_op jit(solution)/shard_map/ppermute | solution.py:213
  29.9 11.3 %collective-permute-start.12 = (bf16[512,128]{1,0:T(8,128)(2,1)S(1)}, bf16[512,128]{1,0:T(8,128)(2,1)S(1)}, u32[]{:S(2)}, u32[]{:S(2)}) collective-permute-start(bf16[512,128]{1,0:T(8,128)(2,1)S(1)} %get-tuple-element.36), channel_id=1, source_target_pairs={{28,0},{30,2},{0,4},{2,6},{4,8},{6,10},{8,12},{10,14},{12,16},{14,... | collective-permute-start | bytes 393224 | tf_op jit(solution)/shard_map/ppermute | solution.py:213
  35.2 9.1 %collective-permute-start.11 = (bf16[512,128]{1,0:T(8,128)(2,1)S(1)}, bf16[512,128]{1,0:T(8,128)(2,1)S(1)}, u32[]{:S(2)}, u32[]{:S(2)}) collective-permute-start(bf16[512,128]{1,0:T(8,128)(2,1)S(1)} %get-tuple-element.35), channel_id=1, source_target_pairs={{28,0},{30,2},{0,4},{2,6},{4,8},{6,10},{8,12},{10,14},{12,16},{14,... | collective-permute-start | bytes 393224 | tf_op jit(solution)/shard_map/ppermute | solution.py:213
  44.3 6.4 %collective-permute-start.14 = (bf16[512,128]{1,0:T(8,128)(2,1)S(1)}, bf16[512,128]{1,0:T(8,128)(2,1)S(1)}, u32[]{:S(2)}, u32[]{:S(2)}) collective-permute-start(bf16[512,128]{1,0:T(8,128)(2,1)S(1)} %fusion), channel_id=1, source_target_pairs={{0,1},{1,0},{2,3},{3,2},{4,5},{5,4},{6,7},{7,6},{8,9},{9,8},{10,11... | collective-permute-start | bytes 393224 | tf_op jit(solution)/shard_map/ppermute | solution.py:227
  45.9 7.4 %collective-permute-start.13 = (bf16[512,128]{1,0:T(8,128)(2,1)S(1)}, bf16[512,128]{1,0:T(8,128)(2,1)S(1)}, u32[]{:S(2)}, u32[]{:S(2)}) collective-permute-start(bf16[512,128]{1,0:T(8,128)(2,1)S(1)} %fusion.1), channel_id=1, source_target_pairs={{0,1},{1,0},{2,3},{3,2},{4,5},{5,4},{6,7},{7,6},{8,9},{9,8},{10,11... | collective-permute-start | bytes 393224 | tf_op jit(solution)/shard_map/ppermute | solution.py:227

commit v3 on v2

--- a/solution.py
+++ b/solution.py
@@ -80,9 +80,11 @@
         copy.wait()
 
 
-def grads_kernel(nb, n_blk, starts_ref, vec_ref, q_ref, g_ref, *refs):
+def grads_kernel(nb, n_blk, first, starts_ref, vec_ref, q_ref, g_ref, *refs):
     ks, vs, places, refs = refs[:nb], refs[nb : 2 * nb], refs[2 * nb : 3 * nb], refs[3 * nb :]
-    dq_ref, own_ref, c_ref, a_ref, b_ref, dk_acc, dv_acc = refs
+    if not first:
+        dq_in, *refs = refs
+    dq_ref, *outs, dk_acc, dv_acc = refs
     hd = q_ref.shape[1]
     tok = ks[0].shape[0]
     heads = q_ref.shape[0] // tok
@@ -106,9 +108,9 @@
         row_place = (row * n_blk).astype(F32)
         oks = []
         for p in places:
-            first = p[0:1, 0:1].astype(F32)
-            ok = row_place >= begin - first
-            oks.append(ok & (row_place <= place - first if top is None else row < top))
+            first_place = p[0:1, 0:1].astype(F32)
+            ok = row_place >= begin - first_place
+            oks.append(ok & (row_place <= place - first_place if top is None else row < top))
         ok = jnp.concatenate(oks, axis=0)
         attend = jnp.where(ok, jnp.exp2(s * (scale * LOG2E) - lse), 0.0)
         low = (attend * (dp - delta)).astype(BF16)
@@ -120,7 +122,9 @@
         return dot(kw, low, TN)
 
     for i in range(tiles):
-        dq_ref[:, columns(i, cols)] = window(i, max((i + 1) * TILE - WIN, 0), None)
+        rows = columns(i, cols)
+        dq = window(i, max((i + 1) * TILE - WIN, 0), None)
+        dq_ref[:, rows] = dq if first else dq_in[:, rows] + dq
     for i in range(tiles):
         top = (i + 1) * TILE - WIN
         if top <= 0:
@@ -129,13 +133,13 @@
 
         def more(w, carry, i=i, top=top):
             edge = top - w * WIN
-            at = pl.multiple_of(jnp.maximum(edge - WIN, 0), TILE)
+            at = pl.multiple_of(jnp.maximum(edge - WIN, 0), math.gcd(TILE, WIN))
             dq_ref[:, columns(i, cols)] += window(i, at, edge)
             return carry
 
         lax.fori_loop(0, far, more, 0)
 
-    for b, out in enumerate((own_ref, a_ref, b_ref, c_ref)):
+    for b, out in enumerate(outs):
         out[0] = (dk_acc[b] * scale).astype(out.dtype)
         out[1] = dv_acc[b].astype(out.dtype)
 
@@ -148,7 +152,7 @@
         out_ref[at, :] = (dq_ref[:, at] * hd**-0.5).T.astype(BF16)
 
 
-def call(body, outs, specs, scratch, flops, *args):
+def call(body, outs, specs, scratch, flops, *args, **more):
     vmem = pl.BlockSpec(memory_space=pltpu.VMEM)
     return pl.pallas_call(
         body,
@@ -158,7 +162,32 @@
         scratch_shapes=scratch,
         compiler_params=pltpu.CompilerParams(vmem_limit_bytes=32 * 2**20),
         cost_estimate=pl.CostEstimate(flops=flops, bytes_accessed=4 * 2**20, transcendentals=0),
+        **more,
     )(*args)
+
+
+def grads(n, types, flops, doc_start, vec, q, g, groups, dq=None):
+    nb = len(groups)
+    rows, hd = q.shape
+    tok = groups[0][0].shape[0]
+    shape = jax.ShapeDtypeStruct
+    last = [] if dq is None else [dq]
+    return call(
+        functools.partial(grads_kernel, nb, n, dq is None),
+        [shape((hd, rows), F32)] + [shape((2, tok, hd), t) for t in types],
+        [pl.BlockSpec(memory_space=pltpu.SMEM)],
+        [pltpu.VMEM((nb, tok, hd), F32)] * 2,
+        flops,
+        doc_start, vec, q, g, *(x[i].reshape(-1, x[i].shape[-1]) for i in range(3) for x in groups), *last,
+        input_output_aliases={} if dq is None else {4 + 3 * nb: 0},
+    )
+
+
+def send(group, pairs):
+    got = []
+    for x in group:
+        got.append(lax.ppermute(x, "blk", pairs))
+    return tuple(got)
 
 
 def on_device(queries, out_grad, outputs, keys, values, logsumexp, positions, doc_start):
@@ -171,10 +200,9 @@
     two_back = [(s, (s - 2) % n) for s in blocks]
     odd_even = [(s, (s - 1) % n if s % 2 else (s - 3) % n) for s in blocks]
     cores = [(s, s ^ 1) for s in blocks]
-    move = lambda group, pairs: tuple(lax.ppermute(x, "blk", pairs) for x in group)
     mine = (keys, values, positions)
-    a = move(mine, two_back)
-    b = move(mine, odd_even)
+    a = send(mine, two_back)
+    b = send(mine, odd_even)
 
     q, g, o = (x.reshape(rows, hd) for x in (queries, out_grad, outputs))
     line = lambda x: x.reshape(1, tok)
@@ -197,27 +225,21 @@
         ),
     )
     a, vec = lax.optimization_barrier((a, vec))
-    c = move(a, cores)
-    part = shape((2, tok, hd), BF16)
-    groups = (mine, a, b, c)
-    dq, own, c_part, a_part, b_part = call(
-        functools.partial(grads_kernel, 4, n),
-        [shape((hd, rows), F32), shape((2, tok, hd), F32), part, part, part],
-        [pl.BlockSpec(memory_space=pltpu.SMEM)],
-        [pltpu.VMEM((4, tok, hd), F32)] * 2,
-        2**35,
-        doc_start, vec, q, g, *(x[0] for x in groups), *(x[1] for x in groups), *(line(x[2]) for x in groups),
-    )
+    c = send(a, cores)
+    dq, a_part = grads(n, [BF16], 2**33, doc_start, vec, q, g, [a])
+    dq, b_part, c_part = grads(n, [BF16, BF16], 2**34, doc_start, vec, q, g, [b, c], dq)
 
     other = [(0, 1), (1, 0)]
-    back = lambda x, pairs: lax.ppermute(x, "blk", [(d, s) for s, d in pairs])
-    near = lax.ppermute(c_part, "blk", cores)
-    from_b = back(b_part, odd_even)
-    from_a = [back(a_part[i] + near[i], two_back) for i in range(2)]
+    near = lax.ppermute(a_part, "blk", cores)
+    b_part, c_part = lax.optimization_barrier((b_part, c_part))
+    from_b = lax.ppermute(b_part, "blk", [(d, s) for s, d in odd_even])
+    home = [(d, (d + 1) % n if d % 2 else (d + 3) % n) for d in blocks]
+    from_a = list(send([c_part[i] + near[i] for i in range(2)], home))
+    dq, own = grads(n, [F32], 2**33, doc_start, vec, q, g, [mine], dq)
     query_grad = call(
         functools.partial(finish_kernel, heads), shape((rows, hd), BF16), [], [], 2**32, dq
     )
-    from_b, query_grad = lax.optimization_barrier((from_b, query_grad))
+    from_b, query_grad, own = lax.optimization_barrier((from_b, query_grad, own))
     halves, rests = [], []
     for i in range(2):
         if i:
@@ -225,10 +247,10 @@
         half = own[i] + from_a[i].astype(F32) + from_b[i].astype(F32)
         halves.append(half.astype(BF16))
         rests.append(lax.ppermute(halves[i], "head", other))
-    grads = []
+    sums = []
     for i in range(2):
-        grads.append((halves[i].astype(F32) + rests[i].astype(F32)).astype(BF16))
-    key_grad, value_grad = grads
+        sums.append((halves[i].astype(F32) + rests[i].astype(F32)).astype(BF16))
+    key_grad, value_grad = sums
     return query_grad.reshape(tok, heads, hd), key_grad, value_grad
 
 

time: 54.1 us -> 51.8 us (0.957)
  Pallas kernels: 13.6 us -> 18.4 us
  starting transfers between devices: 17.2 us -> 13.1 us
  waiting for transfers between devices: 20.9 us -> 17.9 us
    pallas_call x3 -> x5, Pallas kernels: 13.6 us -> 18.4 us  [call(): pl.pallas_call(body, out_shape=outs, in_specs=specs + [vmem] * (len(args)...]
    ppermute x13, starting transfers between devices: 15.1 us -> 11 us  [the longest x11 10.3 us: send(): got.append(lax.ppermute(x, 'blk', pairs))]
    ppermute x2, waiting for transfers between devices: 6.12 us -> 3.75 us  [on_device(): rests.append(lax.ppermute(halves[i], 'head', other))]
    ppermute x13, waiting for transfers between devices: 14.8 us -> 14.1 us  [the longest x11 9.37 us: send(): got.append(lax.ppermute(x, 'blk', pairs))]
  transfers between devices with their start and end apart: 15 -> 15, of which waited for: 9 -> 7; matrix products, arithmetic and copies ran while one was open for 1% -> 2% of each run, Pallas kernels for 10% -> 36%
where the time goes in v3:
time: 51.8 us; the launch traced here: 51.6 us
  Pallas kernels  18.4 us (36%)
  waiting for transfers between devices  17.9 us (35%)
  starting transfers between devices  13.1 us (25%)
  other arithmetic  1.53 us (3%)
  between operations  0.77 us (1%)
    pallas_call x5, Pallas kernels, call(): pl.pallas_call(body, out_shape=outs, in_specs=specs + [vmem] * (len(args)...  18.4 us
    ppermute x11, starting transfers between devices, send(): got.append(lax.ppermute(x, 'blk', pairs))  10.3 us
    ppermute x11, waiting for transfers between devices, send(): got.append(lax.ppermute(x, 'blk', pairs))  9.37 us
    ppermute x1, waiting for transfers between devices, on_device(): from_b = lax.ppermute(b_part, 'blk', [(d, s) for s, d in odd_even])  4.73 us
    ppermute x2, waiting for transfers between devices, on_device(): rests.append(lax.ppermute(halves[i], 'head', other))  3.75 us
    ppermute x2, starting transfers between devices, on_device(): rests.append(lax.ppermute(halves[i], 'head', other))  2.09 us
    convert_element_type x2, other arithmetic, on_device(): sums.append((halves[i].astype(F32) + rests[i].astype(F32)).astype(BF16))  1.38 us
  transfers between devices with their start and end apart: 15, of which 7 were waited for; matrix products, arithmetic and copies ran while one was open for 2% of the time, Pallas kernels for 36%

profile of v3, /device:TPU:0, one launch (start us, length us, event | category | flops | bytes accessed | tf_op | source)
XLA Modules:
  0.0 51.6 jit_solution(16335058360857247732)
XLA Ops:
  0.6 6.1 %collective-permute-start.2 = (s32[512]{0:T(512)}, s32[512]{0:T(512)S(1)}, u32[]{:S(2)}, u32[]{:S(2)}) collective-permute-start(s32[512]{0:T(512)} %param.14), channel_id=1, source_target_pairs={{0,28},{2,30},{4,0},{6,2},{8,4},{10,6},{12,8},{14,10},{16,12},{18,... | collective-permute-start | bytes 6152 | tf_op jit(solution)/shard_map/ppermute | solution.py:189
  6.7 0.0 collective-permute-start.7
  6.7 0.5 collective-permute-start
  7.2 0.3 collective-permute-start.3
  7.5 1.4 %collective-permute-start.1 = (bf16[512,128]{1,0:T(8,128)(2,1)}, bf16[512,128]{1,0:T(8,128)(2,1)S(1)}, u32[]{:S(2)}, u32[]{:S(2)}) collective-permute-start(bf16[512,128]{1,0:T(8,128)(2,1)} %refs_1_.1), channel_id=1, source_target_pairs={{0,28},{2,30},{4,0},{6,2},{8,4},{10,6},{12,8},{14,10},{16,12},{18,... | collective-permute-start | bytes 393224 | tf_op jit(solution)/shard_map/ppermute | solution.py:189
  8.9 0.0 copy-start.1
  8.9 0.0 copy-start.2
  8.9 3.9 %shard_map.103 = (f32[32,4096]{1,0:T(8,128)S(1)}, bf16[4096,128]{1,0:T(8,128)(2,1)S(1)}, bf16[4096,128]{1,0:T(8,128)(2,1)S(1)}) custom-call(bf16[4096,128]{1,0:T(8,128)(2,1)} %bitcast.34, bf16[4096,128]{1,0:T(8,128)(2,1)} %bitcast.35, bf16[4096,128]{1,0:T(8,128)(2,1)} %bitcast.36, s32[1,512]{1,0:T(1,128)} %bitcast.29, s32[1,512]{1,0:T(1,128)} %bitcast.28, ...), custom_call_target="tpu_custom_call" | custom-call | flops 4294967296 | bytes 4194304 | tf_op jit(solution)/shard_map/pallas_call | solution.py:157
  12.8 0.0 collective-permute-done.2
  12.8 0.0 copy-done.1
  12.8 0.1 collective-permute-start.5
  12.9 0.4 collective-permute-done.refs_0_
  13.3 2.3 %collective-permute-done.1.refs_1_ = bf16[512,128]{1,0:T(8,128)(2,1)S(1)} collective-permute-done((bf16[512,128]{1,0:T(8,128)(2,1)}, bf16[512,128]{1,0:T(8,128)(2,1)S(1)}, u32[]{:S(2)}, u32[]{:S(2)}) %collective-permute-start.1) | collective-permute-done | bytes 131104 | tf_op jit(solution)/shard_map/ppermute | solution.py:189
  15.7 0.0 collective-permute-start.8
  15.7 0.5 collective-permute-start.4
  16.2 0.0 collective-permute-done.7
  16.2 0.0 collective-permute-start.6
  16.2 0.0 copy-done.2
  16.2 3.8 %shard_map.104 = (f32[128,4096]{1,0:T(8,128)S(1)}, bf16[2,512,128]{2,1,0:T(8,128)(2,1)S(1)}) custom-call(s32[512]{0:T(512)S(1)} %copy-done.2, f32[32,4096]{1,0:T(8,128)S(1)} %get-tuple-element.25.vec_ref, bf16[4096,128]{1,0:T(8,128)(2,1)S(1)} %get-tuple-element.26.q_ref, bf16[4096,128]{1,0:T(8,128)(2,1)S(1)} %get-tuple-element.27.g_ref, ...), custom_call_target="tpu_custom_call" | custom-call | flops 8589934592 | bytes 4194304 | tf_op jit(solution)/shard_map/pallas_call | solution.py:157
  20.0 0.0 collective-permute-done.3.refs_0_
  20.0 0.6 %collective-permute-start.10 = (bf16[2,512,128]{2,1,0:T(8,128)(2,1)S(1)}, bf16[2,512,128]{2,1,0:T(8,128)(2,1)S(1)}, u32[]{:S(2)}, u32[]{:S(2)}) collective-permute-start(bf16[2,512,128]{2,1,0:T(8,128)(2,1)S(1)} %get-tuple-element.40), channel_id=1, source_target_pairs={{0,2},{2,0},{4,6},{6,4},{8,10},{10,8},{12,14},{14,12},{16,18},{18,... | collective-permute-start | bytes 786440 | tf_op jit(solution)/shard_map/ppermute | solution.py:233
  20.6 0.0 collective-permute-done.5.refs_2_
  20.6 0.0 collective-permute-done.8
  20.6 0.0 collective-permute-done.4.refs_1_
  20.6 0.0 collective-permute-done.6.refs_3_
  20.6 0.0 copy-start
  20.6 0.0 copy-start.3
  20.6 5.4 %shard_map.105 = (f32[128,4096]{1,0:T(8,128)S(1)}, bf16[2,512,128]{2,1,0:T(8,128)(2,1)S(1)}, bf16[2,512,128]{2,1,0:T(8,128)(2,1)S(1)}) custom-call(s32[512]{0:T(512)S(1)} %copy-done.2, f32[32,4096]{1,0:T(8,128)S(1)} %get-tuple-element.25.vec_ref, bf16[4096,128]{1,0:T(8,128)(2,1)S(1)} %get-tuple-element.26.q_ref, ...), custom_call_target="tpu_custom_call", output_to_operand_aliasing={{0}: (10, {})} | custom-call | flops 17179869184 | bytes 4194304 | tf_op jit(solution)/shard_map/pallas_call | solution.py:157
  26.0 0.0 copy-done
  26.1 0.0 copy-done.3
  26.1 4.0 %shard_map.106 = (f32[128,4096]{1,0:T(8,128)S(1)}, f32[2,512,128]{2,1,0:T(8,128)S(1)}) custom-call(s32[512]{0:T(512)S(1)} %copy-done.2, f32[32,4096]{1,0:T(8,128)S(1)} %get-tuple-element.25.vec_ref, bf16[4096,128]{1,0:T(8,128)(2,1)S(1)} %get-tuple-element.26.q_ref, bf16[4096,128]{1,0:T(8,128)(2,1)S(1)} %get-tuple-element.27.g_ref, ...), custom_call_target="tpu_custom_call", output_to_operand_aliasing={{0}: (7, {})} | custom-call | flops 8589934592 | bytes 4194304 | tf_op jit(solution)/shard_map/pallas_call | solution.py:157
  30.1 0.1 collective-permute-start.9
  30.1 0.0 collective-permute-done.10
  30.2 1.3 %collective-permute-start.12 = (bf16[512,128]{1,0:T(8,128)(2,1)S(1)}, bf16[512,128]{1,0:T(8,128)(2,1)S(1)}, u32[]{:S(2)}, u32[]{:S(2)}) collective-permute-start(bf16[512,128]{1,0:T(8,128)(2,1)S(1)} %get-tuple-element.46), channel_id=1, source_target_pairs={{0,6},{2,4},{4,10},{6,8},{8,14},{10,12},{12,18},{14,16},{16,22},{1... | collective-permute-start | bytes 393224 | tf_op jit(solution)/shard_map/ppermute | solution.py:189
  31.4 1.3 %shard_map.107 = bf16[4096,128]{1,0:T(8,128)(2,1)} custom-call(f32[128,4096]{1,0:T(8,128)S(1)} %get-tuple-element.36.dq_ref), custom_call_target="tpu_custom_call" | custom-call | flops 4294967296 | bytes 4194304 | tf_op jit(solution)/shard_map/pallas_call | solution.py:157
  32.8 0.2 collective-permute-start.11
  33.0 4.7 %collective-permute-done.9 = bf16[2,512,128]{2,1,0:T(8,128)(2,1)S(1)} collective-permute-done((bf16[2,512,128]{2,1,0:T(8,128)(2,1)S(1)}, bf16[2,512,128]{2,1,0:T(8,128)(2,1)S(1)}, u32[]{:S(2)}, u32[]{:S(2)}) %collective-permute-start.9) | collective-permute-done | bytes 262176 | tf_op jit(solution)/shard_map/ppermute | solution.py:235
  37.7 5.2 %collective-permute-done.12 = bf16[512,128]{1,0:T(8,128)(2,1)S(1)} collective-permute-done((bf16[512,128]{1,0:T(8,128)(2,1)S(1)}, bf16[512,128]{1,0:T(8,128)(2,1)S(1)}, u32[]{:S(2)}, u32[]{:S(2)}) %collective-permute-start.12) | collective-permute-done | bytes 131104 | tf_op jit(solution)/shard_map/ppermute | solution.py:189
  42.9 0.1 fusion.1
  43.0 1.3 %collective-permute-done.11 = bf16[512,128]{1,0:T(8,128)(2,1)S(1)} collective-permute-done((bf16[512,128]{1,0:T(8,128)(2,1)S(1)}, bf16[512,128]{1,0:T(8,128)(2,1)S(1)}, u32[]{:S(2)}, u32[]{:S(2)}) %collective-permute-start.11) | collective-permute-done | bytes 131104 | tf_op jit(solution)/shard_map/ppermute | solution.py:189
  44.3 0.1 fusion
  44.4 1.6 %collective-permute-start.14 = (bf16[512,128]{1,0:T(8,128)(2,1)S(1)}, bf16[512,128]{1,0:T(8,128)(2,1)S(1)}, u32[]{:S(2)}, u32[]{:S(2)}) collective-permute-start(bf16[512,128]{1,0:T(8,128)(2,1)S(1)} %fusion), channel_id=1, source_target_pairs={{0,1},{1,0},{2,3},{3,2},{4,5},{5,4},{6,7},{7,6},{8,9},{9,8},{10,11... | collective-permute-start | bytes 393224 | tf_op jit(solution)/shard_map/ppermute | solution.py:249
  46.0 0.5 %collective-permute-start.13 = (bf16[512,128]{1,0:T(8,128)(2,1)S(1)}, bf16[512,128]{1,0:T(8,128)(2,1)S(1)}, u32[]{:S(2)}, u32[]{:S(2)}) collective-permute-start(bf16[512,128]{1,0:T(8,128)(2,1)S(1)} %fusion.1), channel_id=1, source_target_pairs={{0,1},{1,0},{2,3},{3,2},{4,5},{5,4},{6,7},{7,6},{8,9},{9,8},{10,11... | collective-permute-start | bytes 393224 | tf_op jit(solution)/shard_map/ppermute | solution.py:249
  46.5 2.9 %collective-permute-done.14 = bf16[512,128]{1,0:T(8,128)(2,1)S(1)} collective-permute-done((bf16[512,128]{1,0:T(8,128)(2,1)S(1)}, bf16[512,128]{1,0:T(8,128)(2,1)S(1)}, u32[]{:S(2)}, u32[]{:S(2)}) %collective-permute-start.14) | collective-permute-done | bytes 131104 | tf_op jit(solution)/shard_map/ppermute | solution.py:249
  49.4 0.7 %add_convert_fusion = bf16[512,128]{1,0:T(8,128)(2,1)} fusion(bf16[512,128]{1,0:T(8,128)(2,1)S(1)} %collective-permute-done.14, bf16[512,128]{1,0:T(8,128)(2,1)S(1)} %fusion), kind=kLoop, calls=%fused_computation.6 | loop fusion | flops 262144 | bytes 393216 | tf_op jit(solution)/shard_map/convert_element_type | solution.py:252
  50.1 0.8 %collective-permute-done.13 = bf16[512,128]{1,0:T(8,128)(2,1)S(1)} collective-permute-done((bf16[512,128]{1,0:T(8,128)(2,1)S(1)}, bf16[512,128]{1,0:T(8,128)(2,1)S(1)}, u32[]{:S(2)}, u32[]{:S(2)}) %collective-permute-start.13) | collective-permute-done | bytes 131104 | tf_op jit(solution)/shard_map/ppermute | solution.py:249
  50.9 0.7 %add_convert_fusion.1 = bf16[512,128]{1,0:T(8,128)(2,1)} fusion(bf16[512,128]{1,0:T(8,128)(2,1)S(1)} %collective-permute-done.13, bf16[512,128]{1,0:T(8,128)(2,1)S(1)} %fusion.1), kind=kLoop, calls=%fused_computation.7 | loop fusion | flops 262144 | bytes 393216 | tf_op jit(solution)/shard_map/convert_element_type | solution.py:252
  (1 shorter events, 0.0 us)
Async XLA Ops:
  0.6 12.2 %collective-permute-start.2 = (s32[512]{0:T(512)}, s32[512]{0:T(512)S(1)}, u32[]{:S(2)}, u32[]{:S(2)}) collective-permute-start(s32[512]{0:T(512)} %param.14), channel_id=1, source_target_pairs={{0,28},{2,30},{4,0},{6,2},{8,4},{10,6},{12,8},{14,10},{16,12},{18,... | collective-permute-start | bytes 6152 | tf_op jit(solution)/shard_map/ppermute | solution.py:189
  6.7 9.4 %collective-permute-start.7 = (s32[512]{0:T(512)}, s32[512]{0:T(512)S(1)}, u32[]{:S(2)}, u32[]{:S(2)}) collective-permute-start(s32[512]{0:T(512)} %param.14), channel_id=1, source_target_pairs={{0,26},{2,0},{4,30},{6,4},{8,2},{10,8},{12,6},{14,12},{16,10},{18,... | collective-permute-start | bytes 6152 | tf_op jit(solution)/shard_map/ppermute | solution.py:189
  6.7 6.6 %collective-permute-start = (bf16[512,128]{1,0:T(8,128)(2,1)}, bf16[512,128]{1,0:T(8,128)(2,1)S(1)}, u32[]{:S(2)}, u32[]{:S(2)}) collective-permute-start(bf16[512,128]{1,0:T(8,128)(2,1)} %refs_0_.1), channel_id=1, source_target_pairs={{0,28},{2,30},{4,0},{6,2},{8,4},{10,6},{12,8},{14,10},{16,12},{18,... | collective-permute-start | bytes 393224 | tf_op jit(solution)/shard_map/ppermute | solution.py:189
  7.2 12.8 %collective-permute-start.3 = (bf16[512,128]{1,0:T(8,128)(2,1)}, bf16[512,128]{1,0:T(8,128)(2,1)S(1)}, u32[]{:S(2)}, u32[]{:S(2)}) collective-permute-start(bf16[512,128]{1,0:T(8,128)(2,1)} %refs_0_.1), channel_id=1, source_target_pairs={{0,26},{2,0},{4,30},{6,4},{8,2},{10,8},{12,6},{14,12},{16,10},{18,... | collective-permute-start | bytes 393224 | tf_op jit(solution)/shard_map/ppermute | solution.py:189
  7.5 8.1 %collective-permute-start.1 = (bf16[512,128]{1,0:T(8,128)(2,1)}, bf16[512,128]{1,0:T(8,128)(2,1)S(1)}, u32[]{:S(2)}, u32[]{:S(2)}) collective-permute-start(bf16[512,128]{1,0:T(8,128)(2,1)} %refs_1_.1), channel_id=1, source_target_pairs={{0,28},{2,30},{4,0},{6,2},{8,4},{10,6},{12,8},{14,10},{16,12},{18,... | collective-permute-start | bytes 393224 | tf_op jit(solution)/shard_map/ppermute | solution.py:189
  8.9 3.9 %copy-start.1 = (bf16[512,128]{1,0:T(8,128)(2,1)S(1)}, bf16[512,128]{1,0:T(8,128)(2,1)}, u32[]{:S(2)}) copy-start(bf16[512,128]{1,0:T(8,128)(2,1)} %refs_1_.1) | copy-start | bytes 393220
  8.9 7.3 %copy-start.2 = (s32[512]{0:T(512)S(1)}, s32[512]{0:T(512)}, u32[]{:S(2)}) copy-start(s32[512]{0:T(512)} %starts_ref.5) | copy-start | bytes 6148
  12.8 7.8 %collective-permute-start.5 = (bf16[512,128]{1,0:T(8,128)(2,1)S(1)}, bf16[512,128]{1,0:T(8,128)(2,1)S(1)}, u32[]{:S(2)}, u32[]{:S(2)}) collective-permute-start(bf16[512,128]{1,0:T(8,128)(2,1)S(1)} %copy-done.1), channel_id=1, source_target_pairs={{0,26},{2,0},{4,30},{6,4},{8,2},{10,8},{12,6},{14,12},{16,10},{18,... | collective-permute-start | bytes 393224 | tf_op jit(solution)/shard_map/ppermute | solution.py:189
  15.7 4.9 %collective-permute-start.8 = (s32[512]{0:T(512)S(1)}, s32[512]{0:T(512)S(1)}, u32[]{:S(2)}, u32[]{:S(2)}) collective-permute-start(s32[512]{0:T(512)S(1)} %collective-permute-done.2), channel_id=1, source_target_pairs={{0,2},{2,0},{4,6},{6,4},{8,10},{10,8},{12,14},{14,12},{16,18},{18,... | collective-permute-start | bytes 6152 | tf_op jit(solution)/shard_map/ppermute | solution.py:189
  15.7 4.9 %collective-permute-start.4 = (bf16[512,128]{1,0:T(8,128)(2,1)S(1)}, bf16[512,128]{1,0:T(8,128)(2,1)S(1)}, u32[]{:S(2)}, u32[]{:S(2)}) collective-permute-start(bf16[512,128]{1,0:T(8,128)(2,1)S(1)} %collective-permute-done.refs_0_), channel_id=1, source_target_pairs={{0,2},{2,0},{4,6},{6,4},{8,10},{10,8},{12,14},{14,12},{16,18},{18,... | collective-permute-start | bytes 393224 | tf_op jit(solution)/shard_map/ppermute | solution.py:189
  16.2 4.4 %collective-permute-start.6 = (bf16[512,128]{1,0:T(8,128)(2,1)S(1)}, bf16[512,128]{1,0:T(8,128)(2,1)S(1)}, u32[]{:S(2)}, u32[]{:S(2)}) collective-permute-start(bf16[512,128]{1,0:T(8,128)(2,1)S(1)} %collective-permute-done.1.refs_1_), channel_id=1, source_target_pairs={{0,2},{2,0},{4,6},{6,4},{8,10},{10,8},{12,14},{14,12},{16,18},{18,... | collective-permute-start | bytes 393224 | tf_op jit(solution)/shard_map/ppermute | solution.py:189
  20.0 10.1 %collective-permute-start.10 = (bf16[2,512,128]{2,1,0:T(8,128)(2,1)S(1)}, bf16[2,512,128]{2,1,0:T(8,128)(2,1)S(1)}, u32[]{:S(2)}, u32[]{:S(2)}) collective-permute-start(bf16[2,512,128]{2,1,0:T(8,128)(2,1)S(1)} %get-tuple-element.40), channel_id=1, source_target_pairs={{0,2},{2,0},{4,6},{6,4},{8,10},{10,8},{12,14},{14,12},{16,18},{18,... | collective-permute-start | bytes 786440 | tf_op jit(solution)/shard_map/ppermute | solution.py:233
  20.6 5.4 %copy-start = (bf16[512,128]{1,0:T(8,128)(2,1)S(1)}, bf16[512,128]{1,0:T(8,128)(2,1)}, u32[]{:S(2)}) copy-start(bf16[512,128]{1,0:T(8,128)(2,1)} %refs_0_.1) | copy-start | bytes 393220
  20.6 5.4 %copy-start.3 = (s32[512]{0:T(512)S(1)}, s32[512]{0:T(512)}, u32[]{:S(2)}) copy-start(s32[512]{0:T(512)} %param.14) | copy-start | bytes 6148
  30.1 7.6 %collective-permute-start.9 = (bf16[2,512,128]{2,1,0:T(8,128)(2,1)S(1)}, bf16[2,512,128]{2,1,0:T(8,128)(2,1)S(1)}, u32[]{:S(2)}, u32[]{:S(2)}) collective-permute-start(bf16[2,512,128]{2,1,0:T(8,128)(2,1)S(1)} %get-tuple-element.34), channel_id=1, source_target_pairs={{26,0},{0,2},{30,4},{4,6},{2,8},{8,10},{6,12},{12,14},{10,16},{16,... | collective-permute-start | bytes 786440 | tf_op jit(solution)/shard_map/ppermute | solution.py:235
  30.2 12.8 %collective-permute-start.12 = (bf16[512,128]{1,0:T(8,128)(2,1)S(1)}, bf16[512,128]{1,0:T(8,128)(2,1)S(1)}, u32[]{:S(2)}, u32[]{:S(2)}) collective-permute-start(bf16[512,128]{1,0:T(8,128)(2,1)S(1)} %get-tuple-element.46), channel_id=1, source_target_pairs={{0,6},{2,4},{4,10},{6,8},{8,14},{10,12},{12,18},{14,16},{16,22},{1... | collective-permute-start | bytes 393224 | tf_op jit(solution)/shard_map/ppermute | solution.py:189
  32.8 11.6 %collective-permute-start.11 = (bf16[512,128]{1,0:T(8,128)(2,1)S(1)}, bf16[512,128]{1,0:T(8,128)(2,1)S(1)}, u32[]{:S(2)}, u32[]{:S(2)}) collective-permute-start(bf16[512,128]{1,0:T(8,128)(2,1)S(1)} %get-tuple-element.45), channel_id=1, source_target_pairs={{0,6},{2,4},{4,10},{6,8},{8,14},{10,12},{12,18},{14,16},{16,22},{1... | collective-permute-start | bytes 393224 | tf_op jit(solution)/shard_map/ppermute | solution.py:189
  44.4 5.0 %collective-permute-start.14 = (bf16[512,128]{1,0:T(8,128)(2,1)S(1)}, bf16[512,128]{1,0:T(8,128)(2,1)S(1)}, u32[]{:S(2)}, u32[]{:S(2)}) collective-permute-start(bf16[512,128]{1,0:T(8,128)(2,1)S(1)} %fusion), channel_id=1, source_target_pairs={{0,1},{1,0},{2,3},{3,2},{4,5},{5,4},{6,7},{7,6},{8,9},{9,8},{10,11... | collective-permute-start | bytes 393224 | tf_op jit(solution)/shard_map/ppermute | solution.py:249
  46.0 5.0 %collective-permute-start.13 = (bf16[512,128]{1,0:T(8,128)(2,1)S(1)}, bf16[512,128]{1,0:T(8,128)(2,1)S(1)}, u32[]{:S(2)}, u32[]{:S(2)}) collective-permute-start(bf16[512,128]{1,0:T(8,128)(2,1)S(1)} %fusion.1), channel_id=1, source_target_pairs={{0,1},{1,0},{2,3},{3,2},{4,5},{5,4},{6,7},{7,6},{8,9},{9,8},{10,11... | collective-permute-start | bytes 393224 | tf_op jit(solution)/shard_map/ppermute | solution.py:249

commit v4 on v3

--- a/solution.py
+++ b/solution.py
@@ -33,14 +33,14 @@
 
 
 def prep_kernel(
-    q_hbm, g_hbm, o_hbm, places_hbm, starts_hbm, lse_hbm,
-    vec_ref, q_ref, g_ref, o_ref, places_ref, starts_ref, lse_ref, sems, row_sems,
+    g_hbm, o_hbm, places_hbm, starts_hbm, lse_hbm,
+    vec_ref, g_ref, o_ref, places_ref, starts_ref, lse_ref, sems, row_sems,
 ):
     heads, tok = lse_ref.shape
     hd = g_ref.shape[1]
     part = 128
     cols = part * heads
-    pairs = ((g_hbm, g_ref), (o_hbm, o_ref), (q_hbm, q_ref))
+    pairs = ((g_hbm, g_ref), (o_hbm, o_ref))
     copies = [
         [
             pltpu.make_async_copy(src.at[columns(i, cols)], dst.at[columns(i, cols)], sems.at[m, i])
@@ -50,7 +50,7 @@
     ]
     small = ((places_hbm, places_ref), (starts_hbm, starts_ref), (lse_hbm, lse_ref))
     small = [pltpu.make_async_copy(x, y, row_sems.at[m]) for m, (x, y) in enumerate(small)]
-    for copy in small + copies[0] + copies[1] + copies[2]:
+    for copy in small + [x for pair in zip(*copies) for x in pair]:
         copy.start()
     for copy in small:
         copy.wait()
@@ -76,8 +76,6 @@
         high = prod.astype(BF16)
         low = (prod - high.astype(F32)).astype(BF16)
         vec_ref[8:16, rows] = dot(ones, jnp.concatenate([high, low], axis=1), NT)
-    for copy in copies[2]:
-        copy.wait()
 
 
 def grads_kernel(nb, n_blk, first, starts_ref, vec_ref, q_ref, g_ref, *refs):
@@ -94,16 +92,20 @@
     dk_acc[...] = jnp.zeros_like(dk_acc)
     dv_acc[...] = jnp.zeros_like(dv_acc)
 
-    def window(i, at, top):
+    def scores(i, at):
+        rows = columns(i, cols)
+        keys = pl.ds(at, WIN)
+        kw = jnp.concatenate([k[keys, :] for k in ks], axis=0)
+        vw = jnp.concatenate([v[keys, :] for v in vs], axis=0)
+        return dot(kw, q_ref[rows, :], NT), dot(vw, g_ref[rows, :], NT)
+
+    def window(i, at, top, s, dp):
         rows = columns(i, cols)
         keys = pl.ds(at, WIN)
         qs, gs = q_ref[rows, :], g_ref[rows, :]
         kw = jnp.concatenate([k[keys, :] for k in ks], axis=0)
-        vw = jnp.concatenate([v[keys, :] for v in vs], axis=0)
         lse, delta = vec_ref[0:1, rows], vec_ref[8:9, rows]
         begin, place = vec_ref[16:17, rows], vec_ref[24:25, rows]
-        s = dot(kw, qs, NT)
-        dp = dot(vw, gs, NT)
         row = lax.broadcasted_iota(jnp.int32, (WIN, cols), 0) + at
         row_place = (row * n_blk).astype(F32)
         oks = []
@@ -121,9 +123,12 @@
             dk_acc[b, keys, :] += dk[b * WIN : (b + 1) * WIN]
         return dot(kw, low, TN)
 
+    starts = [max((i + 1) * TILE - WIN, 0) for i in range(tiles)]
+    ahead = scores(0, starts[0])
     for i in range(tiles):
         rows = columns(i, cols)
-        dq = window(i, max((i + 1) * TILE - WIN, 0), None)
+        now, ahead = ahead, scores(i + 1, starts[i + 1]) if i + 1 < tiles else None
+        dq = window(i, starts[i], None, *now)
         dq_ref[:, rows] = dq if first else dq_in[:, rows] + dq
     for i in range(tiles):
         top = (i + 1) * TILE - WIN
@@ -134,7 +139,7 @@
         def more(w, carry, i=i, top=top):
             edge = top - w * WIN
             at = pl.multiple_of(jnp.maximum(edge - WIN, 0), math.gcd(TILE, WIN))
-            dq_ref[:, columns(i, cols)] += window(i, at, edge)
+            dq_ref[:, columns(i, cols)] += window(i, at, edge, *scores(i, at))
             return carry
 
         lax.fori_loop(0, far, more, 0)
@@ -206,40 +211,40 @@
 
     q, g, o = (x.reshape(rows, hd) for x in (queries, out_grad, outputs))
     line = lambda x: x.reshape(1, tok)
-    vec, q, g = call(
+    vec, g = call(
         prep_kernel,
-        [shape((32, rows), F32)] + [shape((rows, hd), BF16)] * 2,
-        [pl.BlockSpec(memory_space=pltpu.HBM)] * 6,
+        [shape((32, rows), F32), shape((rows, hd), BF16)],
+        [pl.BlockSpec(memory_space=pltpu.HBM)] * 5,
         [
             pltpu.VMEM((rows, hd), BF16),
             pltpu.VMEM((1, tok), jnp.int32),
             pltpu.VMEM((1, tok), jnp.int32),
             pltpu.VMEM((heads, tok), F32),
-            pltpu.SemaphoreType.DMA((3, tok // 128)),
+            pltpu.SemaphoreType.DMA((2, tok // 128)),
             pltpu.SemaphoreType.DMA((3,)),
         ],
         2**32,
         *(
             pltpu.with_memory_space_constraint(x, pltpu.HBM)
-            for x in (q, g, o, line(positions), line(doc_start), logsumexp.T)
+            for x in (g, o, line(positions), line(doc_start), logsumexp.T)
         ),
     )
     a, vec = lax.optimization_barrier((a, vec))
     c = send(a, cores)
     dq, a_part = grads(n, [BF16], 2**33, doc_start, vec, q, g, [a])
-    dq, b_part, c_part = grads(n, [BF16, BF16], 2**34, doc_start, vec, q, g, [b, c], dq)
+    dq, c_part = grads(n, [BF16], 2**33, doc_start, vec, q, g, [c], dq)
 
     other = [(0, 1), (1, 0)]
     near = lax.ppermute(a_part, "blk", cores)
-    b_part, c_part = lax.optimization_barrier((b_part, c_part))
-    from_b = lax.ppermute(b_part, "blk", [(d, s) for s, d in odd_even])
     home = [(d, (d + 1) % n if d % 2 else (d + 3) % n) for d in blocks]
     from_a = list(send([c_part[i] + near[i] for i in range(2)], home))
+    dq, b_part = grads(n, [BF16], 2**33, doc_start, vec, q, g, [b], dq)
+    from_b = send([b_part], [(d, s) for s, d in odd_even])[0]
     dq, own = grads(n, [F32], 2**33, doc_start, vec, q, g, [mine], dq)
+    from_b, own = lax.optimization_barrier((from_b, own))
     query_grad = call(
         functools.partial(finish_kernel, heads), shape((rows, hd), BF16), [], [], 2**32, dq
     )
-    from_b, query_grad, own = lax.optimization_barrier((from_b, query_grad, own))
     halves, rests = [], []
     for i in range(2):
         if i:

time: 51.8 us -> 53.7 us (1.037)
  starting transfers between devices: 13.1 us -> 16.6 us
  waiting for transfers between devices: 17.9 us -> 15.8 us
    ppermute x1 -> x0, waiting for transfers between devices: 4.73 us -> none  [on_device(): from_b = lax.ppermute(b_part, 'blk', [(d, s) for s, d in odd_even])]
    ppermute x11 -> x12, starting transfers between devices: 10.3 us -> 14.4 us  [send(): got.append(lax.ppermute(x, 'blk', pairs))]
    ppermute x11 -> x12, waiting for transfers between devices: 9.37 us -> 11.3 us  [send(): got.append(lax.ppermute(x, 'blk', pairs))]
    ppermute x2, waiting for transfers between devices: 3.75 us -> 4.5 us  [on_device(): rests.append(lax.ppermute(halves[i], 'head', other))]
    pallas_call x5 -> x6, Pallas kernels: 18.4 us -> 18.8 us  [call(): pl.pallas_call(body, out_shape=outs, in_specs=specs + [vmem] * (len(args)...]
  transfers between devices with their start and end apart: 15 -> 15, of which waited for: 7 -> 6; matrix products, arithmetic and copies ran while one was open for 2% -> 1% of each run, Pallas kernels for 36% -> 35%
where the time goes in v4:
time: 53.7 us; the launch traced here: 53.5 us
  Pallas kernels  18.8 us (35%)
  starting transfers between devices  16.6 us (31%)
  waiting for transfers between devices  15.8 us (29%)
  other arithmetic  1.53 us (3%)
  between operations  0.77 us (1%)
    pallas_call x6, Pallas kernels, call(): pl.pallas_call(body, out_shape=outs, in_specs=specs + [vmem] * (len(args)...  18.8 us
    ppermute x12, starting transfers between devices, send(): got.append(lax.ppermute(x, 'blk', pairs))  14.4 us
    ppermute x12, waiting for transfers between devices, send(): got.append(lax.ppermute(x, 'blk', pairs))  11.3 us
    ppermute x2, waiting for transfers between devices, on_device(): rests.append(lax.ppermute(halves[i], 'head', other))  4.5 us
    ppermute x2, starting transfers between devices, on_device(): rests.append(lax.ppermute(halves[i], 'head', other))  2.09 us
    convert_element_type x2, other arithmetic, on_device(): sums.append((halves[i].astype(F32) + rests[i].astype(F32)).astype(BF16))  1.38 us
  transfers between devices with their start and end apart: 15, of which 6 were waited for; matrix products, arithmetic and copies ran while one was open for 1% of the time, Pallas kernels for 35%

profile of v4, /device:TPU:0, one launch (start us, length us, event | category | flops | bytes accessed | tf_op | source)
XLA Modules:
  0.0 53.5 jit_solution(4364792413806551816)
XLA Ops:
  0.6 6.1 %collective-permute-start.2 = (s32[512]{0:T(512)}, s32[512]{0:T(512)S(1)}, u32[]{:S(2)}, u32[]{:S(2)}) collective-permute-start(s32[512]{0:T(512)} %param.14), channel_id=1, source_target_pairs={{0,28},{2,30},{4,0},{6,2},{8,4},{10,6},{12,8},{14,10},{16,12},{18,... | collective-permute-start | bytes 6152 | tf_op jit(solution)/shard_map/ppermute | solution.py:194
  6.7 0.0 collective-permute-start.5
  6.7 0.5 collective-permute-start
  7.2 0.3 collective-permute-start.3
  7.5 1.4 %collective-permute-start.1 = (bf16[512,128]{1,0:T(8,128)(2,1)}, bf16[512,128]{1,0:T(8,128)(2,1)S(1)}, u32[]{:S(2)}, u32[]{:S(2)}) collective-permute-start(bf16[512,128]{1,0:T(8,128)(2,1)} %refs_1_.1), channel_id=1, source_target_pairs={{0,28},{2,30},{4,0},{6,2},{8,4},{10,6},{12,8},{14,10},{16,12},{18,... | collective-permute-start | bytes 393224 | tf_op jit(solution)/shard_map/ppermute | solution.py:194
  8.9 3.5 %shard_map.103 = (f32[32,4096]{1,0:T(8,128)S(1)}, bf16[4096,128]{1,0:T(8,128)(2,1)S(1)}) custom-call(bf16[4096,128]{1,0:T(8,128)(2,1)} %bitcast.38, bf16[4096,128]{1,0:T(8,128)(2,1)} %bitcast.39, s32[1,512]{1,0:T(1,128)} %bitcast.33, s32[1,512]{1,0:T(1,128)} %bitcast.32, f32[8,512]{1,0:T(8,128)} %bitcast.40), custom_call_target="tpu_custom_call" | custom-call | flops 4294967296 | bytes 4194304 | tf_op jit(solution)/shard_map/pallas_call | solution.py:162
  12.4 0.0 collective-permute-done.2
  12.5 0.8 %collective-permute-done.refs_0_ = bf16[512,128]{1,0:T(8,128)(2,1)S(1)} collective-permute-done((bf16[512,128]{1,0:T(8,128)(2,1)}, bf16[512,128]{1,0:T(8,128)(2,1)S(1)}, u32[]{:S(2)}, u32[]{:S(2)}) %collective-permute-start) | collective-permute-done | bytes 131104 | tf_op jit(solution)/shard_map/ppermute | solution.py:194
  13.3 2.3 %collective-permute-done.1.refs_1_ = bf16[512,128]{1,0:T(8,128)(2,1)S(1)} collective-permute-done((bf16[512,128]{1,0:T(8,128)(2,1)}, bf16[512,128]{1,0:T(8,128)(2,1)S(1)}, u32[]{:S(2)}, u32[]{:S(2)}) %collective-permute-start.1) | collective-permute-done | bytes 131104 | tf_op jit(solution)/shard_map/ppermute | solution.py:194
  15.7 0.0 collective-permute-start.8
  15.7 0.5 collective-permute-start.6
  16.2 0.0 collective-permute-start.7
  16.2 0.0 copy-done
  16.2 0.0 copy-done.3
  16.2 0.0 copy-start.2
  16.2 3.3 %shard_map.104 = (f32[128,4096]{1,0:T(8,128)S(1)}, bf16[2,512,128]{2,1,0:T(8,128)(2,1)S(1)}) custom-call(s32[512]{0:T(512)S(1)} %copy-done.3, f32[32,4096]{1,0:T(8,128)S(1)} %get-tuple-element.22.vec_ref, bf16[4096,128]{1,0:T(8,128)(2,1)S(1)} %bitcast.28, bf16[4096,128]{1,0:T(8,128)(2,1)S(1)} %get-tuple-element.23.g_ref, ...), custom_call_target="tpu_custom_call" | custom-call | flops 8589934592 | bytes 4194304 | tf_op jit(solution)/shard_map/pallas_call | solution.py:162
  19.5 0.0 collective-permute-done.8
  19.5 0.0 copy-done.2
  19.5 0.6 %collective-permute-start.4 = (bf16[512,128]{1,0:T(8,128)(2,1)S(1)}, bf16[512,128]{1,0:T(8,128)(2,1)S(1)}, u32[]{:S(2)}, u32[]{:S(2)}) collective-permute-start(bf16[512,128]{1,0:T(8,128)(2,1)S(1)} %copy-done.2), channel_id=1, source_target_pairs={{0,26},{2,0},{4,30},{6,4},{8,2},{10,8},{12,6},{14,12},{16,10},{18,... | collective-permute-start | bytes 393224 | tf_op jit(solution)/shard_map/ppermute | solution.py:194
  20.1 0.0 collective-permute-done.6.refs_0_
  20.1 0.0 collective-permute-start.9
  20.1 0.0 collective-permute-done.7.refs_1_
  20.1 3.5 %shard_map.105 = (f32[128,4096]{1,0:T(8,128)S(1)}, bf16[2,512,128]{2,1,0:T(8,128)(2,1)S(1)}) custom-call(s32[512]{0:T(512)S(1)} %copy-done.3, f32[32,4096]{1,0:T(8,128)S(1)} %get-tuple-element.22.vec_ref, bf16[4096,128]{1,0:T(8,128)(2,1)S(1)} %bitcast.29, bf16[4096,128]{1,0:T(8,128)(2,1)S(1)} %get-tuple-element.23.g_ref, ...), custom_call_target="tpu_custom_call", output_to_operand_aliasing={{0}: (7, {})} | custom-call | flops 8589934592 | bytes 4194304 | tf_op jit(solution)/shard_map/pallas_call | solution.py:162
  23.6 0.0 collective-permute-done.5
  23.7 0.0 collective-permute-done.3.refs_0_
  23.7 0.0 collective-permute-done.4.refs_1_
  23.7 0.0 copy-start.1
  23.7 0.0 copy-start.4
  23.7 3.7 %shard_map.106 = (f32[128,4096]{1,0:T(8,128)S(1)}, bf16[2,512,128]{2,1,0:T(8,128)(2,1)S(1)}) custom-call(s32[512]{0:T(512)S(1)} %copy-done.3, f32[32,4096]{1,0:T(8,128)S(1)} %get-tuple-element.22.vec_ref, bf16[4096,128]{1,0:T(8,128)(2,1)S(1)} %bitcast.30, bf16[4096,128]{1,0:T(8,128)(2,1)S(1)} %get-tuple-element.23.g_ref, ...), custom_call_target="tpu_custom_call", output_to_operand_aliasing={{0}: (7, {})} | custom-call | flops 8589934592 | bytes 4194304 | tf_op jit(solution)/shard_map/pallas_call | solution.py:162
  27.4 0.8 %collective-permute-start.11 = (bf16[2,512,128]{2,1,0:T(8,128)(2,1)S(1)}, bf16[2,512,128]{2,1,0:T(8,128)(2,1)S(1)}, u32[]{:S(2)}, u32[]{:S(2)}) collective-permute-start(bf16[2,512,128]{2,1,0:T(8,128)(2,1)S(1)} %get-tuple-element.33), channel_id=1, source_target_pairs={{26,0},{0,2},{30,4},{4,6},{2,8},{8,10},{6,12},{12,14},{10,16},{16,... | collective-permute-start | bytes 786440 | tf_op jit(solution)/shard_map/ppermute | solution.py:194
  28.2 0.0 collective-permute-done.9
  28.2 4.2 %collective-permute-start.12 = (bf16[512,128]{1,0:T(8,128)(2,1)S(1)}, bf16[512,128]{1,0:T(8,128)(2,1)S(1)}, u32[]{:S(2)}, u32[]{:S(2)}) collective-permute-start(bf16[512,128]{1,0:T(8,128)(2,1)S(1)} %get-tuple-element.40), channel_id=1, source_target_pairs={{0,6},{2,4},{4,10},{6,8},{8,14},{10,12},{12,18},{14,16},{16,22},{1... | collective-permute-start | bytes 393224 | tf_op jit(solution)/shard_map/ppermute | solution.py:194
  32.4 0.0 copy-done.1
  32.4 0.0 copy-done.4
  32.4 3.5 %shard_map.107 = (f32[128,4096]{1,0:T(8,128)S(1)}, f32[2,512,128]{2,1,0:T(8,128)S(1)}) custom-call(s32[512]{0:T(512)S(1)} %copy-done.3, f32[32,4096]{1,0:T(8,128)S(1)} %get-tuple-element.22.vec_ref, bf16[4096,128]{1,0:T(8,128)(2,1)S(1)} %bitcast.31, bf16[4096,128]{1,0:T(8,128)(2,1)S(1)} %get-tuple-element.23.g_ref, ...), custom_call_target="tpu_custom_call", output_to_operand_aliasing={{0}: (7, {})} | custom-call | flops 8589934592 | bytes 4194304 | tf_op jit(solution)/shard_map/pallas_call | solution.py:162
  35.9 0.1 collective-permute-start.10
  36.0 0.0 collective-permute-done.11
  36.0 5.8 %collective-permute-done.12 = bf16[512,128]{1,0:T(8,128)(2,1)S(1)} collective-permute-done((bf16[512,128]{1,0:T(8,128)(2,1)S(1)}, bf16[512,128]{1,0:T(8,128)(2,1)S(1)}, u32[]{:S(2)}, u32[]{:S(2)}) %collective-permute-start.12) | collective-permute-done | bytes 131104 | tf_op jit(solution)/shard_map/ppermute | solution.py:194
  41.8 0.1 fusion.1
  41.9 2.2 %collective-permute-done.10 = bf16[512,128]{1,0:T(8,128)(2,1)S(1)} collective-permute-done((bf16[512,128]{1,0:T(8,128)(2,1)S(1)}, bf16[512,128]{1,0:T(8,128)(2,1)S(1)}, u32[]{:S(2)}, u32[]{:S(2)}) %collective-permute-start.10) | collective-permute-done | bytes 131104 | tf_op jit(solution)/shard_map/ppermute | solution.py:194
  44.2 0.1 fusion
  44.2 1.6 %collective-permute-start.14 = (bf16[512,128]{1,0:T(8,128)(2,1)S(1)}, bf16[512,128]{1,0:T(8,128)(2,1)S(1)}, u32[]{:S(2)}, u32[]{:S(2)}) collective-permute-start(bf16[512,128]{1,0:T(8,128)(2,1)S(1)} %fusion), channel_id=1, source_target_pairs={{0,1},{1,0},{2,3},{3,2},{4,5},{5,4},{6,7},{7,6},{8,9},{9,8},{10,11... | collective-permute-start | bytes 393224 | tf_op jit(solution)/shard_map/ppermute | solution.py:254
  45.8 1.3 %shard_map.108 = bf16[4096,128]{1,0:T(8,128)(2,1)} custom-call(f32[128,4096]{1,0:T(8,128)S(1)} %get-tuple-element.30.dq_ref), custom_call_target="tpu_custom_call" | custom-call | flops 4294967296 | bytes 4194304 | tf_op jit(solution)/shard_map/pallas_call | solution.py:162
  47.1 0.5 %collective-permute-start.13 = (bf16[512,128]{1,0:T(8,128)(2,1)S(1)}, bf16[512,128]{1,0:T(8,128)(2,1)S(1)}, u32[]{:S(2)}, u32[]{:S(2)}) collective-permute-start(bf16[512,128]{1,0:T(8,128)(2,1)S(1)} %fusion.1), channel_id=1, source_target_pairs={{0,1},{1,0},{2,3},{3,2},{4,5},{5,4},{6,7},{7,6},{8,9},{9,8},{10,11... | collective-permute-start | bytes 393224 | tf_op jit(solution)/shard_map/ppermute | solution.py:254
  47.6 2.7 %collective-permute-done.14 = bf16[512,128]{1,0:T(8,128)(2,1)S(1)} collective-permute-done((bf16[512,128]{1,0:T(8,128)(2,1)S(1)}, bf16[512,128]{1,0:T(8,128)(2,1)S(1)}, u32[]{:S(2)}, u32[]{:S(2)}) %collective-permute-start.14) | collective-permute-done | bytes 131104 | tf_op jit(solution)/shard_map/ppermute | solution.py:254
  50.3 0.7 %add_convert_fusion = bf16[512,128]{1,0:T(8,128)(2,1)} fusion(bf16[512,128]{1,0:T(8,128)(2,1)S(1)} %collective-permute-done.14, bf16[512,128]{1,0:T(8,128)(2,1)S(1)} %fusion), kind=kLoop, calls=%fused_computation.6 | loop fusion | flops 262144 | bytes 393216 | tf_op jit(solution)/shard_map/convert_element_type | solution.py:257
  51.0 1.8 %collective-permute-done.13 = bf16[512,128]{1,0:T(8,128)(2,1)S(1)} collective-permute-done((bf16[512,128]{1,0:T(8,128)(2,1)S(1)}, bf16[512,128]{1,0:T(8,128)(2,1)S(1)}, u32[]{:S(2)}, u32[]{:S(2)}) %collective-permute-start.13) | collective-permute-done | bytes 131104 | tf_op jit(solution)/shard_map/ppermute | solution.py:254
  52.8 0.7 %add_convert_fusion.1 = bf16[512,128]{1,0:T(8,128)(2,1)} fusion(bf16[512,128]{1,0:T(8,128)(2,1)S(1)} %collective-permute-done.13, bf16[512,128]{1,0:T(8,128)(2,1)S(1)} %fusion.1), kind=kLoop, calls=%fused_computation.7 | loop fusion | flops 262144 | bytes 393216 | tf_op jit(solution)/shard_map/convert_element_type | solution.py:257
  (3 shorter events, 0.0 us)
Async XLA Ops:
  0.6 11.8 %collective-permute-start.2 = (s32[512]{0:T(512)}, s32[512]{0:T(512)S(1)}, u32[]{:S(2)}, u32[]{:S(2)}) collective-permute-start(s32[512]{0:T(512)} %param.14), channel_id=1, source_target_pairs={{0,28},{2,30},{4,0},{6,2},{8,4},{10,6},{12,8},{14,10},{16,12},{18,... | collective-permute-start | bytes 6152 | tf_op jit(solution)/shard_map/ppermute | solution.py:194
  6.7 16.9 %collective-permute-start.5 = (s32[512]{0:T(512)}, s32[512]{0:T(512)S(1)}, u32[]{:S(2)}, u32[]{:S(2)}) collective-permute-start(s32[512]{0:T(512)} %param.14), channel_id=1, source_target_pairs={{0,26},{2,0},{4,30},{6,4},{8,2},{10,8},{12,6},{14,12},{16,10},{18,... | collective-permute-start | bytes 6152 | tf_op jit(solution)/shard_map/ppermute | solution.py:194
  6.7 6.6 %collective-permute-start = (bf16[512,128]{1,0:T(8,128)(2,1)}, bf16[512,128]{1,0:T(8,128)(2,1)S(1)}, u32[]{:S(2)}, u32[]{:S(2)}) collective-permute-start(bf16[512,128]{1,0:T(8,128)(2,1)} %refs_0_.1), channel_id=1, source_target_pairs={{0,28},{2,30},{4,0},{6,2},{8,4},{10,6},{12,8},{14,10},{16,12},{18,... | collective-permute-start | bytes 393224 | tf_op jit(solution)/shard_map/ppermute | solution.py:194
  7.2 16.4 %collective-permute-start.3 = (bf16[512,128]{1,0:T(8,128)(2,1)}, bf16[512,128]{1,0:T(8,128)(2,1)S(1)}, u32[]{:S(2)}, u32[]{:S(2)}) collective-permute-start(bf16[512,128]{1,0:T(8,128)(2,1)} %refs_0_.1), channel_id=1, source_target_pairs={{0,26},{2,0},{4,30},{6,4},{8,2},{10,8},{12,6},{14,12},{16,10},{18,... | collective-permute-start | bytes 393224 | tf_op jit(solution)/shard_map/ppermute | solution.py:194
  7.5 8.1 %collective-permute-start.1 = (bf16[512,128]{1,0:T(8,128)(2,1)}, bf16[512,128]{1,0:T(8,128)(2,1)S(1)}, u32[]{:S(2)}, u32[]{:S(2)}) collective-permute-start(bf16[512,128]{1,0:T(8,128)(2,1)} %refs_1_.1), channel_id=1, source_target_pairs={{0,28},{2,30},{4,0},{6,2},{8,4},{10,6},{12,8},{14,10},{16,12},{18,... | collective-permute-start | bytes 393224 | tf_op jit(solution)/shard_map/ppermute | solution.py:194
  8.9 7.3 %copy-start = (bf16[512,8,128]{2,1,0:T(8,128)(2,1)S(1)}, bf16[512,8,128]{2,1,0:T(8,128)(2,1)}, u32[]{:S(2)}) copy-start(bf16[512,8,128]{2,1,0:T(8,128)(2,1)} %param.8) | copy-start | bytes 3145732
  8.9 7.3 %copy-start.3 = (s32[512]{0:T(512)S(1)}, s32[512]{0:T(512)}, u32[]{:S(2)}) copy-start(s32[512]{0:T(512)} %starts_ref.7) | copy-start | bytes 6148
  15.7 3.8 %collective-permute-start.8 = (s32[512]{0:T(512)S(1)}, s32[512]{0:T(512)S(1)}, u32[]{:S(2)}, u32[]{:S(2)}) collective-permute-start(s32[512]{0:T(512)S(1)} %collective-permute-done.2), channel_id=1, source_target_pairs={{0,2},{2,0},{4,6},{6,4},{8,10},{10,8},{12,14},{14,12},{16,18},{18,... | collective-permute-start | bytes 6152 | tf_op jit(solution)/shard_map/ppermute | solution.py:194
  15.7 4.4 %collective-permute-start.6 = (bf16[512,128]{1,0:T(8,128)(2,1)S(1)}, bf16[512,128]{1,0:T(8,128)(2,1)S(1)}, u32[]{:S(2)}, u32[]{:S(2)}) collective-permute-start(bf16[512,128]{1,0:T(8,128)(2,1)S(1)} %collective-permute-done.refs_0_), channel_id=1, source_target_pairs={{0,2},{2,0},{4,6},{6,4},{8,10},{10,8},{12,14},{14,12},{16,18},{18,... | collective-permute-start | bytes 393224 | tf_op jit(solution)/shard_map/ppermute | solution.py:194
  16.2 4.0 %collective-permute-start.7 = (bf16[512,128]{1,0:T(8,128)(2,1)S(1)}, bf16[512,128]{1,0:T(8,128)(2,1)S(1)}, u32[]{:S(2)}, u32[]{:S(2)}) collective-permute-start(bf16[512,128]{1,0:T(8,128)(2,1)S(1)} %collective-permute-done.1.refs_1_), channel_id=1, source_target_pairs={{0,2},{2,0},{4,6},{6,4},{8,10},{10,8},{12,14},{14,12},{16,18},{18,... | collective-permute-start | bytes 393224 | tf_op jit(solution)/shard_map/ppermute | solution.py:194
  16.2 3.3 %copy-start.2 = (bf16[512,128]{1,0:T(8,128)(2,1)S(1)}, bf16[512,128]{1,0:T(8,128)(2,1)}, u32[]{:S(2)}) copy-start(bf16[512,128]{1,0:T(8,128)(2,1)} %refs_1_.1) | copy-start | bytes 393220
  19.5 4.2 %collective-permute-start.4 = (bf16[512,128]{1,0:T(8,128)(2,1)S(1)}, bf16[512,128]{1,0:T(8,128)(2,1)S(1)}, u32[]{:S(2)}, u32[]{:S(2)}) collective-permute-start(bf16[512,128]{1,0:T(8,128)(2,1)S(1)} %copy-done.2), channel_id=1, source_target_pairs={{0,26},{2,0},{4,30},{6,4},{8,2},{10,8},{12,6},{14,12},{16,10},{18,... | collective-permute-start | bytes 393224 | tf_op jit(solution)/shard_map/ppermute | solution.py:194
  20.1 8.1 %collective-permute-start.9 = (bf16[2,512,128]{2,1,0:T(8,128)(2,1)S(1)}, bf16[2,512,128]{2,1,0:T(8,128)(2,1)S(1)}, u32[]{:S(2)}, u32[]{:S(2)}) collective-permute-start(bf16[2,512,128]{2,1,0:T(8,128)(2,1)S(1)} %get-tuple-element.32), channel_id=1, source_target_pairs={{0,2},{2,0},{4,6},{6,4},{8,10},{10,8},{12,14},{14,12},{16,18},{18,... | collective-permute-start | bytes 786440 | tf_op jit(solution)/shard_map/ppermute | solution.py:238
  23.7 8.7 %copy-start.1 = (bf16[512,128]{1,0:T(8,128)(2,1)S(1)}, bf16[512,128]{1,0:T(8,128)(2,1)}, u32[]{:S(2)}) copy-start(bf16[512,128]{1,0:T(8,128)(2,1)} %refs_0_.1) | copy-start | bytes 393220
  23.7 8.7 %copy-start.4 = (s32[512]{0:T(512)S(1)}, s32[512]{0:T(512)}, u32[]{:S(2)}) copy-start(s32[512]{0:T(512)} %param.14) | copy-start | bytes 6148
  27.4 8.6 %collective-permute-start.11 = (bf16[2,512,128]{2,1,0:T(8,128)(2,1)S(1)}, bf16[2,512,128]{2,1,0:T(8,128)(2,1)S(1)}, u32[]{:S(2)}, u32[]{:S(2)}) collective-permute-start(bf16[2,512,128]{2,1,0:T(8,128)(2,1)S(1)} %get-tuple-element.33), channel_id=1, source_target_pairs={{26,0},{0,2},{30,4},{4,6},{2,8},{8,10},{6,12},{12,14},{10,16},{16,... | collective-permute-start | bytes 786440 | tf_op jit(solution)/shard_map/ppermute | solution.py:194
  28.2 13.6 %collective-permute-start.12 = (bf16[512,128]{1,0:T(8,128)(2,1)S(1)}, bf16[512,128]{1,0:T(8,128)(2,1)S(1)}, u32[]{:S(2)}, u32[]{:S(2)}) collective-permute-start(bf16[512,128]{1,0:T(8,128)(2,1)S(1)} %get-tuple-element.40), channel_id=1, source_target_pairs={{0,6},{2,4},{4,10},{6,8},{8,14},{10,12},{12,18},{14,16},{16,22},{1... | collective-permute-start | bytes 393224 | tf_op jit(solution)/shard_map/ppermute | solution.py:194
  35.9 8.2 %collective-permute-start.10 = (bf16[512,128]{1,0:T(8,128)(2,1)S(1)}, bf16[512,128]{1,0:T(8,128)(2,1)S(1)}, u32[]{:S(2)}, u32[]{:S(2)}) collective-permute-start(bf16[512,128]{1,0:T(8,128)(2,1)S(1)} %get-tuple-element.39), channel_id=1, source_target_pairs={{0,6},{2,4},{4,10},{6,8},{8,14},{10,12},{12,18},{14,16},{16,22},{1... | collective-permute-start | bytes 393224 | tf_op jit(solution)/shard_map/ppermute | solution.py:194
  44.2 6.1 %collective-permute-start.14 = (bf16[512,128]{1,0:T(8,128)(2,1)S(1)}, bf16[512,128]{1,0:T(8,128)(2,1)S(1)}, u32[]{:S(2)}, u32[]{:S(2)}) collective-permute-start(bf16[512,128]{1,0:T(8,128)(2,1)S(1)} %fusion), channel_id=1, source_target_pairs={{0,1},{1,0},{2,3},{3,2},{4,5},{5,4},{6,7},{7,6},{8,9},{9,8},{10,11... | collective-permute-start | bytes 393224 | tf_op jit(solution)/shard_map/ppermute | solution.py:254
  47.1 5.7 %collective-permute-start.13 = (bf16[512,128]{1,0:T(8,128)(2,1)S(1)}, bf16[512,128]{1,0:T(8,128)(2,1)S(1)}, u32[]{:S(2)}, u32[]{:S(2)}) collective-permute-start(bf16[512,128]{1,0:T(8,128)(2,1)S(1)} %fusion.1), channel_id=1, source_target_pairs={{0,1},{1,0},{2,3},{3,2},{4,5},{5,4},{6,7},{7,6},{8,9},{9,8},{10,11... | collective-permute-start | bytes 393224 | tf_op jit(solution)/shard_map/ppermute | solution.py:254

commit v5 on v4

--- a/solution.py
+++ b/solution.py
@@ -50,8 +50,8 @@
     ]
     small = ((places_hbm, places_ref), (starts_hbm, starts_ref), (lse_hbm, lse_ref))
     small = [pltpu.make_async_copy(x, y, row_sems.at[m]) for m, (x, y) in enumerate(small)]
-    for copy in small + [x for pair in zip(*copies) for x in pair]:
-        copy.start()
+    for i, copy in enumerate(small + [x for pair in zip(*copies) for x in pair]):
+        copy.start(priority=i % 2)
     for copy in small:
         copy.wait()
     spread = lax.broadcasted_iota(jnp.int32, (part, cols), 1) // heads == lax.broadcasted_iota(
@@ -78,10 +78,8 @@
         vec_ref[8:16, rows] = dot(ones, jnp.concatenate([high, low], axis=1), NT)
 
 
-def grads_kernel(nb, n_blk, first, starts_ref, vec_ref, q_ref, g_ref, *refs):
+def grads_kernel(nb, n_blk, starts_ref, vec_ref, q_ref, g_ref, *refs):
     ks, vs, places, refs = refs[:nb], refs[nb : 2 * nb], refs[2 * nb : 3 * nb], refs[3 * nb :]
-    if not first:
-        dq_in, *refs = refs
     dq_ref, *outs, dk_acc, dv_acc = refs
     hd = q_ref.shape[1]
     tok = ks[0].shape[0]
@@ -128,8 +126,7 @@
     for i in range(tiles):
         rows = columns(i, cols)
         now, ahead = ahead, scores(i + 1, starts[i + 1]) if i + 1 < tiles else None
-        dq = window(i, starts[i], None, *now)
-        dq_ref[:, rows] = dq if first else dq_in[:, rows] + dq
+        dq_ref[:, rows] = window(i, starts[i], None, *now)
     for i in range(tiles):
         top = (i + 1) * TILE - WIN
         if top <= 0:
@@ -144,20 +141,24 @@
 
         lax.fori_loop(0, far, more, 0)
 
+    if len(outs) > nb:
+        outs = [jax.tree.map(lambda x: x.at[0], outs)]
     for b, out in enumerate(outs):
-        out[0] = (dk_acc[b] * scale).astype(out.dtype)
-        out[1] = dv_acc[b].astype(out.dtype)
-
-
-def finish_kernel(heads, dq_ref, out_ref):
-    hd, rows = dq_ref.shape
+        for at, x in ((0, dk_acc[b] * scale), (1, dv_acc[b])):
+            part = out[at] if isinstance(out, list) else out.at[at]
+            part[...] = x.astype(part.dtype)
+
+
+def finish_kernel(heads, *refs):
+    *parts, out_ref = refs
+    rows, hd = out_ref.shape
     cols = TILE * heads
     for i in range(rows // cols):
         at = columns(i, cols)
-        out_ref[at, :] = (dq_ref[:, at] * hd**-0.5).T.astype(BF16)
-
-
-def call(body, outs, specs, scratch, flops, *args, **more):
+        out_ref[at, :] = (sum(x[:, at] for x in parts) * hd**-0.5).T.astype(BF16)
+
+
+def call(body, outs, specs, scratch, flops, *args):
     vmem = pl.BlockSpec(memory_space=pltpu.VMEM)
     return pl.pallas_call(
         body,
@@ -167,24 +168,22 @@
         scratch_shapes=scratch,
         compiler_params=pltpu.CompilerParams(vmem_limit_bytes=32 * 2**20),
         cost_estimate=pl.CostEstimate(flops=flops, bytes_accessed=4 * 2**20, transcendentals=0),
-        **more,
     )(*args)
 
 
-def grads(n, types, flops, doc_start, vec, q, g, groups, dq=None):
+def grads(n, types, flops, doc_start, vec, q, g, groups, split=False):
     nb = len(groups)
     rows, hd = q.shape
     tok = groups[0][0].shape[0]
     shape = jax.ShapeDtypeStruct
-    last = [] if dq is None else [dq]
     return call(
-        functools.partial(grads_kernel, nb, n, dq is None),
-        [shape((hd, rows), F32)] + [shape((2, tok, hd), t) for t in types],
+        functools.partial(grads_kernel, nb, n),
+        [shape((hd, rows), F32)]
+        + [shape((1, tok, hd) if split else (2, tok, hd), t) for t in types for _ in range(2 if split else 1)],
         [pl.BlockSpec(memory_space=pltpu.SMEM)],
         [pltpu.VMEM((nb, tok, hd), F32)] * 2,
         flops,
-        doc_start, vec, q, g, *(x[i].reshape(-1, x[i].shape[-1]) for i in range(3) for x in groups), *last,
-        input_output_aliases={} if dq is None else {4 + 3 * nb: 0},
+        doc_start, vec, q, g, *(x[i].reshape(-1, x[i].shape[-1]) for i in range(3) for x in groups),
     )
 
 
@@ -231,25 +230,26 @@
     )
     a, vec = lax.optimization_barrier((a, vec))
     c = send(a, cores)
-    dq, a_part = grads(n, [BF16], 2**33, doc_start, vec, q, g, [a])
-    dq, c_part = grads(n, [BF16], 2**33, doc_start, vec, q, g, [c], dq)
+    dq_a, a_part = grads(n, [BF16], 2**33, doc_start, vec, q, g, [a])
+    dq_c, c_part = grads(n, [BF16], 2**33, doc_start, vec, q, g, [c])
 
     other = [(0, 1), (1, 0)]
     near = lax.ppermute(a_part, "blk", cores)
     home = [(d, (d + 1) % n if d % 2 else (d + 3) % n) for d in blocks]
     from_a = list(send([c_part[i] + near[i] for i in range(2)], home))
-    dq, b_part = grads(n, [BF16], 2**33, doc_start, vec, q, g, [b], dq)
-    from_b = send([b_part], [(d, s) for s, d in odd_even])[0]
-    dq, own = grads(n, [F32], 2**33, doc_start, vec, q, g, [mine], dq)
-    from_b, own = lax.optimization_barrier((from_b, own))
+    dq_b, *b_parts = grads(n, [BF16], 2**33, doc_start, vec, q, g, [b], split=True)
+    from_b = list(send(b_parts, [(d, s) for s, d in odd_even]))
+    dq_own, own = grads(n, [F32], 2**33, doc_start, vec, q, g, [mine])
+    from_b[0], own = lax.optimization_barrier((from_b[0], own))
     query_grad = call(
-        functools.partial(finish_kernel, heads), shape((rows, hd), BF16), [], [], 2**32, dq
+        functools.partial(finish_kernel, heads), shape((rows, hd), BF16), [], [], 2**32,
+        dq_a, dq_c, dq_b, dq_own,
     )
     halves, rests = [], []
     for i in range(2):
         if i:
-            from_a[i], halves[0] = lax.optimization_barrier((from_a[i], halves[0]))
-        half = own[i] + from_a[i].astype(F32) + from_b[i].astype(F32)
+            from_b[i], from_a[i], halves[0] = lax.optimization_barrier((from_b[i], from_a[i], halves[0]))
+        half = own[i] + from_a[i].astype(F32) + from_b[i].reshape(tok, hd).astype(F32)
         halves.append(half.astype(BF16))
         rests.append(lax.ppermute(halves[i], "head", other))
     sums = []

time: 53.7 us -> 49.5 us (0.922)
  starting transfers between devices: 16.6 us -> 14.1 us
  waiting for transfers between devices: 15.8 us -> 14.7 us
  Pallas kernels: 18.8 us -> 18.2 us
    ppermute x12 -> x13, starting transfers between devices: 14.4 us -> 12 us  [send(): got.append(lax.ppermute(x, 'blk', pairs))]
    ppermute x12 -> x13, waiting for transfers between devices: 11.3 us -> 10.2 us  [send(): got.append(lax.ppermute(x, 'blk', pairs))]
    pallas_call x6, Pallas kernels: 18.8 us -> 18.2 us  [call(): pl.pallas_call(body, out_shape=outs, in_specs=specs + [vmem] * (len(args)...]
  transfers between devices with their start and end apart: 15 -> 16, of which waited for: 6 -> 8; matrix products, arithmetic and copies ran while one was open for 1% -> 2% of each run, Pallas kernels for 35% -> 37%
where the time goes in v5:
time: 49.5 us; the launch traced here: 49.3 us
  Pallas kernels  18.2 us (37%)
  waiting for transfers between devices  14.7 us (30%)
  starting transfers between devices  14.1 us (28%)
  other arithmetic  1.52 us (3%)
  between operations  0.77 us (2%)
    pallas_call x6, Pallas kernels, call(): pl.pallas_call(body, out_shape=outs, in_specs=specs + [vmem] * (len(args)...  18.2 us
    ppermute x13, starting transfers between devices, send(): got.append(lax.ppermute(x, 'blk', pairs))  12 us
    ppermute x13, waiting for transfers between devices, send(): got.append(lax.ppermute(x, 'blk', pairs))  10.2 us
    ppermute x2, waiting for transfers between devices, on_device(): rests.append(lax.ppermute(halves[i], 'head', other))  4.52 us
    ppermute x2, starting transfers between devices, on_device(): rests.append(lax.ppermute(halves[i], 'head', other))  2.09 us
    convert_element_type x2, other arithmetic, on_device(): sums.append((halves[i].astype(F32) + rests[i].astype(F32)).astype(BF16))  1.38 us
  transfers between devices with their start and end apart: 16, of which 8 were waited for; matrix products, arithmetic and copies ran while one was open for 2% of the time, Pallas kernels for 37%

profile of v5, /device:TPU:0, one launch (start us, length us, event | category | flops | bytes accessed | tf_op | source)
XLA Modules:
  0.0 49.3 jit_solution(5495351447171817526)
XLA Ops:
  0.6 6.1 %collective-permute-start.2 = (s32[512]{0:T(512)}, s32[512]{0:T(512)S(1)}, u32[]{:S(2)}, u32[]{:S(2)}) collective-permute-start(s32[512]{0:T(512)} %param.14), channel_id=1, source_target_pairs={{0,28},{2,30},{4,0},{6,2},{8,4},{10,6},{12,8},{14,10},{16,12},{18,... | collective-permute-start | bytes 6152 | tf_op jit(solution)/shard_map/ppermute | solution.py:193
  6.7 0.0 collective-permute-start.8
  6.7 0.5 %collective-permute-start = (bf16[512,128]{1,0:T(8,128)(2,1)}, bf16[512,128]{1,0:T(8,128)(2,1)S(1)}, u32[]{:S(2)}, u32[]{:S(2)}) collective-permute-start(bf16[512,128]{1,0:T(8,128)(2,1)} %refs_0_.1), channel_id=1, source_target_pairs={{0,28},{2,30},{4,0},{6,2},{8,4},{10,6},{12,8},{14,10},{16,12},{18,... | collective-permute-start | bytes 393224 | tf_op jit(solution)/shard_map/ppermute | solution.py:193
  7.2 0.3 collective-permute-start.6
  7.5 1.4 %collective-permute-start.1 = (bf16[512,128]{1,0:T(8,128)(2,1)}, bf16[512,128]{1,0:T(8,128)(2,1)S(1)}, u32[]{:S(2)}, u32[]{:S(2)}) collective-permute-start(bf16[512,128]{1,0:T(8,128)(2,1)} %refs_1_.1), channel_id=1, source_target_pairs={{0,28},{2,30},{4,0},{6,2},{8,4},{10,6},{12,8},{14,10},{16,12},{18,... | collective-permute-start | bytes 393224 | tf_op jit(solution)/shard_map/ppermute | solution.py:193
  8.9 0.0 collective-permute-done.2
  8.9 0.0 collective-permute-start.7
  8.9 0.0 copy-start.3
  8.9 3.5 %shard_map.103 = (f32[32,4096]{1,0:T(8,128)S(1)}, bf16[4096,128]{1,0:T(8,128)(2,1)S(1)}) custom-call(bf16[4096,128]{1,0:T(8,128)(2,1)} %bitcast.38, bf16[4096,128]{1,0:T(8,128)(2,1)} %bitcast.39, s32[1,512]{1,0:T(1,128)} %bitcast.33, s32[1,512]{1,0:T(1,128)} %bitcast.32, f32[8,512]{1,0:T(8,128)} %bitcast.40), custom_call_target="tpu_custom_call" | custom-call | flops 4294967296 | bytes 4194304 | tf_op jit(solution)/shard_map/pallas_call | solution.py:163
  12.4 0.9 %collective-permute-done.refs_0_ = bf16[512,128]{1,0:T(8,128)(2,1)S(1)} collective-permute-done((bf16[512,128]{1,0:T(8,128)(2,1)}, bf16[512,128]{1,0:T(8,128)(2,1)S(1)}, u32[]{:S(2)}, u32[]{:S(2)}) %collective-permute-start) | collective-permute-done | bytes 131104 | tf_op jit(solution)/shard_map/ppermute | solution.py:193
  13.3 2.3 %collective-permute-done.1.refs_1_ = bf16[512,128]{1,0:T(8,128)(2,1)S(1)} collective-permute-done((bf16[512,128]{1,0:T(8,128)(2,1)}, bf16[512,128]{1,0:T(8,128)(2,1)S(1)}, u32[]{:S(2)}, u32[]{:S(2)}) %collective-permute-start.1) | collective-permute-done | bytes 131104 | tf_op jit(solution)/shard_map/ppermute | solution.py:193
  15.7 0.0 collective-permute-start.5
  15.7 0.5 %collective-permute-start.3 = (bf16[512,128]{1,0:T(8,128)(2,1)S(1)}, bf16[512,128]{1,0:T(8,128)(2,1)S(1)}, u32[]{:S(2)}, u32[]{:S(2)}) collective-permute-start(bf16[512,128]{1,0:T(8,128)(2,1)S(1)} %collective-permute-done.refs_0_), channel_id=1, source_target_pairs={{0,2},{2,0},{4,6},{6,4},{8,10},{10,8},{12,14},{14,12},{16,18},{18,... | collective-permute-start | bytes 393224 | tf_op jit(solution)/shard_map/ppermute | solution.py:193
  16.2 0.0 collective-permute-done.8
  16.2 0.0 collective-permute-start.4
  16.2 0.0 collective-permute-done.6.refs_0_
  16.2 0.4 collective-permute-done.7.refs_1_
  16.6 0.0 copy-done
  16.6 0.0 copy-done.3
  16.6 3.2 %shard_map.106 = (f32[128,4096]{1,0:T(8,128)S(1)}, bf16[1,512,128]{2,1,0:T(8,128)(2,1)S(1)}, bf16[1,512,128]{2,1,0:T(8,128)(2,1)S(1)}) custom-call(s32[512]{0:T(512)S(1)} %copy-done.3, f32[32,4096]{1,0:T(8,128)S(1)} %get-tuple-element.24.vec_ref, bf16[4096,128]{1,0:T(8,128)(2,1)S(1)} %bitcast.28, bf16[4096,128]{1,0:T(8,128)(2,1)S(1)} %get-tuple-element.25.g_ref, ...), custom_call_target="tpu_custom_call" | custom-call | flops 8589934592 | bytes 4194304 | tf_op jit(solution)/shard_map/pallas_call | solution.py:163
  19.9 0.5 collective-permute-start.12
  20.3 3.2 %shard_map.104 = (f32[128,4096]{1,0:T(8,128)S(1)}, bf16[2,512,128]{2,1,0:T(8,128)(2,1)S(1)}) custom-call(s32[512]{0:T(512)S(1)} %copy-done.3, f32[32,4096]{1,0:T(8,128)S(1)} %get-tuple-element.24.vec_ref, bf16[4096,128]{1,0:T(8,128)(2,1)S(1)} %bitcast.29, bf16[4096,128]{1,0:T(8,128)(2,1)S(1)} %get-tuple-element.25.g_ref, ...), custom_call_target="tpu_custom_call" | custom-call | flops 8589934592 | bytes 4194304 | tf_op jit(solution)/shard_map/pallas_call | solution.py:163
  23.6 0.1 collective-permute-start.10
  23.6 0.0 collective-permute-done.5
  23.7 0.0 collective-permute-done.3.refs_0_
  23.7 0.0 collective-permute-done.4.refs_1_
  23.7 0.0 copy-start.1
  23.7 0.0 copy-start.2
  23.7 0.0 copy-start.4
  23.7 3.4 %shard_map.105 = (f32[128,4096]{1,0:T(8,128)S(1)}, bf16[2,512,128]{2,1,0:T(8,128)(2,1)S(1)}) custom-call(s32[512]{0:T(512)S(1)} %copy-done.3, f32[32,4096]{1,0:T(8,128)S(1)} %get-tuple-element.24.vec_ref, bf16[4096,128]{1,0:T(8,128)(2,1)S(1)} %bitcast.30, bf16[4096,128]{1,0:T(8,128)(2,1)S(1)} %get-tuple-element.25.g_ref, ...), custom_call_target="tpu_custom_call" | custom-call | flops 8589934592 | bytes 4194304 | tf_op jit(solution)/shard_map/pallas_call | solution.py:163
  27.1 0.0 collective-permute-done.10
  27.2 1.4 %collective-permute-start.13 = (bf16[512,128]{1,0:T(8,128)(2,1)S(1)}, bf16[512,128]{1,0:T(8,128)(2,1)S(1)}, u32[]{:S(2)}, u32[]{:S(2)}) collective-permute-start(bf16[512,128]{1,0:T(8,128)(2,1)S(1)} %get-tuple-element.44), channel_id=1, source_target_pairs={{0,6},{2,4},{4,10},{6,8},{8,14},{10,12},{12,18},{14,16},{16,22},{1... | collective-permute-start | bytes 393224 | tf_op jit(solution)/shard_map/ppermute | solution.py:193
  28.6 0.0 copy-done.1
  28.6 3.2 %shard_map.107 = (f32[128,4096]{1,0:T(8,128)S(1)}, f32[2,512,128]{2,1,0:T(8,128)S(1)}) custom-call(s32[512]{0:T(512)S(1)} %copy-done.3, f32[32,4096]{1,0:T(8,128)S(1)} %get-tuple-element.24.vec_ref, bf16[4096,128]{1,0:T(8,128)(2,1)S(1)} %bitcast.31, bf16[4096,128]{1,0:T(8,128)(2,1)S(1)} %get-tuple-element.25.g_ref, bf16[512,128]{1,0:T(8,128)(2,1)S(1)} %copy-done.1, ...), custom_call_target="tpu_custom_call" | custom-call | flops 8589934592 | bytes 4194304 | tf_op jit(solution)/shard_map/pallas_call | solution.py:163
  31.9 0.1 collective-permute-start.9
  31.9 0.0 collective-permute-done.12
  31.9 1.2 %collective-permute-start.11 = (bf16[512,128]{1,0:T(8,128)(2,1)S(1)}, bf16[512,128]{1,0:T(8,128)(2,1)S(1)}, u32[]{:S(2)}, u32[]{:S(2)}) collective-permute-start(bf16[512,128]{1,0:T(8,128)(2,1)S(1)} %get-tuple-element.43), channel_id=1, source_target_pairs={{0,6},{2,4},{4,10},{6,8},{8,14},{10,12},{12,18},{14,16},{16,22},{1... | collective-permute-start | bytes 393224 | tf_op jit(solution)/shard_map/ppermute | solution.py:193
  33.2 1.9 %collective-permute-done.13 = bf16[512,128]{1,0:T(8,128)(2,1)S(1)} collective-permute-done((bf16[512,128]{1,0:T(8,128)(2,1)S(1)}, bf16[512,128]{1,0:T(8,128)(2,1)S(1)}, u32[]{:S(2)}, u32[]{:S(2)}) %collective-permute-start.13) | collective-permute-done | bytes 131104 | tf_op jit(solution)/shard_map/ppermute | solution.py:193
  35.1 3.0 %collective-permute-done.9 = bf16[1,512,128]{2,1,0:T(8,128)(2,1)S(1)} collective-permute-done((bf16[1,512,128]{2,1,0:T(8,128)(2,1)S(1)}, bf16[1,512,128]{2,1,0:T(8,128)(2,1)S(1)}, u32[]{:S(2)}, u32[]{:S(2)}) %collective-permute-start.9) | collective-permute-done | bytes 131104 | tf_op jit(solution)/shard_map/ppermute | solution.py:193
  38.1 1.7 %collective-permute-done.11 = bf16[512,128]{1,0:T(8,128)(2,1)S(1)} collective-permute-done((bf16[512,128]{1,0:T(8,128)(2,1)S(1)}, bf16[512,128]{1,0:T(8,128)(2,1)S(1)}, u32[]{:S(2)}, u32[]{:S(2)}) %collective-permute-start.11) | collective-permute-done | bytes 131104 | tf_op jit(solution)/shard_map/ppermute | solution.py:193
  39.8 0.1 fusion
  39.8 1.5 %collective-permute-start.15 = (bf16[512,128]{1,0:T(8,128)(2,1)S(1)}, bf16[512,128]{1,0:T(8,128)(2,1)S(1)}, u32[]{:S(2)}, u32[]{:S(2)}) collective-permute-start(bf16[512,128]{1,0:T(8,128)(2,1)S(1)} %fusion), channel_id=1, source_target_pairs={{0,1},{1,0},{2,3},{3,2},{4,5},{5,4},{6,7},{7,6},{8,9},{9,8},{10,11... | collective-permute-start | bytes 393224 | tf_op jit(solution)/shard_map/ppermute | solution.py:254
  41.4 1.5 %shard_map.108 = bf16[4096,128]{1,0:T(8,128)(2,1)} custom-call(f32[128,4096]{1,0:T(8,128)S(1)} %get-tuple-element.29.refs_0_, f32[128,4096]{1,0:T(8,128)S(1)} %get-tuple-element.30.refs_1_, f32[128,4096]{1,0:T(8,128)S(1)} %get-tuple-element.31.refs_2_, f32[128,4096]{1,0:T(8,128)S(1)} %get-tuple-element.32.refs_3_), custom_call_target="tpu_custom_call" | custom-call | flops 4294967296 | bytes 4194304 | tf_op jit(solution)/shard_map/pallas_call | solution.py:163
  42.9 0.6 %collective-permute-start.14 = (bf16[512,128]{1,0:T(8,128)(2,1)S(1)}, bf16[512,128]{1,0:T(8,128)(2,1)S(1)}, u32[]{:S(2)}, u32[]{:S(2)}) collective-permute-start(bf16[512,128]{1,0:T(8,128)(2,1)S(1)} %fusion.1), channel_id=1, source_target_pairs={{0,1},{1,0},{2,3},{3,2},{4,5},{5,4},{6,7},{7,6},{8,9},{9,8},{10,11... | collective-permute-start | bytes 393224 | tf_op jit(solution)/shard_map/ppermute | solution.py:254
  43.4 2.5 %collective-permute-done.15 = bf16[512,128]{1,0:T(8,128)(2,1)S(1)} collective-permute-done((bf16[512,128]{1,0:T(8,128)(2,1)S(1)}, bf16[512,128]{1,0:T(8,128)(2,1)S(1)}, u32[]{:S(2)}, u32[]{:S(2)}) %collective-permute-start.15) | collective-permute-done | bytes 131104 | tf_op jit(solution)/shard_map/ppermute | solution.py:254
  45.9 0.7 %add_convert_fusion = bf16[512,128]{1,0:T(8,128)(2,1)} fusion(bf16[512,128]{1,0:T(8,128)(2,1)S(1)} %collective-permute-done.15, bf16[512,128]{1,0:T(8,128)(2,1)S(1)} %fusion), kind=kLoop, calls=%fused_computation.6 | loop fusion | flops 262144 | bytes 393216 | tf_op jit(solution)/shard_map/convert_element_type | solution.py:257
  46.6 2.0 %collective-permute-done.14 = bf16[512,128]{1,0:T(8,128)(2,1)S(1)} collective-permute-done((bf16[512,128]{1,0:T(8,128)(2,1)S(1)}, bf16[512,128]{1,0:T(8,128)(2,1)S(1)}, u32[]{:S(2)}, u32[]{:S(2)}) %collective-permute-start.14) | collective-permute-done | bytes 131104 | tf_op jit(solution)/shard_map/ppermute | solution.py:254
  48.6 0.7 %add_convert_fusion.1 = bf16[512,128]{1,0:T(8,128)(2,1)} fusion(bf16[512,128]{1,0:T(8,128)(2,1)S(1)} %collective-permute-done.14, bf16[512,128]{1,0:T(8,128)(2,1)S(1)} %fusion.1), kind=kLoop, calls=%fused_computation.7 | loop fusion | flops 262144 | bytes 393216 | tf_op jit(solution)/shard_map/convert_element_type | solution.py:257
  (5 shorter events, 0.1 us)
Async XLA Ops:
  0.6 8.3 %collective-permute-start.2 = (s32[512]{0:T(512)}, s32[512]{0:T(512)S(1)}, u32[]{:S(2)}, u32[]{:S(2)}) collective-permute-start(s32[512]{0:T(512)} %param.14), channel_id=1, source_target_pairs={{0,28},{2,30},{4,0},{6,2},{8,4},{10,6},{12,8},{14,10},{16,12},{18,... | collective-permute-start | bytes 6152 | tf_op jit(solution)/shard_map/ppermute | solution.py:193
  6.7 9.4 %collective-permute-start.8 = (s32[512]{0:T(512)}, s32[512]{0:T(512)S(1)}, u32[]{:S(2)}, u32[]{:S(2)}) collective-permute-start(s32[512]{0:T(512)} %param.14), channel_id=1, source_target_pairs={{0,26},{2,0},{4,30},{6,4},{8,2},{10,8},{12,6},{14,12},{16,10},{18,... | collective-permute-start | bytes 6152 | tf_op jit(solution)/shard_map/ppermute | solution.py:193
  6.7 6.6 %collective-permute-start = (bf16[512,128]{1,0:T(8,128)(2,1)}, bf16[512,128]{1,0:T(8,128)(2,1)S(1)}, u32[]{:S(2)}, u32[]{:S(2)}) collective-permute-start(bf16[512,128]{1,0:T(8,128)(2,1)} %refs_0_.1), channel_id=1, source_target_pairs={{0,28},{2,30},{4,0},{6,2},{8,4},{10,6},{12,8},{14,10},{16,12},{18,... | collective-permute-start | bytes 393224 | tf_op jit(solution)/shard_map/ppermute | solution.py:193
  7.2 8.9 %collective-permute-start.6 = (bf16[512,128]{1,0:T(8,128)(2,1)}, bf16[512,128]{1,0:T(8,128)(2,1)S(1)}, u32[]{:S(2)}, u32[]{:S(2)}) collective-permute-start(bf16[512,128]{1,0:T(8,128)(2,1)} %refs_0_.1), channel_id=1, source_target_pairs={{0,26},{2,0},{4,30},{6,4},{8,2},{10,8},{12,6},{14,12},{16,10},{18,... | collective-permute-start | bytes 393224 | tf_op jit(solution)/shard_map/ppermute | solution.py:193
  7.5 8.1 %collective-permute-start.1 = (bf16[512,128]{1,0:T(8,128)(2,1)}, bf16[512,128]{1,0:T(8,128)(2,1)S(1)}, u32[]{:S(2)}, u32[]{:S(2)}) collective-permute-start(bf16[512,128]{1,0:T(8,128)(2,1)} %refs_1_.1), channel_id=1, source_target_pairs={{0,28},{2,30},{4,0},{6,2},{8,4},{10,6},{12,8},{14,10},{16,12},{18,... | collective-permute-start | bytes 393224 | tf_op jit(solution)/shard_map/ppermute | solution.py:193
  8.9 7.7 %collective-permute-start.7 = (bf16[512,128]{1,0:T(8,128)(2,1)}, bf16[512,128]{1,0:T(8,128)(2,1)S(1)}, u32[]{:S(2)}, u32[]{:S(2)}) collective-permute-start(bf16[512,128]{1,0:T(8,128)(2,1)} %refs_1_.1), channel_id=1, source_target_pairs={{0,26},{2,0},{4,30},{6,4},{8,2},{10,8},{12,6},{14,12},{16,10},{18,... | collective-permute-start | bytes 393224 | tf_op jit(solution)/shard_map/ppermute | solution.py:193
  8.9 7.7 %copy-start = (bf16[512,8,128]{2,1,0:T(8,128)(2,1)S(1)}, bf16[512,8,128]{2,1,0:T(8,128)(2,1)}, u32[]{:S(2)}) copy-start(bf16[512,8,128]{2,1,0:T(8,128)(2,1)} %param.8) | copy-start | bytes 3145732
  8.9 7.7 %copy-start.3 = (s32[512]{0:T(512)S(1)}, s32[512]{0:T(512)}, u32[]{:S(2)}) copy-start(s32[512]{0:T(512)} %starts_ref.7) | copy-start | bytes 6148
  15.7 8.0 %collective-permute-start.5 = (s32[512]{0:T(512)S(1)}, s32[512]{0:T(512)S(1)}, u32[]{:S(2)}, u32[]{:S(2)}) collective-permute-start(s32[512]{0:T(512)S(1)} %collective-permute-done.2), channel_id=1, source_target_pairs={{0,2},{2,0},{4,6},{6,4},{8,10},{10,8},{12,14},{14,12},{16,18},{18,... | collective-permute-start | bytes 6152 | tf_op jit(solution)/shard_map/ppermute | solution.py:193
  15.7 8.0 %collective-permute-start.3 = (bf16[512,128]{1,0:T(8,128)(2,1)S(1)}, bf16[512,128]{1,0:T(8,128)(2,1)S(1)}, u32[]{:S(2)}, u32[]{:S(2)}) collective-permute-start(bf16[512,128]{1,0:T(8,128)(2,1)S(1)} %collective-permute-done.refs_0_), channel_id=1, source_target_pairs={{0,2},{2,0},{4,6},{6,4},{8,10},{10,8},{12,14},{14,12},{16,18},{18,... | collective-permute-start | bytes 393224 | tf_op jit(solution)/shard_map/ppermute | solution.py:193
  16.2 7.5 %collective-permute-start.4 = (bf16[512,128]{1,0:T(8,128)(2,1)S(1)}, bf16[512,128]{1,0:T(8,128)(2,1)S(1)}, u32[]{:S(2)}, u32[]{:S(2)}) collective-permute-start(bf16[512,128]{1,0:T(8,128)(2,1)S(1)} %collective-permute-done.1.refs_1_), channel_id=1, source_target_pairs={{0,2},{2,0},{4,6},{6,4},{8,10},{10,8},{12,14},{14,12},{16,18},{18,... | collective-permute-start | bytes 393224 | tf_op jit(solution)/shard_map/ppermute | solution.py:193
  19.9 12.1 %collective-permute-start.12 = (bf16[1,512,128]{2,1,0:T(8,128)(2,1)S(1)}, bf16[1,512,128]{2,1,0:T(8,128)(2,1)S(1)}, u32[]{:S(2)}, u32[]{:S(2)}) collective-permute-start(bf16[1,512,128]{2,1,0:T(8,128)(2,1)S(1)} %get-tuple-element.36), channel_id=1, source_target_pairs={{26,0},{0,2},{30,4},{4,6},{2,8},{8,10},{6,12},{12,14},{10,16},{16,... | collective-permute-start | bytes 393224 | tf_op jit(solution)/shard_map/ppermute | solution.py:193
  23.6 3.6 %collective-permute-start.10 = (bf16[2,512,128]{2,1,0:T(8,128)(2,1)S(1)}, bf16[2,512,128]{2,1,0:T(8,128)(2,1)S(1)}, u32[]{:S(2)}, u32[]{:S(2)}) collective-permute-start(bf16[2,512,128]{2,1,0:T(8,128)(2,1)S(1)} %get-tuple-element.35), channel_id=1, source_target_pairs={{0,2},{2,0},{4,6},{6,4},{8,10},{10,8},{12,14},{14,12},{16,18},{18,... | collective-permute-start | bytes 786440 | tf_op jit(solution)/shard_map/ppermute | solution.py:237
  23.7 4.9 %copy-start.1 = (bf16[512,128]{1,0:T(8,128)(2,1)S(1)}, bf16[512,128]{1,0:T(8,128)(2,1)}, u32[]{:S(2)}) copy-start(bf16[512,128]{1,0:T(8,128)(2,1)} %refs_0_.1) | copy-start | bytes 393220
  23.7 4.9 %copy-start.2 = (bf16[512,128]{1,0:T(8,128)(2,1)S(1)}, bf16[512,128]{1,0:T(8,128)(2,1)}, u32[]{:S(2)}) copy-start(bf16[512,128]{1,0:T(8,128)(2,1)} %refs_1_.1) | copy-start | bytes 393220
  23.7 4.9 %copy-start.4 = (s32[512]{0:T(512)S(1)}, s32[512]{0:T(512)}, u32[]{:S(2)}) copy-start(s32[512]{0:T(512)} %param.14) | copy-start | bytes 6148
  27.2 7.9 %collective-permute-start.13 = (bf16[512,128]{1,0:T(8,128)(2,1)S(1)}, bf16[512,128]{1,0:T(8,128)(2,1)S(1)}, u32[]{:S(2)}, u32[]{:S(2)}) collective-permute-start(bf16[512,128]{1,0:T(8,128)(2,1)S(1)} %get-tuple-element.44), channel_id=1, source_target_pairs={{0,6},{2,4},{4,10},{6,8},{8,14},{10,12},{12,18},{14,16},{16,22},{1... | collective-permute-start | bytes 393224 | tf_op jit(solution)/shard_map/ppermute | solution.py:193
  31.9 6.2 %collective-permute-start.9 = (bf16[1,512,128]{2,1,0:T(8,128)(2,1)S(1)}, bf16[1,512,128]{2,1,0:T(8,128)(2,1)S(1)}, u32[]{:S(2)}, u32[]{:S(2)}) collective-permute-start(bf16[1,512,128]{2,1,0:T(8,128)(2,1)S(1)} %get-tuple-element.33), channel_id=1, source_target_pairs={{26,0},{0,2},{30,4},{4,6},{2,8},{8,10},{6,12},{12,14},{10,16},{16,... | collective-permute-start | bytes 393224 | tf_op jit(solution)/shard_map/ppermute | solution.py:193
  31.9 7.8 %collective-permute-start.11 = (bf16[512,128]{1,0:T(8,128)(2,1)S(1)}, bf16[512,128]{1,0:T(8,128)(2,1)S(1)}, u32[]{:S(2)}, u32[]{:S(2)}) collective-permute-start(bf16[512,128]{1,0:T(8,128)(2,1)S(1)} %get-tuple-element.43), channel_id=1, source_target_pairs={{0,6},{2,4},{4,10},{6,8},{8,14},{10,12},{12,18},{14,16},{16,22},{1... | collective-permute-start | bytes 393224 | tf_op jit(solution)/shard_map/ppermute | solution.py:193
  39.8 6.1 %collective-permute-start.15 = (bf16[512,128]{1,0:T(8,128)(2,1)S(1)}, bf16[512,128]{1,0:T(8,128)(2,1)S(1)}, u32[]{:S(2)}, u32[]{:S(2)}) collective-permute-start(bf16[512,128]{1,0:T(8,128)(2,1)S(1)} %fusion), channel_id=1, source_target_pairs={{0,1},{1,0},{2,3},{3,2},{4,5},{5,4},{6,7},{7,6},{8,9},{9,8},{10,11... | collective-permute-start | bytes 393224 | tf_op jit(solution)/shard_map/ppermute | solution.py:254
  42.9 5.8 %collective-permute-start.14 = (bf16[512,128]{1,0:T(8,128)(2,1)S(1)}, bf16[512,128]{1,0:T(8,128)(2,1)S(1)}, u32[]{:S(2)}, u32[]{:S(2)}) collective-permute-start(bf16[512,128]{1,0:T(8,128)(2,1)S(1)} %fusion.1), channel_id=1, source_target_pairs={{0,1},{1,0},{2,3},{3,2},{4,5},{5,4},{6,7},{7,6},{8,9},{9,8},{10,11... | collective-permute-start | bytes 393224 | tf_op jit(solution)/shard_map/ppermute | solution.py:254

commit v6 on v5

--- a/solution.py
+++ b/solution.py
@@ -13,7 +13,7 @@
 TN = (((0,), (0,)), ((), ()))
 NN = (((1,), (0,)), ((), ()))
 TILE = 64
-WIN = 128
+WIN = 192
 LOG2E = math.log2(math.e)
 
 
@@ -90,21 +90,21 @@
     dk_acc[...] = jnp.zeros_like(dk_acc)
     dv_acc[...] = jnp.zeros_like(dv_acc)
 
-    def scores(i, at):
+    def scores(i, at, size):
         rows = columns(i, cols)
-        keys = pl.ds(at, WIN)
+        keys = pl.ds(at, size)
         kw = jnp.concatenate([k[keys, :] for k in ks], axis=0)
         vw = jnp.concatenate([v[keys, :] for v in vs], axis=0)
         return dot(kw, q_ref[rows, :], NT), dot(vw, g_ref[rows, :], NT)
 
-    def window(i, at, top, s, dp):
+    def window(i, at, size, top, s, dp):
         rows = columns(i, cols)
-        keys = pl.ds(at, WIN)
+        keys = pl.ds(at, size)
         qs, gs = q_ref[rows, :], g_ref[rows, :]
         kw = jnp.concatenate([k[keys, :] for k in ks], axis=0)
         lse, delta = vec_ref[0:1, rows], vec_ref[8:9, rows]
         begin, place = vec_ref[16:17, rows], vec_ref[24:25, rows]
-        row = lax.broadcasted_iota(jnp.int32, (WIN, cols), 0) + at
+        row = lax.broadcasted_iota(jnp.int32, (size, cols), 0) + at
         row_place = (row * n_blk).astype(F32)
         oks = []
         for p in places:
@@ -117,16 +117,16 @@
         dv = dot(attend.astype(BF16), gs, NN)
         dk = dot(low, qs, NN)
         for b in range(nb):
-            dv_acc[b, keys, :] += dv[b * WIN : (b + 1) * WIN]
-            dk_acc[b, keys, :] += dk[b * WIN : (b + 1) * WIN]
+            dv_acc[b, keys, :] += dv[b * size : (b + 1) * size]
+            dk_acc[b, keys, :] += dk[b * size : (b + 1) * size]
         return dot(kw, low, TN)
 
-    starts = [max((i + 1) * TILE - WIN, 0) for i in range(tiles)]
-    ahead = scores(0, starts[0])
+    spans = [(max((i + 1) * TILE - WIN, 0), min((i + 1) * TILE, WIN)) for i in range(tiles)]
+    ahead = scores(0, *spans[0])
     for i in range(tiles):
         rows = columns(i, cols)
-        now, ahead = ahead, scores(i + 1, starts[i + 1]) if i + 1 < tiles else None
-        dq_ref[:, rows] = window(i, starts[i], None, *now)
+        now, ahead = ahead, scores(i + 1, *spans[i + 1]) if i + 1 < tiles else None
+        dq_ref[:, rows] = window(i, *spans[i], None, *now)
     for i in range(tiles):
         top = (i + 1) * TILE - WIN
         if top <= 0:
@@ -136,7 +136,7 @@
         def more(w, carry, i=i, top=top):
             edge = top - w * WIN
             at = pl.multiple_of(jnp.maximum(edge - WIN, 0), math.gcd(TILE, WIN))
-            dq_ref[:, columns(i, cols)] += window(i, at, edge, *scores(i, at))
+            dq_ref[:, columns(i, cols)] += window(i, at, WIN, edge, *scores(i, at, WIN))
             return carry
 
         lax.fori_loop(0, far, more, 0)

time: 49.5 us -> 47.9 us (0.968)
  Pallas kernels: 18.2 us -> 16.5 us
    pallas_call x6, Pallas kernels: 18.2 us -> 16.5 us  [call(): pl.pallas_call(body, out_shape=outs, in_specs=specs + [vmem] * (len(args)...]
  transfers between devices with their start and end apart: 16 -> 16, of which waited for: 8 -> 8; matrix products, arithmetic and copies ran while one was open for 2% -> 2% of each run, Pallas kernels for 37% -> 35%
where the time goes in v6:
time: 47.9 us; the launch traced here: 47.7 us
  Pallas kernels  16.5 us (34%)
  waiting for transfers between devices  14.7 us (31%)
  starting transfers between devices  14.2 us (30%)
  other arithmetic  1.52 us (3%)
  between operations  0.75 us (2%)
    pallas_call x6, Pallas kernels, call(): pl.pallas_call(body, out_shape=outs, in_specs=specs + [vmem] * (len(args)...  16.5 us
    ppermute x13, starting transfers between devices, send(): got.append(lax.ppermute(x, 'blk', pairs))  12 us
    ppermute x13, waiting for transfers between devices, send(): got.append(lax.ppermute(x, 'blk', pairs))  10.2 us
    ppermute x2, waiting for transfers between devices, on_device(): rests.append(lax.ppermute(halves[i], 'head', other))  4.49 us
    ppermute x2, starting transfers between devices, on_device(): rests.append(lax.ppermute(halves[i], 'head', other))  2.09 us
    convert_element_type x2, other arithmetic, on_device(): sums.append((halves[i].astype(F32) + rests[i].astype(F32)).astype(BF16))  1.38 us
  transfers between devices with their start and end apart: 16, of which 8 were waited for; matrix products, arithmetic and copies ran while one was open for 2% of the time, Pallas kernels for 35%

profile of v6, /device:TPU:0, one launch (start us, length us, event | category | flops | bytes accessed | tf_op | source)
XLA Modules:
  0.0 47.7 jit_solution(14917368482049330690)
XLA Ops:
  0.6 6.1 %collective-permute-start.2 = (s32[512]{0:T(512)}, s32[512]{0:T(512)S(1)}, u32[]{:S(2)}, u32[]{:S(2)}) collective-permute-start(s32[512]{0:T(512)} %param.14), channel_id=1, source_target_pairs={{0,28},{2,30},{4,0},{6,2},{8,4},{10,6},{12,8},{14,10},{16,12},{18,... | collective-permute-start | bytes 6152 | tf_op jit(solution)/shard_map/ppermute | solution.py:193
  6.7 0.0 collective-permute-start.8
  6.7 0.5 %collective-permute-start = (bf16[512,128]{1,0:T(8,128)(2,1)}, bf16[512,128]{1,0:T(8,128)(2,1)S(1)}, u32[]{:S(2)}, u32[]{:S(2)}) collective-permute-start(bf16[512,128]{1,0:T(8,128)(2,1)} %refs_0_.1), channel_id=1, source_target_pairs={{0,28},{2,30},{4,0},{6,2},{8,4},{10,6},{12,8},{14,10},{16,12},{18,... | collective-permute-start | bytes 393224 | tf_op jit(solution)/shard_map/ppermute | solution.py:193
  7.2 0.3 collective-permute-start.6
  7.5 1.4 %collective-permute-start.1 = (bf16[512,128]{1,0:T(8,128)(2,1)}, bf16[512,128]{1,0:T(8,128)(2,1)S(1)}, u32[]{:S(2)}, u32[]{:S(2)}) collective-permute-start(bf16[512,128]{1,0:T(8,128)(2,1)} %refs_1_.1), channel_id=1, source_target_pairs={{0,28},{2,30},{4,0},{6,2},{8,4},{10,6},{12,8},{14,10},{16,12},{18,... | collective-permute-start | bytes 393224 | tf_op jit(solution)/shard_map/ppermute | solution.py:193
  8.9 0.0 collective-permute-done.2
  8.9 0.0 collective-permute-start.7
  8.9 0.0 copy-start.3
  8.9 3.5 %shard_map.103 = (f32[32,4096]{1,0:T(8,128)S(1)}, bf16[4096,128]{1,0:T(8,128)(2,1)S(1)}) custom-call(bf16[4096,128]{1,0:T(8,128)(2,1)} %bitcast.38, bf16[4096,128]{1,0:T(8,128)(2,1)} %bitcast.39, s32[1,512]{1,0:T(1,128)} %bitcast.33, s32[1,512]{1,0:T(1,128)} %bitcast.32, f32[8,512]{1,0:T(8,128)} %bitcast.40), custom_call_target="tpu_custom_call" | custom-call | flops 4294967296 | bytes 4194304 | tf_op jit(solution)/shard_map/pallas_call | solution.py:163
  12.4 0.9 %collective-permute-done.refs_0_ = bf16[512,128]{1,0:T(8,128)(2,1)S(1)} collective-permute-done((bf16[512,128]{1,0:T(8,128)(2,1)}, bf16[512,128]{1,0:T(8,128)(2,1)S(1)}, u32[]{:S(2)}, u32[]{:S(2)}) %collective-permute-start) | collective-permute-done | bytes 131104 | tf_op jit(solution)/shard_map/ppermute | solution.py:193
  13.3 2.3 %collective-permute-done.1.refs_1_ = bf16[512,128]{1,0:T(8,128)(2,1)S(1)} collective-permute-done((bf16[512,128]{1,0:T(8,128)(2,1)}, bf16[512,128]{1,0:T(8,128)(2,1)S(1)}, u32[]{:S(2)}, u32[]{:S(2)}) %collective-permute-start.1) | collective-permute-done | bytes 131104 | tf_op jit(solution)/shard_map/ppermute | solution.py:193
  15.7 0.0 collective-permute-start.5
  15.7 0.5 %collective-permute-start.3 = (bf16[512,128]{1,0:T(8,128)(2,1)S(1)}, bf16[512,128]{1,0:T(8,128)(2,1)S(1)}, u32[]{:S(2)}, u32[]{:S(2)}) collective-permute-start(bf16[512,128]{1,0:T(8,128)(2,1)S(1)} %collective-permute-done.refs_0_), channel_id=1, source_target_pairs={{0,2},{2,0},{4,6},{6,4},{8,10},{10,8},{12,14},{14,12},{16,18},{18,... | collective-permute-start | bytes 393224 | tf_op jit(solution)/shard_map/ppermute | solution.py:193
  16.2 0.0 collective-permute-done.8
  16.2 0.0 collective-permute-start.4
  16.2 0.0 collective-permute-done.6.refs_0_
  16.2 0.4 collective-permute-done.7.refs_1_
  16.6 0.0 copy-done
  16.6 2.8 %shard_map.106 = (f32[128,4096]{1,0:T(8,128)S(1)}, bf16[1,512,128]{2,1,0:T(8,128)(2,1)S(1)}, bf16[1,512,128]{2,1,0:T(8,128)(2,1)S(1)}) custom-call(s32[512]{0:T(512)S(1)} %copy-done.3, f32[32,4096]{1,0:T(8,128)S(1)} %get-tuple-element.24.vec_ref, bf16[4096,128]{1,0:T(8,128)(2,1)S(1)} %bitcast.28, bf16[4096,128]{1,0:T(8,128)(2,1)S(1)} %get-tuple-element.25.g_ref, ...), custom_call_target="tpu_custom_call" | custom-call | flops 8589934592 | bytes 4194304 | tf_op jit(solution)/shard_map/pallas_call | solution.py:163
  19.5 0.5 collective-permute-start.12
  19.9 3.0 %shard_map.104 = (f32[128,4096]{1,0:T(8,128)S(1)}, bf16[2,512,128]{2,1,0:T(8,128)(2,1)S(1)}) custom-call(s32[512]{0:T(512)S(1)} %copy-done.3, f32[32,4096]{1,0:T(8,128)S(1)} %get-tuple-element.24.vec_ref, bf16[4096,128]{1,0:T(8,128)(2,1)S(1)} %bitcast.29, bf16[4096,128]{1,0:T(8,128)(2,1)S(1)} %get-tuple-element.25.g_ref, ...), custom_call_target="tpu_custom_call" | custom-call | flops 8589934592 | bytes 4194304 | tf_op jit(solution)/shard_map/pallas_call | solution.py:163
  22.9 0.1 collective-permute-start.10
  23.0 0.0 collective-permute-done.5
  23.0 0.0 collective-permute-done.3.refs_0_
  23.0 0.0 collective-permute-done.4.refs_1_
  23.1 0.0 copy-start.1
  23.1 0.0 copy-start.2
  23.1 0.0 copy-start.4
  23.1 2.8 %shard_map.105 = (f32[128,4096]{1,0:T(8,128)S(1)}, bf16[2,512,128]{2,1,0:T(8,128)(2,1)S(1)}) custom-call(s32[512]{0:T(512)S(1)} %copy-done.3, f32[32,4096]{1,0:T(8,128)S(1)} %get-tuple-element.24.vec_ref, bf16[4096,128]{1,0:T(8,128)(2,1)S(1)} %bitcast.30, bf16[4096,128]{1,0:T(8,128)(2,1)S(1)} %get-tuple-element.25.g_ref, ...), custom_call_target="tpu_custom_call" | custom-call | flops 8589934592 | bytes 4194304 | tf_op jit(solution)/shard_map/pallas_call | solution.py:163
  25.9 0.0 collective-permute-done.10
  26.0 1.4 %collective-permute-start.13 = (bf16[512,128]{1,0:T(8,128)(2,1)S(1)}, bf16[512,128]{1,0:T(8,128)(2,1)S(1)}, u32[]{:S(2)}, u32[]{:S(2)}) collective-permute-start(bf16[512,128]{1,0:T(8,128)(2,1)S(1)} %get-tuple-element.44), channel_id=1, source_target_pairs={{0,6},{2,4},{4,10},{6,8},{8,14},{10,12},{12,18},{14,16},{16,22},{1... | collective-permute-start | bytes 393224 | tf_op jit(solution)/shard_map/ppermute | solution.py:193
  27.4 0.0 copy-done.1
  27.4 0.0 copy-done.4
  27.4 2.8 %shard_map.107 = (f32[128,4096]{1,0:T(8,128)S(1)}, f32[2,512,128]{2,1,0:T(8,128)S(1)}) custom-call(s32[512]{0:T(512)S(1)} %copy-done.3, f32[32,4096]{1,0:T(8,128)S(1)} %get-tuple-element.24.vec_ref, bf16[4096,128]{1,0:T(8,128)(2,1)S(1)} %bitcast.31, bf16[4096,128]{1,0:T(8,128)(2,1)S(1)} %get-tuple-element.25.g_ref, bf16[512,128]{1,0:T(8,128)(2,1)S(1)} %copy-done.1, ...), custom_call_target="tpu_custom_call" | custom-call | flops 8589934592 | bytes 4194304 | tf_op jit(solution)/shard_map/pallas_call | solution.py:163
  30.3 0.1 collective-permute-start.9
  30.4 0.0 collective-permute-done.12
  30.4 1.2 %collective-permute-start.11 = (bf16[512,128]{1,0:T(8,128)(2,1)S(1)}, bf16[512,128]{1,0:T(8,128)(2,1)S(1)}, u32[]{:S(2)}, u32[]{:S(2)}) collective-permute-start(bf16[512,128]{1,0:T(8,128)(2,1)S(1)} %get-tuple-element.43), channel_id=1, source_target_pairs={{0,6},{2,4},{4,10},{6,8},{8,14},{10,12},{12,18},{14,16},{16,22},{1... | collective-permute-start | bytes 393224 | tf_op jit(solution)/shard_map/ppermute | solution.py:193
  31.6 2.3 %collective-permute-done.13 = bf16[512,128]{1,0:T(8,128)(2,1)S(1)} collective-permute-done((bf16[512,128]{1,0:T(8,128)(2,1)S(1)}, bf16[512,128]{1,0:T(8,128)(2,1)S(1)}, u32[]{:S(2)}, u32[]{:S(2)}) %collective-permute-start.13) | collective-permute-done | bytes 131104 | tf_op jit(solution)/shard_map/ppermute | solution.py:193
  33.9 2.6 %collective-permute-done.9 = bf16[1,512,128]{2,1,0:T(8,128)(2,1)S(1)} collective-permute-done((bf16[1,512,128]{2,1,0:T(8,128)(2,1)S(1)}, bf16[1,512,128]{2,1,0:T(8,128)(2,1)S(1)}, u32[]{:S(2)}, u32[]{:S(2)}) %collective-permute-start.9) | collective-permute-done | bytes 131104 | tf_op jit(solution)/shard_map/ppermute | solution.py:193
  36.5 1.7 %collective-permute-done.11 = bf16[512,128]{1,0:T(8,128)(2,1)S(1)} collective-permute-done((bf16[512,128]{1,0:T(8,128)(2,1)S(1)}, bf16[512,128]{1,0:T(8,128)(2,1)S(1)}, u32[]{:S(2)}, u32[]{:S(2)}) %collective-permute-start.11) | collective-permute-done | bytes 131104 | tf_op jit(solution)/shard_map/ppermute | solution.py:193
  38.2 0.1 fusion
  38.3 1.5 %collective-permute-start.15 = (bf16[512,128]{1,0:T(8,128)(2,1)S(1)}, bf16[512,128]{1,0:T(8,128)(2,1)S(1)}, u32[]{:S(2)}, u32[]{:S(2)}) collective-permute-start(bf16[512,128]{1,0:T(8,128)(2,1)S(1)} %fusion), channel_id=1, source_target_pairs={{0,1},{1,0},{2,3},{3,2},{4,5},{5,4},{6,7},{7,6},{8,9},{9,8},{10,11... | collective-permute-start | bytes 393224 | tf_op jit(solution)/shard_map/ppermute | solution.py:254
  39.8 1.5 %shard_map.108 = bf16[4096,128]{1,0:T(8,128)(2,1)} custom-call(f32[128,4096]{1,0:T(8,128)S(1)} %get-tuple-element.29.refs_0_, f32[128,4096]{1,0:T(8,128)S(1)} %get-tuple-element.30.refs_1_, f32[128,4096]{1,0:T(8,128)S(1)} %get-tuple-element.31.refs_2_, f32[128,4096]{1,0:T(8,128)S(1)} %get-tuple-element.32.refs_3_), custom_call_target="tpu_custom_call" | custom-call | flops 4294967296 | bytes 4194304 | tf_op jit(solution)/shard_map/pallas_call | solution.py:163
  41.3 0.6 %collective-permute-start.14 = (bf16[512,128]{1,0:T(8,128)(2,1)S(1)}, bf16[512,128]{1,0:T(8,128)(2,1)S(1)}, u32[]{:S(2)}, u32[]{:S(2)}) collective-permute-start(bf16[512,128]{1,0:T(8,128)(2,1)S(1)} %fusion.1), channel_id=1, source_target_pairs={{0,1},{1,0},{2,3},{3,2},{4,5},{5,4},{6,7},{7,6},{8,9},{9,8},{10,11... | collective-permute-start | bytes 393224 | tf_op jit(solution)/shard_map/ppermute | solution.py:254
  41.9 2.5 %collective-permute-done.15 = bf16[512,128]{1,0:T(8,128)(2,1)S(1)} collective-permute-done((bf16[512,128]{1,0:T(8,128)(2,1)S(1)}, bf16[512,128]{1,0:T(8,128)(2,1)S(1)}, u32[]{:S(2)}, u32[]{:S(2)}) %collective-permute-start.15) | collective-permute-done | bytes 131104 | tf_op jit(solution)/shard_map/ppermute | solution.py:254
  44.3 0.7 %add_convert_fusion = bf16[512,128]{1,0:T(8,128)(2,1)} fusion(bf16[512,128]{1,0:T(8,128)(2,1)S(1)} %collective-permute-done.15, bf16[512,128]{1,0:T(8,128)(2,1)S(1)} %fusion), kind=kLoop, calls=%fused_computation.6 | loop fusion | flops 262144 | bytes 393216 | tf_op jit(solution)/shard_map/convert_element_type | solution.py:257
  45.0 2.0 %collective-permute-done.14 = bf16[512,128]{1,0:T(8,128)(2,1)S(1)} collective-permute-done((bf16[512,128]{1,0:T(8,128)(2,1)S(1)}, bf16[512,128]{1,0:T(8,128)(2,1)S(1)}, u32[]{:S(2)}, u32[]{:S(2)}) %collective-permute-start.14) | collective-permute-done | bytes 131104 | tf_op jit(solution)/shard_map/ppermute | solution.py:254
  47.1 0.7 %add_convert_fusion.1 = bf16[512,128]{1,0:T(8,128)(2,1)} fusion(bf16[512,128]{1,0:T(8,128)(2,1)S(1)} %collective-permute-done.14, bf16[512,128]{1,0:T(8,128)(2,1)S(1)} %fusion.1), kind=kLoop, calls=%fused_computation.7 | loop fusion | flops 262144 | bytes 393216 | tf_op jit(solution)/shard_map/convert_element_type | solution.py:257
  (5 shorter events, 0.1 us)
Async XLA Ops:
  0.6 8.3 %collective-permute-start.2 = (s32[512]{0:T(512)}, s32[512]{0:T(512)S(1)}, u32[]{:S(2)}, u32[]{:S(2)}) collective-permute-start(s32[512]{0:T(512)} %param.14), channel_id=1, source_target_pairs={{0,28},{2,30},{4,0},{6,2},{8,4},{10,6},{12,8},{14,10},{16,12},{18,... | collective-permute-start | bytes 6152 | tf_op jit(solution)/shard_map/ppermute | solution.py:193
  6.7 9.4 %collective-permute-start.8 = (s32[512]{0:T(512)}, s32[512]{0:T(512)S(1)}, u32[]{:S(2)}, u32[]{:S(2)}) collective-permute-start(s32[512]{0:T(512)} %param.14), channel_id=1, source_target_pairs={{0,26},{2,0},{4,30},{6,4},{8,2},{10,8},{12,6},{14,12},{16,10},{18,... | collective-permute-start | bytes 6152 | tf_op jit(solution)/shard_map/ppermute | solution.py:193
  6.7 6.6 %collective-permute-start = (bf16[512,128]{1,0:T(8,128)(2,1)}, bf16[512,128]{1,0:T(8,128)(2,1)S(1)}, u32[]{:S(2)}, u32[]{:S(2)}) collective-permute-start(bf16[512,128]{1,0:T(8,128)(2,1)} %refs_0_.1), channel_id=1, source_target_pairs={{0,28},{2,30},{4,0},{6,2},{8,4},{10,6},{12,8},{14,10},{16,12},{18,... | collective-permute-start | bytes 393224 | tf_op jit(solution)/shard_map/ppermute | solution.py:193
  7.2 8.9 %collective-permute-start.6 = (bf16[512,128]{1,0:T(8,128)(2,1)}, bf16[512,128]{1,0:T(8,128)(2,1)S(1)}, u32[]{:S(2)}, u32[]{:S(2)}) collective-permute-start(bf16[512,128]{1,0:T(8,128)(2,1)} %refs_0_.1), channel_id=1, source_target_pairs={{0,26},{2,0},{4,30},{6,4},{8,2},{10,8},{12,6},{14,12},{16,10},{18,... | collective-permute-start | bytes 393224 | tf_op jit(solution)/shard_map/ppermute | solution.py:193
  7.5 8.1 %collective-permute-start.1 = (bf16[512,128]{1,0:T(8,128)(2,1)}, bf16[512,128]{1,0:T(8,128)(2,1)S(1)}, u32[]{:S(2)}, u32[]{:S(2)}) collective-permute-start(bf16[512,128]{1,0:T(8,128)(2,1)} %refs_1_.1), channel_id=1, source_target_pairs={{0,28},{2,30},{4,0},{6,2},{8,4},{10,6},{12,8},{14,10},{16,12},{18,... | collective-permute-start | bytes 393224 | tf_op jit(solution)/shard_map/ppermute | solution.py:193
  8.9 7.7 %collective-permute-start.7 = (bf16[512,128]{1,0:T(8,128)(2,1)}, bf16[512,128]{1,0:T(8,128)(2,1)S(1)}, u32[]{:S(2)}, u32[]{:S(2)}) collective-permute-start(bf16[512,128]{1,0:T(8,128)(2,1)} %refs_1_.1), channel_id=1, source_target_pairs={{0,26},{2,0},{4,30},{6,4},{8,2},{10,8},{12,6},{14,12},{16,10},{18,... | collective-permute-start | bytes 393224 | tf_op jit(solution)/shard_map/ppermute | solution.py:193
  8.9 7.7 %copy-start = (bf16[512,8,128]{2,1,0:T(8,128)(2,1)S(1)}, bf16[512,8,128]{2,1,0:T(8,128)(2,1)}, u32[]{:S(2)}) copy-start(bf16[512,8,128]{2,1,0:T(8,128)(2,1)} %param.8) | copy-start | bytes 3145732
  8.9 7.7 %copy-start.3 = (s32[512]{0:T(512)S(1)}, s32[512]{0:T(512)}, u32[]{:S(2)}) copy-start(s32[512]{0:T(512)} %starts_ref.7) | copy-start | bytes 6148
  15.7 7.4 %collective-permute-start.5 = (s32[512]{0:T(512)S(1)}, s32[512]{0:T(512)S(1)}, u32[]{:S(2)}, u32[]{:S(2)}) collective-permute-start(s32[512]{0:T(512)S(1)} %collective-permute-done.2), channel_id=1, source_target_pairs={{0,2},{2,0},{4,6},{6,4},{8,10},{10,8},{12,14},{14,12},{16,18},{18,... | collective-permute-start | bytes 6152 | tf_op jit(solution)/shard_map/ppermute | solution.py:193
  15.7 7.4 %collective-permute-start.3 = (bf16[512,128]{1,0:T(8,128)(2,1)S(1)}, bf16[512,128]{1,0:T(8,128)(2,1)S(1)}, u32[]{:S(2)}, u32[]{:S(2)}) collective-permute-start(bf16[512,128]{1,0:T(8,128)(2,1)S(1)} %collective-permute-done.refs_0_), channel_id=1, source_target_pairs={{0,2},{2,0},{4,6},{6,4},{8,10},{10,8},{12,14},{14,12},{16,18},{18,... | collective-permute-start | bytes 393224 | tf_op jit(solution)/shard_map/ppermute | solution.py:193
  16.2 6.9 %collective-permute-start.4 = (bf16[512,128]{1,0:T(8,128)(2,1)S(1)}, bf16[512,128]{1,0:T(8,128)(2,1)S(1)}, u32[]{:S(2)}, u32[]{:S(2)}) collective-permute-start(bf16[512,128]{1,0:T(8,128)(2,1)S(1)} %collective-permute-done.1.refs_1_), channel_id=1, source_target_pairs={{0,2},{2,0},{4,6},{6,4},{8,10},{10,8},{12,14},{14,12},{16,18},{18,... | collective-permute-start | bytes 393224 | tf_op jit(solution)/shard_map/ppermute | solution.py:193
  19.5 10.9 %collective-permute-start.12 = (bf16[1,512,128]{2,1,0:T(8,128)(2,1)S(1)}, bf16[1,512,128]{2,1,0:T(8,128)(2,1)S(1)}, u32[]{:S(2)}, u32[]{:S(2)}) collective-permute-start(bf16[1,512,128]{2,1,0:T(8,128)(2,1)S(1)} %get-tuple-element.36), channel_id=1, source_target_pairs={{26,0},{0,2},{30,4},{4,6},{2,8},{8,10},{6,12},{12,14},{10,16},{16,... | collective-permute-start | bytes 393224 | tf_op jit(solution)/shard_map/ppermute | solution.py:193
  22.9 3.0 %collective-permute-start.10 = (bf16[2,512,128]{2,1,0:T(8,128)(2,1)S(1)}, bf16[2,512,128]{2,1,0:T(8,128)(2,1)S(1)}, u32[]{:S(2)}, u32[]{:S(2)}) collective-permute-start(bf16[2,512,128]{2,1,0:T(8,128)(2,1)S(1)} %get-tuple-element.35), channel_id=1, source_target_pairs={{0,2},{2,0},{4,6},{6,4},{8,10},{10,8},{12,14},{14,12},{16,18},{18,... | collective-permute-start | bytes 786440 | tf_op jit(solution)/shard_map/ppermute | solution.py:237
  23.1 4.4 %copy-start.1 = (bf16[512,128]{1,0:T(8,128)(2,1)S(1)}, bf16[512,128]{1,0:T(8,128)(2,1)}, u32[]{:S(2)}) copy-start(bf16[512,128]{1,0:T(8,128)(2,1)} %refs_0_.1) | copy-start | bytes 393220
  23.1 4.4 %copy-start.2 = (bf16[512,128]{1,0:T(8,128)(2,1)S(1)}, bf16[512,128]{1,0:T(8,128)(2,1)}, u32[]{:S(2)}) copy-start(bf16[512,128]{1,0:T(8,128)(2,1)} %refs_1_.1) | copy-start | bytes 393220
  23.1 4.4 %copy-start.4 = (s32[512]{0:T(512)S(1)}, s32[512]{0:T(512)}, u32[]{:S(2)}) copy-start(s32[512]{0:T(512)} %param.14) | copy-start | bytes 6148
  26.0 7.9 %collective-permute-start.13 = (bf16[512,128]{1,0:T(8,128)(2,1)S(1)}, bf16[512,128]{1,0:T(8,128)(2,1)S(1)}, u32[]{:S(2)}, u32[]{:S(2)}) collective-permute-start(bf16[512,128]{1,0:T(8,128)(2,1)S(1)} %get-tuple-element.44), channel_id=1, source_target_pairs={{0,6},{2,4},{4,10},{6,8},{8,14},{10,12},{12,18},{14,16},{16,22},{1... | collective-permute-start | bytes 393224 | tf_op jit(solution)/shard_map/ppermute | solution.py:193
  30.3 6.2 %collective-permute-start.9 = (bf16[1,512,128]{2,1,0:T(8,128)(2,1)S(1)}, bf16[1,512,128]{2,1,0:T(8,128)(2,1)S(1)}, u32[]{:S(2)}, u32[]{:S(2)}) collective-permute-start(bf16[1,512,128]{2,1,0:T(8,128)(2,1)S(1)} %get-tuple-element.33), channel_id=1, source_target_pairs={{26,0},{0,2},{30,4},{4,6},{2,8},{8,10},{6,12},{12,14},{10,16},{16,... | collective-permute-start | bytes 393224 | tf_op jit(solution)/shard_map/ppermute | solution.py:193
  30.4 7.8 %collective-permute-start.11 = (bf16[512,128]{1,0:T(8,128)(2,1)S(1)}, bf16[512,128]{1,0:T(8,128)(2,1)S(1)}, u32[]{:S(2)}, u32[]{:S(2)}) collective-permute-start(bf16[512,128]{1,0:T(8,128)(2,1)S(1)} %get-tuple-element.43), channel_id=1, source_target_pairs={{0,6},{2,4},{4,10},{6,8},{8,14},{10,12},{12,18},{14,16},{16,22},{1... | collective-permute-start | bytes 393224 | tf_op jit(solution)/shard_map/ppermute | solution.py:193
  38.3 6.1 %collective-permute-start.15 = (bf16[512,128]{1,0:T(8,128)(2,1)S(1)}, bf16[512,128]{1,0:T(8,128)(2,1)S(1)}, u32[]{:S(2)}, u32[]{:S(2)}) collective-permute-start(bf16[512,128]{1,0:T(8,128)(2,1)S(1)} %fusion), channel_id=1, source_target_pairs={{0,1},{1,0},{2,3},{3,2},{4,5},{5,4},{6,7},{7,6},{8,9},{9,8},{10,11... | collective-permute-start | bytes 393224 | tf_op jit(solution)/shard_map/ppermute | solution.py:254
  41.3 5.8 %collective-permute-start.14 = (bf16[512,128]{1,0:T(8,128)(2,1)S(1)}, bf16[512,128]{1,0:T(8,128)(2,1)S(1)}, u32[]{:S(2)}, u32[]{:S(2)}) collective-permute-start(bf16[512,128]{1,0:T(8,128)(2,1)S(1)} %fusion.1), channel_id=1, source_target_pairs={{0,1},{1,0},{2,3},{3,2},{4,5},{5,4},{6,7},{7,6},{8,9},{9,8},{10,11... | collective-permute-start | bytes 393224 | tf_op jit(solution)/shard_map/ppermute | solution.py:254
